TPU v7x, 32 devices: a whole 2x2x4 slice. The times are simulated.
32 devices in a mesh: wide: 8 (over z, x), narrow: 4 (over y, core).
Axes of the slice: x: 2, y: 2, z: 4, core: 2. Of those that a mesh axis runs over, the one named last changes fastest.
Arguments:
- images: bfloat16 [512, 82, 512], P(('wide', 'narrow')), may hold values from -6 to 6
- grid_sizes: int32 [512], P(('wide', 'narrow')), may hold values from 5 to 9, as said below
- qkv_weight: bfloat16 [2, 786432], P(None, ('wide', 'narrow')), may hold values from -0.375 to 0.375
- proj_weight: bfloat16 [2, 262144], P(None, ('wide', 'narrow')), may hold values from -0.25 to 0.25
- fc1_weight: bfloat16 [2, 1048576], P(None, ('wide', 'narrow')), may hold values from -0.25 to 0.25
- fc2_weight: bfloat16 [2, 1048576], P(None, ('wide', 'narrow')), may hold values from -0.125 to 0.125
- small_params: bfloat16 [2, 36864], P(None, ('wide', 'narrow'))
- cotangent: bfloat16 [512, 82, 512], P(('wide', 'narrow')), may hold values from -6 to 6
Outputs:
- output: bfloat16 [512, 82, 512], P(('wide', 'narrow'))
- grad_images: float32 [512, 82, 512], P(('wide', 'narrow'))
- grad_qkv: float32 [2, 786432], P(None, ('wide', 'narrow'))
- grad_proj: float32 [2, 262144], P(None, ('wide', 'narrow'))
- grad_fc1: float32 [2, 1048576], P(None, ('wide', 'narrow'))
- grad_fc2: float32 [2, 1048576], P(None, ('wide', 'narrow'))
- grad_small: float32 [2, 36864], P(None, ('wide', 'narrow'))
Inputs may be any that keep to these rules, and one draw needn't show every extreme that they name: `grid_sizes`: each image's grid side is one of 5, 7, 9; some image has side 9.
All inputs are finite; a program needn't handle non-finite values.
Results may differ from a plain program's by a relative error of at most 0.0095.
Values may be sent and summed in bfloat16 or wider, within the bound.
A program may use at most 320 MiB of HBM per device.

v0:
```python
import jax
import jax.numpy as jnp
from jax import lax
from jax.sharding import PartitionSpec as P

D = 512
FF = 2048
HEADS = 8
GRID_MAX = 9
SMALL_COLS = 58
CPE_COLS = 10


PRECISE = lax.Precision.HIGHEST
NORM_EPS = 1e-06
ROOT_HALF = 0.7071067811865476
INV_ROOT_TAU = 0.3989422804014327


def grid_masks(grid_sides, slot_count):
    slot_index = lax.broadcasted_iota(jnp.int32, (grid_sides.shape[0], slot_count), 1)
    cell_index = jnp.maximum(slot_index - 1, 0)
    side_col = grid_sides[:, None]
    inside = (
        (slot_index >= 1) & (cell_index // GRID_MAX < side_col) & (cell_index % GRID_MAX < side_col)
    )
    present = inside | (slot_index == 0)
    return (present.astype(jnp.float32)[:, :, None], inside.astype(jnp.float32)[:, :, None])


def to_grid(stream):
    return stream[:, 1:, :].reshape(stream.shape[0], GRID_MAX, GRID_MAX, stream.shape[2])


def from_grid(grid_cells):
    images_in = grid_cells.shape[0]
    channels = grid_cells.shape[3]
    flat_cells = grid_cells.reshape(images_in, GRID_MAX * GRID_MAX, channels)
    return jnp.concatenate([jnp.zeros((images_in, 1, channels), jnp.float32), flat_cells], axis=1)


def depthwise(grid_cells, kernel, radius):
    span_taps = 2 * radius + 1
    padded = jnp.pad(grid_cells, ((0, 0), (radius, radius), (radius, radius), (0, 0)))
    summed = jnp.zeros_like(grid_cells)
    for row_tap in range(span_taps):
        for col_tap in range(span_taps):
            window_part = padded[:, row_tap : row_tap + GRID_MAX, col_tap : col_tap + GRID_MAX, :]
            summed = summed + window_part * kernel[:, row_tap * span_taps + col_tap]
    return summed


def depthwise_back(grid_grads, kernel, radius):
    span_taps = 2 * radius + 1
    padded = jnp.pad(grid_grads, ((0, 0), (radius, radius), (radius, radius), (0, 0)))
    summed = jnp.zeros_like(grid_grads)
    for row_tap in range(span_taps):
        for col_tap in range(span_taps):
            row_start = 2 * radius - row_tap
            col_start = 2 * radius - col_tap
            window_part = padded[
                :, row_start : row_start + GRID_MAX, col_start : col_start + GRID_MAX, :
            ]
            summed = summed + window_part * kernel[:, row_tap * span_taps + col_tap]
    return summed


def kernel_grad(grid_grads, source, radius):
    span_taps = 2 * radius + 1
    padded = jnp.pad(source, ((0, 0), (radius, radius), (radius, radius), (0, 0)))
    columns = []
    for row_tap in range(span_taps):
        for col_tap in range(span_taps):
            window_part = padded[:, row_tap : row_tap + GRID_MAX, col_tap : col_tap + GRID_MAX, :]
            columns.append(jnp.sum(grid_grads * window_part, axis=(0, 1, 2)))
    return jnp.stack(columns, axis=1)


def window_mask(channels):
    channel = lax.broadcasted_iota(jnp.int32, (channels, 49), 0)
    tap_pos = lax.broadcasted_iota(jnp.int32, (channels, 49), 1)
    head_num = channel // (channels // HEADS)
    radius_of = jnp.where(head_num < 2, 1, jnp.where(head_num < 5, 2, 3))
    inside = (jnp.abs(tap_pos // 7 - 3) <= radius_of) & (jnp.abs(tap_pos % 7 - 3) <= radius_of)
    return inside.astype(jnp.float32)


def layer_norm(stream, gain_col, shift_col):
    average = jnp.mean(stream, axis=-1, keepdims=True)
    centred = stream - average
    inv_std = lax.rsqrt(jnp.mean(centred * centred, axis=-1, keepdims=True) + NORM_EPS)
    normed = centred * inv_std
    return (normed * gain_col + shift_col, normed, inv_std)


def norm_back(upstream, normed, inv_std, gain_col):
    scaled = upstream * gain_col
    scaled_mean = jnp.mean(scaled, axis=-1, keepdims=True)
    cross_mean = jnp.mean(scaled * normed, axis=-1, keepdims=True)
    result = inv_std * (scaled - scaled_mean - normed * cross_mean)
    return (result, jnp.sum(upstream * normed, axis=(0, 1)), jnp.sum(upstream, axis=(0, 1)))


def project(stream, matrix):
    lead = stream.shape[0] * stream.shape[1]
    product = jnp.dot(
        stream.reshape(lead, stream.shape[2]), matrix, preferred_element_type=jnp.float32
    )
    return product.reshape(stream.shape[0], stream.shape[1], matrix.shape[1])


def rows_dot(left_rows, right_rows):
    return lax.dot_general(
        left_rows, right_rows, (((0,), (0,)), ((), ())), preferred_element_type=jnp.float32
    )


def back_dot(left_rows, matrix):
    return lax.dot_general(
        left_rows, matrix, (((1,), (1,)), ((), ())), preferred_element_type=jnp.float32
    )


def unpack(pieces):
    qkv_flat, proj_flat, fc1_flat, fc2_flat, small_vec = pieces
    small_vec = small_vec.astype(jnp.float32)
    table_end = SMALL_COLS * D
    table_cols = small_vec[:table_end].reshape(D, SMALL_COLS)
    fc1_bias = small_vec[table_end : table_end + FF]
    cpe_cols = small_vec[table_end + FF :].reshape(D, CPE_COLS)
    return (
        qkv_flat.reshape(D, 3 * D),
        proj_flat.reshape(D, D),
        fc1_flat.reshape(D, FF),
        fc2_flat.reshape(FF, D),
        table_cols,
        fc1_bias,
        cpe_cols,
    )


def block_forward(stream, pieces, present, inside):
    qkv_mat, proj_mat, fc1_mat, fc2_mat, table_cols, fc1_bias, cpe_cols = unpack(pieces)
    window = window_mask(D)
    head_dim = D // HEADS
    shaped = (stream.shape[0], stream.shape[1], HEADS, head_dim)
    conv_part = from_grid(depthwise(to_grid(stream * inside), cpe_cols[:, 0:9], 1))
    first = stream + inside * (conv_part + cpe_cols[:, 9])
    normed_one, hat_one, inv_one = layer_norm(first, table_cols[:, 0], table_cols[:, 1])
    low_one = normed_one.astype(jnp.bfloat16)
    qkv_bias = jnp.concatenate(
        [table_cols[:, 4], jnp.zeros_like(table_cols[:, 4]), table_cols[:, 5]]
    )
    joined = project(low_one, qkv_mat) + qkv_bias
    query, keys, values = jnp.split(joined, 3, axis=2)
    masked = jnp.where(present > 0, keys, -1e30)
    largest = jnp.max(masked, axis=1, keepdims=True)
    raised = jnp.exp(masked - largest)
    key_probs = raised / jnp.sum(raised, axis=1, keepdims=True)
    summary = jnp.einsum(
        "bshi,bshj->bhij", key_probs.reshape(shaped), values.reshape(shaped), precision=PRECISE
    )
    factor = jnp.einsum(
        "bshi,bhij->bshj", query.reshape(shaped), summary, precision=PRECISE
    ).reshape(stream.shape)
    relative = (
        from_grid(depthwise(to_grid(values * inside), table_cols[:, 9:] * window, 3))
        + table_cols[:, 8]
    )
    attended = (factor * head_dim ** (-0.5) + inside * query * relative).astype(jnp.bfloat16)
    second = first + project(attended, proj_mat) + table_cols[:, 6]
    normed_two, hat_two, inv_two = layer_norm(second, table_cols[:, 2], table_cols[:, 3])
    low_two = normed_two.astype(jnp.bfloat16)
    hidden_pre = project(low_two, fc1_mat) + fc1_bias
    activated = (0.5 * hidden_pre * (1.0 + lax.erf(hidden_pre * ROOT_HALF))).astype(jnp.bfloat16)
    third = second + project(activated, fc2_mat) + table_cols[:, 7]
    saved = (
        stream,
        hat_one,
        inv_one,
        low_one,
        query,
        values,
        key_probs,
        summary,
        relative,
        attended,
        hat_two,
        inv_two,
        low_two,
        hidden_pre,
        activated,
    )
    return (third, saved)


def block_backward(upstream, saved, pieces, inside):
    qkv_mat, proj_mat, fc1_mat, fc2_mat, table_cols, fc1_bias, cpe_cols = unpack(pieces)
    (
        stream,
        hat_one,
        inv_one,
        low_one,
        query,
        values,
        key_probs,
        summary,
        relative,
        attended,
        hat_two,
        inv_two,
        low_two,
        hidden_pre,
        activated,
    ) = saved
    window = window_mask(D)
    head_dim = D // HEADS
    shaped = (stream.shape[0], stream.shape[1], HEADS, head_dim)
    row_count = stream.shape[0] * stream.shape[1]
    grad_m = upstream.astype(jnp.bfloat16).reshape(row_count, D)
    g_fc2 = rows_dot(activated.reshape(row_count, FF), grad_m)
    g_bias_fc2 = jnp.sum(grad_m.astype(jnp.float32), axis=0)
    d_act = back_dot(grad_m, fc2_mat)
    pre_rows = hidden_pre.reshape(row_count, FF)
    gelu_slope = (
        0.5 * (1.0 + lax.erf(pre_rows * ROOT_HALF))
        + pre_rows * jnp.exp(-0.5 * pre_rows * pre_rows) * INV_ROOT_TAU
    )
    d_pre = (d_act * gelu_slope).astype(jnp.bfloat16)
    g_fc1 = rows_dot(low_two.reshape(row_count, D), d_pre)
    g_bias_fc1 = jnp.sum(d_pre.astype(jnp.float32), axis=0)
    d_two = back_dot(d_pre, fc1_mat).reshape(stream.shape)
    d_second, g_gain_two, g_shift_two = norm_back(d_two, hat_two, inv_two, table_cols[:, 2])
    d_second = upstream + d_second
    grad_y = d_second.astype(jnp.bfloat16).reshape(row_count, D)
    g_proj = rows_dot(attended.reshape(row_count, D), grad_y)
    g_bias_proj = jnp.sum(grad_y.astype(jnp.float32), axis=0)
    d_mixed = back_dot(grad_y, proj_mat).reshape(stream.shape)
    d_factor = (d_mixed * head_dim ** (-0.5)).reshape(shaped)
    d_rel = inside * query * d_mixed
    g_bias_rel = jnp.sum(d_rel, axis=(0, 1))
    d_summary = jnp.einsum("bshi,bshj->bhij", query.reshape(shaped), d_factor, precision=PRECISE)
    d_query = inside * relative * d_mixed + jnp.einsum(
        "bshj,bhij->bshi", d_factor, summary, precision=PRECISE
    ).reshape(stream.shape)
    rel_grid = to_grid(d_rel)
    g_rel_kernel = kernel_grad(rel_grid, to_grid(values * inside), 3) * window
    rel_back = from_grid(depthwise_back(rel_grid, table_cols[:, 9:] * window, 3))
    d_values = inside * rel_back + jnp.einsum(
        "bshi,bhij->bshj", key_probs.reshape(shaped), d_summary, precision=PRECISE
    ).reshape(stream.shape)
    d_probs = jnp.einsum(
        "bshj,bhij->bshi", values.reshape(shaped), d_summary, precision=PRECISE
    ).reshape(stream.shape)
    d_keys = key_probs * (d_probs - jnp.sum(key_probs * d_probs, axis=1, keepdims=True))
    d_joined = (
        jnp.concatenate([d_query, d_keys, d_values], axis=2)
        .astype(jnp.bfloat16)
        .reshape(row_count, 3 * D)
    )
    g_qkv = rows_dot(low_one.reshape(row_count, D), d_joined)
    joined_sums = jnp.sum(d_joined.astype(jnp.float32), axis=0)
    d_one = back_dot(d_joined, qkv_mat).reshape(stream.shape)
    d_first, g_gain_one, g_shift_one = norm_back(d_one, hat_one, inv_one, table_cols[:, 0])
    d_first = d_second + d_first
    d_conv = inside * d_first
    g_bias_cpe = jnp.sum(d_conv, axis=(0, 1))
    conv_grid = to_grid(d_conv)
    g_cpe_kernel = kernel_grad(conv_grid, to_grid(stream * inside), 1)
    d_stream = d_first + inside * from_grid(depthwise_back(conv_grid, cpe_cols[:, 0:9], 1))
    table_front = jnp.stack(
        [
            g_gain_one,
            g_shift_one,
            g_gain_two,
            g_shift_two,
            joined_sums[:D],
            joined_sums[2 * D :],
            g_bias_proj,
            g_bias_fc2,
            g_bias_rel,
        ],
        axis=1,
    )
    table_grad = jnp.concatenate([table_front, g_rel_kernel], axis=1)
    cpe_grad = jnp.concatenate([g_cpe_kernel, g_bias_cpe[:, None]], axis=1)
    small_grad = jnp.concatenate([table_grad.reshape(-1), g_bias_fc1, cpe_grad.reshape(-1)])
    terms = (
        g_qkv.reshape(-1),
        g_proj.reshape(-1),
        g_fc1.reshape(-1),
        g_fc2.reshape(-1),
        small_grad,
    )
    return (d_stream, terms)


def shards(
    images, grid_sizes, qkv_weight, proj_weight, fc1_weight, fc2_weight, small_params, cotangent
):
    present, inside = grid_masks(grid_sizes, images.shape[1])
    layer_count = qkv_weight.shape[0]
    stream = images.astype(jnp.float32)
    records = []
    held_pieces = []
    for layer_index in range(layer_count):
        pieces = (
            lax.all_gather(qkv_weight[layer_index], ("wide", "narrow"), axis=0, tiled=True),
            lax.all_gather(proj_weight[layer_index], ("wide", "narrow"), axis=0, tiled=True),
            lax.all_gather(fc1_weight[layer_index], ("wide", "narrow"), axis=0, tiled=True),
            lax.all_gather(fc2_weight[layer_index], ("wide", "narrow"), axis=0, tiled=True),
            lax.all_gather(small_params[layer_index], ("wide", "narrow"), axis=0, tiled=True),
        )
        stream, saved = block_forward(stream, pieces, present, inside)
        records.append(saved)
        held_pieces.append(pieces)
    output = (stream * present).astype(jnp.bfloat16)
    upstream = cotangent.astype(jnp.float32) * present
    shard_list = [None] * layer_count
    for layer_index in reversed(range(layer_count)):
        pieces = (
            lax.all_gather(qkv_weight[layer_index], ("wide", "narrow"), axis=0, tiled=True),
            lax.all_gather(proj_weight[layer_index], ("wide", "narrow"), axis=0, tiled=True),
            lax.all_gather(fc1_weight[layer_index], ("wide", "narrow"), axis=0, tiled=True),
            lax.all_gather(fc2_weight[layer_index], ("wide", "narrow"), axis=0, tiled=True),
            lax.all_gather(small_params[layer_index], ("wide", "narrow"), axis=0, tiled=True),
        )
        upstream, terms = block_backward(upstream, records[layer_index], pieces, inside)
        shard_list[layer_index] = (
            lax.psum_scatter(terms[0], ("wide", "narrow"), scatter_dimension=0, tiled=True),
            lax.psum_scatter(terms[1], ("wide", "narrow"), scatter_dimension=0, tiled=True),
            lax.psum_scatter(terms[2], ("wide", "narrow"), scatter_dimension=0, tiled=True),
            lax.psum_scatter(terms[3], ("wide", "narrow"), scatter_dimension=0, tiled=True),
            lax.psum_scatter(terms[4], ("wide", "narrow"), scatter_dimension=0, tiled=True),
        )
    grad_qkv = jnp.stack([shard_list[index_l][0] for index_l in range(layer_count)])
    grad_proj = jnp.stack([shard_list[index_l][1] for index_l in range(layer_count)])
    grad_fc1 = jnp.stack([shard_list[index_l][2] for index_l in range(layer_count)])
    grad_fc2 = jnp.stack([shard_list[index_l][3] for index_l in range(layer_count)])
    grad_small = jnp.stack([shard_list[index_l][4] for index_l in range(layer_count)])
    return (output, upstream, grad_qkv, grad_proj, grad_fc1, grad_fc2, grad_small)


def solution(mesh):
    placed = (
        P(("wide", "narrow"), None, None),
        P(("wide", "narrow")),
        P(None, ("wide", "narrow")),
        P(None, ("wide", "narrow")),
        P(None, ("wide", "narrow")),
        P(None, ("wide", "narrow")),
        P(None, ("wide", "narrow")),
        P(("wide", "narrow"), None, None),
    )
    return jax.shard_map(
        shards,
        mesh=mesh,
        in_specs=placed,
        out_specs=(
            P(("wide", "narrow"), None, None),
            P(("wide", "narrow"), None, None),
            P(None, ("wide", "narrow")),
            P(None, ("wide", "narrow")),
            P(None, ("wide", "narrow")),
            P(None, ("wide", "narrow")),
            P(None, ("wide", "narrow")),
        ),
        check_vma=False,
    )
```

profile of v0, /device:TPU:0, one launch (start us, length us, event | category | flops | bytes accessed | tf_op | source)
XLA Modules:
  0.0 1627.7 jit_solution(7273917154135766971)
XLA Ops:
  15.8 44.0 %all-gather = bf16[1,36864]{1,0:T(2,128)(2,1)S(1)} all-gather(bf16[1,1152]{1,0:T(2,128)(2,1)S(1)} %get-tuple-element.360), channel_id=2, replica_groups=mesh['wide'=8,'narrow'=4] {'wide','narrow'}, dimensions={1}, use_global_device_ids=true | all-gather | bytes 76032 | tf_op jit(solution)/shard_map/all_gather | solution.py:312
  60.0 37.1 %all-gather.5 = bf16[1,36864]{1,0:T(2,128)(2,1)S(1)} all-gather(bf16[1,1152]{1,0:T(2,128)(2,1)S(1)} %get-tuple-element.359), channel_id=7, replica_groups=mesh['wide'=8,'narrow'=4] {'wide','narrow'}, dimensions={1}, use_global_device_ids=true | all-gather | bytes 76032 | tf_op jit(solution)/shard_map/all_gather | solution.py:312
  135.2 44.7 %all-gather.2 = bf16[1,262144]{1,0:T(2,128)(2,1)} all-gather(bf16[1,8192]{1,0:T(2,128)(2,1)S(1)} %get-tuple-element.350), channel_id=4, replica_groups=mesh['wide'=8,'narrow'=4] {'wide','narrow'}, dimensions={1}, use_global_device_ids=true | all-gather | bytes 540672 | tf_op jit(solution)/shard_map/all_gather | solution.py:309
  180.0 11.9 reduce.75
  195.2 43.6 %all-gather.7 = bf16[1,262144]{1,0:T(2,128)(2,1)} all-gather(bf16[1,8192]{1,0:T(2,128)(2,1)S(1)} %get-tuple-element.349), channel_id=9, replica_groups=mesh['wide'=8,'narrow'=4] {'wide','narrow'}, dimensions={1}, use_global_device_ids=true | all-gather | bytes 540672 | tf_op jit(solution)/shard_map/all_gather | solution.py:309
  238.9 12.7 reduce.149
  259.2 34.8 %reduce.22 = bf16[786432]{0:T(1024)(128)(2,1)} reduce(bf16[1,786432]{1,0:T(2,128)(2,1)} %all-gather.17.cloned.1.call-done, bf16[]{:T(256)} %constant.217), dimensions={0}, to_apply=%all-gather.1.reduce_sub_computation | reduce | bytes 3145730 | tf_op jit(solution)/shard_map/all_gather | solution.py:308
  318.3 17.3 %multiply_add_fusion.10 = f32[16,9,9,512]{3,0,2,1:T(8,128)} fusion(f32[16,9,9,512]{3,0,2,1:T(8,128)S(1)} %bitcast.279, f32[512]{0:T(512)S(1)} %get-tuple-element.234, f32[512]{0:T(512)S(1)} %get-tuple-element.235, f32[512]{0:T(512)S(1)} %get-tuple-element.236, f32[512]{0:T(512)S(1)} %get-tuple-element.237, f32[512]{0:T(512)S(1)} %get-tuple-element.238, ...), kind=kLoop, calls=%fused_computation.660 | loop fusion | flops 64364544 | bytes 5408768 | tf_op jit(solution)/shard_map/add | solution.py:49
  349.1 9.7 fusion.299
  358.9 8.5 convolution_multiply_fusion.1
  378.2 35.0 %reduce.96 = bf16[786432]{0:T(1024)(128)(2,1)} reduce(bf16[1,786432]{1,0:T(2,128)(2,1)} %all-gather.23.cloned.1.call-done, bf16[]{:T(256)} %constant.217), dimensions={0}, to_apply=%all-gather.6.reduce_sub_computation | reduce | bytes 3145730 | tf_op jit(solution)/shard_map/all_gather | solution.py:308
  421.5 45.8 %reduce.79 = bf16[1048576]{0:T(1024)(128)(2,1)} reduce(bf16[1,1048576]{1,0:T(2,128)(2,1)} %all-gather.19.cloned.1.call-done, bf16[]{:T(256)} %constant.217), dimensions={0}, to_apply=%all-gather.3.reduce_sub_computation | reduce | bytes 4194306 | tf_op jit(solution)/shard_map/all_gather | solution.py:310
  471.8 45.9 %reduce.80 = bf16[1048576]{0:T(1024)(128)(2,1)} reduce(bf16[1,1048576]{1,0:T(2,128)(2,1)} %all-gather.21.cloned.1.call-done, bf16[]{:T(256)} %constant.217), dimensions={0}, to_apply=%all-gather.4.reduce_sub_computation | reduce | bytes 4194306 | tf_op jit(solution)/shard_map/all_gather | solution.py:311
  522.0 9.3 multiply_convert_fusion.1
  557.4 18.8 %multiply_add_fusion.8 = f32[16,9,9,512]{3,0,2,1:T(8,128)} fusion(f32[16,9,9,512]{3,0,2,1:T(8,128)S(1)} %bitcast.283, f32[512]{0:T(512)S(1)} %copy-done.197, f32[512]{0:T(512)S(1)} %copy-done.198, f32[512]{0:T(512)S(1)} %copy-done.199, f32[512]{0:T(512)S(1)} %copy-done.200, f32[512]{0:T(512)S(1)} %copy-done.201, f32[512]{0:T(512)S(1)} %copy-done.202, ...), kind=kLoop, calls=%fused_computation.658 | loop fusion | flops 64364544 | bytes 5408768 | tf_op jit(solution)/shard_map/add | solution.py:49
  594.5 9.3 fusion.300
  603.9 8.7 convolution_multiply_fusion
  617.8 45.8 %reduce.153 = bf16[1048576]{0:T(1024)(128)(2,1)} reduce(bf16[1,1048576]{1,0:T(2,128)(2,1)} %all-gather.25.cloned.1.call-done, bf16[]{:T(256)} %constant.217), dimensions={0}, to_apply=%all-gather.8.reduce_sub_computation | reduce | bytes 4194306 | tf_op jit(solution)/shard_map/all_gather | solution.py:310
  675.7 8.6 multiply_convert_fusion
  684.3 8.7 reshape.873
  692.9 45.9 %reduce.154 = bf16[1048576]{0:T(1024)(128)(2,1)} reduce(bf16[1,1048576]{1,0:T(2,128)(2,1)} %all-gather.27.cloned.1.call-done, bf16[]{:T(256)} %constant.217), dimensions={0}, to_apply=%all-gather.9.reduce_sub_computation | reduce | bytes 4194306 | tf_op jit(solution)/shard_map/all_gather | solution.py:311
  743.2 11.4 convert_reduce_fusion
  777.4 9.3 fusion.302
  798.6 8.7 fusion.304
  834.1 17.0 %fusion.141 = f32[16,9,9,512]{3,0,2,1:T(8,128)} fusion(f32[16,9,9,512]{3,0,2,1:T(8,128)S(1)} %bitcast.287, f32[512]{0:T(512)S(1)} %copy-done.197, f32[512]{0:T(512)S(1)} %copy-done.198, f32[512]{0:T(512)S(1)} %copy-done.199, f32[512]{0:T(512)S(1)} %copy-done.200, f32[512]{0:T(512)S(1)} %copy-done.201, f32[512]{0:T(512)S(1)} %copy-done.202, ...), kind=kLoop, calls=%fused_computation.444 | loop fusion | flops 64364544 | bytes 5408768 | tf_op jit(solution)/shard_map/add | solution.py:64
  890.0 8.7 reshape.883
  898.7 11.4 convert_reduce_fusion.1
  916.1 9.2 multiply_reduce_fusion.6
  936.0 9.8 fusion.306
  995.0 44.7 %fusion.237 = f32[16,9,9,512]{3,0,2,1:T(8,128)} fusion(f32[16,9,9,512]{3,0,2,1:T(8,128)} %bitcast.291, f32[512]{0:T(512)S(1)} %copy-done.111, f32[512]{0:T(512)S(1)} %copy-done.113, f32[512]{0:T(512)S(1)} %copy-done.115, f32[512]{0:T(512)S(1)} %copy-done.117, f32[512]{0:T(512)S(1)} %copy-done.119, f32[512]{0:T(512)S(1)} %copy-done.121, ...), kind=kLoop, calls=%fused_computation.540 | loop fusion | flops 64364544 | bytes 5408768 | tf_op jit(solution)/shard_map/add | solution.py:64
  1098.8 8.7 convolution_bitcast_fusion.5
  1222.1 385.6 %all-reduce.29.cloned.1.call-done = (f32[786432]{0:T(1024)}, f32[786432]{0:T(1024)}, f32[262144]{0:T(1024)}, f32[262144]{0:T(1024)}, f32[1048576]{0:T(1024)}, /*...) async-done(((f32[786432]{0:T(1024)}, f32[786432]{0:T(1024)}, f32[262144]{0:T(1024)}, f32[262144]{0:T(1024)}, ...) | async-done | bytes 25460752
  (1007 shorter events, 537.5 us)
Async XLA Ops:
  7.2 252.1 %all-gather.17.cloned.1.call-start = ((), (), s32[]{:S(2)}) async-start(), calls=%async_computation | async-start | bytes 3244032 | tf_op jit(solution)/shard_map/all_gather | solution.py:308
  9.1 369.2 %all-gather.23.cloned.1.call-start = ((), (), s32[]{:S(2)}) async-start(), calls=%async_computation.3 | async-start | bytes 3244032 | tf_op jit(solution)/shard_map/all_gather | solution.py:308
  9.8 411.7 %all-gather.19.cloned.1.call-start = ((), (), s32[]{:S(2)}) async-start(), calls=%async_computation.1 | async-start | bytes 4325376 | tf_op jit(solution)/shard_map/all_gather | solution.py:310
  11.8 460.0 %all-gather.21.cloned.1.call-start = ((), (), s32[]{:S(2)}) async-start(), calls=%async_computation.2 | async-start | bytes 4325376 | tf_op jit(solution)/shard_map/all_gather | solution.py:311
  13.8 604.0 %all-gather.25.cloned.1.call-start = ((), (), s32[]{:S(2)}) async-start(), calls=%async_computation.4 | async-start | bytes 4325376 | tf_op jit(solution)/shard_map/all_gather | solution.py:310
  14.4 678.6 %all-gather.27.cloned.1.call-start = ((), (), s32[]{:S(2)}) async-start(), calls=%async_computation.5 | async-start | bytes 4325376 | tf_op jit(solution)/shard_map/all_gather | solution.py:311
  14.9 1592.8 %all-reduce.29.cloned.1.call-start = ((), (), s32[]{:S(2)}) async-start(), calls=%async_computation.6 | async-start | bytes 50921472
  106.1 211.8 %copy-start.108 = (f32[512]{0:T(512)}, f32[512]{0:T(512)S(1)}, u32[]{:S(2)}) copy-start(f32[512]{0:T(512)S(1)} %get-tuple-element.233) | copy-start | bytes 6148
  106.1 211.8 %copy-start.110 = (f32[512]{0:T(512)}, f32[512]{0:T(512)S(1)}, u32[]{:S(2)}) copy-start(f32[512]{0:T(512)S(1)} %get-tuple-element.234) | copy-start | bytes 6148
  106.1 211.8 %copy-start.112 = (f32[512]{0:T(512)}, f32[512]{0:T(512)S(1)}, u32[]{:S(2)}) copy-start(f32[512]{0:T(512)S(1)} %get-tuple-element.235) | copy-start | bytes 6148
  106.1 211.8 %copy-start.114 = (f32[512]{0:T(512)}, f32[512]{0:T(512)S(1)}, u32[]{:S(2)}) copy-start(f32[512]{0:T(512)S(1)} %get-tuple-element.236) | copy-start | bytes 6148
  106.1 211.8 %copy-start.116 = (f32[512]{0:T(512)}, f32[512]{0:T(512)S(1)}, u32[]{:S(2)}) copy-start(f32[512]{0:T(512)S(1)} %get-tuple-element.237) | copy-start | bytes 6148
  106.1 211.8 %copy-start.118 = (f32[512]{0:T(512)}, f32[512]{0:T(512)S(1)}, u32[]{:S(2)}) copy-start(f32[512]{0:T(512)S(1)} %get-tuple-element.238) | copy-start | bytes 6148
  106.1 211.8 %copy-start.120 = (f32[512]{0:T(512)}, f32[512]{0:T(512)S(1)}, u32[]{:S(2)}) copy-start(f32[512]{0:T(512)S(1)} %get-tuple-element.239) | copy-start | bytes 6148
  106.1 211.8 %copy-start.122 = (f32[512]{0:T(512)}, f32[512]{0:T(512)S(1)}, u32[]{:S(2)}) copy-start(f32[512]{0:T(512)S(1)} %get-tuple-element.240) | copy-start | bytes 6148
  106.1 211.8 %copy-start.124 = (f32[512]{0:T(512)}, f32[512]{0:T(512)S(1)}, u32[]{:S(2)}) copy-start(f32[512]{0:T(512)S(1)} %get-tuple-element.241) | copy-start | bytes 6148
  106.1 211.8 %copy-start.126 = (f32[512]{0:T(512)}, f32[512]{0:T(512)S(1)}, u32[]{:S(2)}) copy-start(f32[512]{0:T(512)S(1)} %get-tuple-element.242) | copy-start | bytes 6148
  106.2 211.8 %copy-start.128 = (f32[512]{0:T(512)}, f32[512]{0:T(512)S(1)}, u32[]{:S(2)}) copy-start(f32[512]{0:T(512)S(1)} %get-tuple-element.243) | copy-start | bytes 6148
  106.2 211.8 %copy-start.130 = (f32[512]{0:T(512)}, f32[512]{0:T(512)S(1)}, u32[]{:S(2)}) copy-start(f32[512]{0:T(512)S(1)} %get-tuple-element.244) | copy-start | bytes 6148
  106.2 211.8 %copy-start.132 = (f32[512]{0:T(512)}, f32[512]{0:T(512)S(1)}, u32[]{:S(2)}) copy-start(f32[512]{0:T(512)S(1)} %get-tuple-element.245) | copy-start | bytes 6148
  121.8 131.2 %copy-start.103 = (f32[16,82]{1,0:T(8,128)}, f32[16,82]{1,0:T(8,128)S(1)}, u32[]{:S(2)}) copy-start(f32[16,82]{1,0:T(8,128)S(1)} %get-tuple-element.318) | copy-start | bytes 15748
  134.4 164.1 %copy-start.15 = (f32[16,82,512]{2,1,0:T(8,128)}, f32[16,82,512]{2,1,0:T(8,128)S(1)}, u32[]{:S(2)}) copy-start(f32[16,82,512]{2,1,0:T(8,128)S(1)} %get-tuple-element.323) | copy-start | bytes 8060932
  134.4 164.1 %copy-start.99 = (f32[16,82]{1,0:T(8,128)}, f32[16,82]{1,0:T(8,128)S(1)}, u32[]{:S(2)}) copy-start(f32[16,82]{1,0:T(8,128)S(1)} %broadcast_multiply_fusion.15) | copy-start | bytes 15748
  135.2 163.3 %copy-start.106 = (f32[16,82]{1,0:T(8,128)}, f32[16,82]{1,0:T(8,128)S(1)}, u32[]{:S(2)}) copy-start(f32[16,82]{1,0:T(8,128)S(1)} %add_rsqrt_fusion.3) | copy-start | bytes 15748
  317.8 17.8 %copy-start = (f32[16,81,512]{2,0,1:T(8,128)}, f32[16,81,512]{2,0,1:T(8,128)S(1)}, u32[]{:S(2)}) copy-start(f32[16,81,512]{2,0,1:T(8,128)S(1)} %copy.242) | copy-start | bytes 7962628
  377.5 153.8 %copy-start.18 = (f32[16,82,512]{2,1,0:T(8,128)}, f32[16,82,512]{2,1,0:T(8,128)S(1)}, u32[]{:S(2)}) copy-start(f32[16,82,512]{2,1,0:T(8,128)S(1)} %get-tuple-element.368) | copy-start | bytes 8060932
  377.5 40.0 %copy-start.96 = (f32[16,82]{1,0:T(8,128)}, f32[16,82]{1,0:T(8,128)S(1)}, u32[]{:S(2)}) copy-start(f32[16,82]{1,0:T(8,128)S(1)} %broadcast_multiply_fusion.14) | copy-start | bytes 15748
  378.2 39.3 %copy-start.101 = (f32[16,82]{1,0:T(8,128)}, f32[16,82]{1,0:T(8,128)S(1)}, u32[]{:S(2)}) copy-start(f32[16,82]{1,0:T(8,128)S(1)} %add_rsqrt_fusion.2) | copy-start | bytes 15748
  557.0 19.2 %copy-start.2 = (f32[16,81,512]{2,0,1:T(8,128)}, f32[16,81,512]{2,0,1:T(8,128)S(1)}, u32[]{:S(2)}) copy-start(f32[16,81,512]{2,0,1:T(8,128)S(1)} %copy.255) | copy-start | bytes 7962628
  672.6 95.5 %copy-start.5 = (f32[16,82,512]{2,1,0:T(8,128)}, f32[16,82,512]{2,1,0:T(8,128)S(1)}, u32[]{:S(2)}) copy-start(f32[16,82,512]{2,1,0:T(8,128)S(1)} %get-tuple-element.374) | copy-start | bytes 8060932
  995.0 44.7 %copy-start.1 = (f32[16,81,512]{2,0,1:T(8,128)S(1)}, f32[16,81,512]{2,0,1:T(8,128)}, u32[]{:S(2)}) copy-start(f32[16,81,512]{2,0,1:T(8,128)} %copy-done) | copy-start | bytes 7962628
  1175.8 13.4 slice-start
  (344 other events, 1274.6 us)
Sparse Core Ops, SparseCore 0:
  10.9 62.0 all-gather.16
  75.9 57.8 all-gather.22
  137.2 61.7 all-gather.18
  201.7 61.3 all-gather.20
  266.4 60.4 all-gather.24
  330.3 60.3 all-gather.26
  1206.0 401.7 all-reduce.28
where the time goes:
time: 1640 us; the launch traced here: 1630 us
  other arithmetic  516 us (31%)
  waiting for transfers between devices  387 us (24%)
  local copies, waits for them, and re-layouts  309 us (19%)
  matrix products  226 us (14%)
  blocking collectives  170 us (10%)
  between operations  19.6 us (1%)
    unnamed x8, waiting for transfers between devices  387 us
    all_gather x2, other arithmetic, shards(): lax.all_gather(fc2_weight[layer_index], ('wide', 'narrow'), axis=0, tiled...  91.8 us
    all_gather x2, other arithmetic, shards(): lax.all_gather(fc1_weight[layer_index], ('wide', 'narrow'), axis=0, tiled...  91.7 us
    all_gather x2, blocking collectives, shards(): lax.all_gather(proj_weight[layer_index], ('wide', 'narrow'), axis=0, tile...  88.4 us
    all_gather x2, blocking collectives, shards(): lax.all_gather(small_params[layer_index], ('wide', 'narrow'), axis=0, til...  81.1 us
    all_gather x2, other arithmetic, shards(): lax.all_gather(qkv_weight[layer_index], ('wide', 'narrow'), axis=0, tiled...  69.8 us
    add x2, other arithmetic, depthwise_back(): summed = summed + window_part * kernel[:, row_tap * span_taps + col_tap]  61.7 us
    dot_general x8, matrix products, back_dot(): lax.dot_general(left_rows, matrix, (((1,), (1,)), ((), ())), preferred_el...  58.6 us
  transfers between devices with their start and end apart: 7, of which 1 were waited for; matrix products, arithmetic and copies ran while one was open for 32% of the time, Pallas kernels for 0%

commit v1 on v0

v1 whole, which is shorter than its diff:
```python
import functools
import jax
import jax.numpy as jnp
from jax import lax
from jax.experimental import pallas as pl
from jax.experimental.pallas import tpu as pltpu

F32, BF16 = jnp.float32, jnp.bfloat16
D, FF, HEADS, GRID, SLOT = 512, 2048, 8, 9, 82
TABLE = 58
EPS = 1e-6
NI = 16
R = SLOT * NI
PADS = 96
RP = PADS * NI
RADII = (1, 2, 3, 3)
TAPS, CPE, CPEB, TROWS = 9, 58, 67, 72


def ds(start, size, align=8):
    if not isinstance(start, int):
        start = pl.multiple_of(start, align)
    return pl.ds(start, size)


def row8(ref, i, lg):
    return ref[lg, pl.ds(i, 8, stride=0), :]


def row(tab, i, j=None):
    parts = range(4) if j is None else (2 * j, 2 * j + 1)
    return jnp.concatenate([tab[g, i:i + 1, :] for g in parts], axis=1)


def put2(ref, at, j, val):
    ref[2 * j, at, :] = val[:, :128]
    ref[2 * j + 1, at, :] = val[:, 128:]


def cell(y, x, ig):
    return ds((1 + GRID * y + x) * NI + 8 * ig, 8)


def inside_at(sz, y, x):
    return sz > max(y, x)


def conv_pass(load_row, load_tap, radius, emit, flip=False):
    span = 2 * radius + 1
    for y in range(GRID):
        acc = [None] * GRID
        for a in range(span):
            yy = y - (a - radius) if flip else y + a - radius
            if not 0 <= yy < GRID:
                continue
            row = load_row(yy)
            for b in range(span):
                tap = load_tap(a - radius, b - radius)
                for x in range(GRID):
                    xx = x - (b - radius) if flip else x + b - radius
                    if 0 <= xx < GRID:
                        term = row[xx] * tap
                        acc[x] = term if acc[x] is None else acc[x] + term
        emit(y, acc)


def conv_kgrad(load_grad, load_src, radius, emit):
    span = 2 * radius + 1
    for a in range(span):
        acc = [None] * span
        for y in range(GRID):
            yy = y + a - radius
            if not 0 <= yy < GRID:
                continue
            grad = load_grad(y)
            src = load_src(yy)
            for b in range(span):
                for x in range(GRID):
                    xx = x + b - radius
                    if 0 <= xx < GRID:
                        term = grad[x] * src[xx]
                        acc[b] = term if acc[b] is None else acc[b] + term
        for b in range(span):
            emit(a - radius, b - radius, acc[b])


def lane_of(lg):
    return ds(lg * 128, 128, 128)


def for_groups(body):
    def one(radius, base):
        def run(i, c):
            body(radius, base + i // 2, i % 2)
            return c
        return run
    lax.fori_loop(0, 2, one(1, 0), 0)
    lax.fori_loop(0, 2, one(2, 1), 0)
    lax.fori_loop(0, 4, one(3, 2), 0)


def norm_rows(x):
    mean = jnp.mean(x, axis=-1, keepdims=True)
    cen = x - mean
    inv = lax.rsqrt(jnp.mean(cen * cen, axis=-1, keepdims=True) + EPS)
    return cen * inv, inv


def normal_cdf(u):
    a = jnp.abs(u)
    t = 1.0 / (1.0 + a * (0.3275911 * 0.7071067811865476))
    e = jnp.exp(-0.5 * u * u)
    poly = t * (0.5 * 0.254829592 + t * (0.5 * -0.284496736 + t * (0.5 * 1.421413741 + t * (0.5 * -1.453152027 + t * (0.5 * 1.061405429)))))
    tail = poly * e
    return jnp.where(u >= 0, 1.0 - tail, tail), e


LN_T = 112
ROW_T = 336


def tile_start(i, size):
    return pl.multiple_of(jnp.minimum(i * size, R - size), 16)


def head_mask():
    r = lax.broadcasted_iota(jnp.int32, (256, 256), 0) // 64
    c = lax.broadcasted_iota(jnp.int32, (256, 256), 1) // 64
    return r == c


def dot(a, b, ca, cb):
    return lax.dot_general(a, b, (((ca,), (cb,)), ((), ())), preferred_element_type=F32)


def fwd_conv1(x, sz, tab, x1):
    def body(i, c):
        lg, ig = i // 2, i % 2
        lane = lane_of(lg)
        size = sz[ds(8 * ig, 8), :]
        cls = ds(8 * ig, 8)
        x1[cls, lane] = x[cls, lane].astype(F32)
        bias = row8(tab, CPEB, lg)

        def load_row(y):
            return [jnp.where(inside_at(size, y, k), x[cell(y, k, ig), lane].astype(F32), 0.0) for k in range(GRID)]

        def emit(y, acc):
            for k in range(GRID):
                at = cell(y, k, ig)
                x1[at, lane] = x[at, lane].astype(F32) + jnp.where(inside_at(size, y, k), acc[k] + bias, 0.0)

        conv_pass(load_row, lambda a, b: row8(tab, CPE + (a + 1) * 3 + b + 1, lg), 1, emit)
        return c
    lax.fori_loop(0, 8, body, 0)


def norm_phase(src, tab, gain, shift, hat, low, inv_ref):
    def body(i, c):
        at = pl.ds(tile_start(i, LN_T), LN_T)
        n, inv = norm_rows(src[at, :])
        hat[at, :] = n.astype(BF16)
        low[at, :] = (n * row(tab, gain) + row(tab, shift)).astype(BF16)
        inv_ref[at, :] = jnp.broadcast_to(inv, (LN_T, 128))
        return c
    lax.fori_loop(0, 12, body, 0)


def fwd_qkv(low, w, tab, q, k, v):
    def body(i, c):
        at = pl.ds(tile_start(i, ROW_T), ROW_T)
        h = low[at, :]
        for j in range(2):
            cols = slice(256 * j, 256 * j + 256)
            put2(q, at, j, dot(h, w[:, cols], 1, 0) + row(tab, 4, j))
            put2(k, at, j, dot(h, w[:, 512 + 256 * j:768 + 256 * j], 1, 0))
            put2(v, at, j, dot(h, w[:, 1024 + 256 * j:1280 + 256 * j], 1, 0) + row(tab, 5, j))
        return c
    lax.fori_loop(0, 4, body, 0)
    tail = slice(R, RP)
    for ref in (q, k, v):
        ref[:, tail, :] = jnp.zeros((4, RP - R, 128), F32)


def each_pos(size, ig, fn):
    fn(ds(8 * ig, 8), None)
    for y in range(GRID):
        for x in range(GRID):
            fn(cell(y, x, ig), inside_at(size, y, x))


def fwd_softmax(k, sz):
    def body(i, c):
        lg, ig = i // 2, i % 2
        lane = lane_of(lg)
        size = sz[ds(8 * ig, 8), :]
        best = [None] * 4
        cnt = [0]

        def first(at, ok):
            val = k[lg, at, :]
            if ok is not None:
                val = jnp.where(ok, val, -1e30)
            j = cnt[0] % 4
            best[j] = val if best[j] is None else jnp.maximum(best[j], val)
            cnt[0] += 1
        each_pos(size, ig, first)
        top = jnp.maximum(jnp.maximum(best[0], best[1]), jnp.maximum(best[2], best[3]))
        total = [None] * 4
        cnt[0] = 0

        def second(at, ok):
            val = jnp.exp(k[lg, at, :] - top)
            if ok is not None:
                val = jnp.where(ok, val, 0.0)
            k[lg, at, :] = val
            j = cnt[0] % 4
            total[j] = val if total[j] is None else total[j] + val
            cnt[0] += 1
        each_pos(size, ig, second)
        scale = 1.0 / ((total[0] + total[1]) + (total[2] + total[3]))

        def third(at, ok):
            k[lg, at, :] = k[lg, at, :] * scale
        each_pos(size, ig, third)
        return c
    lax.fori_loop(0, 8, body, 0)


def img_load(ref, i, half):
    return jnp.concatenate([ref[2 * half + j, pl.ds(i, PADS, stride=NI), :] for j in range(2)], axis=1)


def img_store(ref, i, half, val):
    for j in range(2):
        ref[2 * half + j, pl.ds(i, PADS, stride=NI), :] = val[:, 128 * j:128 * j + 128]


def fwd_attn(q, p, v, s, f):
    def body(t, c):
        i, half = t // 2, t % 2
        pi = img_load(p, i, half).astype(BF16)
        vi = img_load(v, i, half).astype(BF16)
        summ = jnp.where(head_mask(), dot(pi, vi, 0, 0), 0.0).astype(BF16)
        s[t] = summ
        qi = img_load(q, i, half).astype(BF16)
        img_store(f, i, half, dot(qi, summ, 1, 0) * 0.125)
        return c
    lax.fori_loop(0, 2 * NI, body, 0)


def fwd_conv3(v, q, f, sz, tab, rel, att):
    def body(radius, lg, ig):
        lane = lane_of(lg)
        size = sz[ds(8 * ig, 8), :]
        bias = row8(tab, 8, lg)

        def load_row(y):
            return [jnp.where(inside_at(size, y, k), v[lg, cell(y, k, ig), :], 0.0) for k in range(GRID)]

        def emit(y, acc):
            for k in range(GRID):
                at = cell(y, k, ig)
                r = acc[k] + bias
                rel[lg, at, :] = r
                att[lg, at, :] = f[lg, at, :] + jnp.where(inside_at(size, y, k), q[lg, at, :] * r, 0.0)
        conv_pass(load_row, lambda a, b: row8(tab, TAPS + (a + 3) * 7 + b + 3, lg), radius, emit)
    for_groups(body)


def fwd_proj(att, w, tab, x1, a_low):
    def body(i, c):
        at = pl.ds(pl.multiple_of(i * 656, 16), 656)
        low = jnp.concatenate([att[g, at, :] for g in range(4)], axis=1).astype(BF16)
        a_low[at, :] = low
        for j in range(2):
            cols = slice(256 * j, 256 * j + 256)
            x1[at, cols] = x1[at, cols] + dot(low, w[:, cols], 1, 0) + row(tab, 6, j)
        return c
    lax.fori_loop(0, 2, body, 0)


def fwd_fc1(low, w, b1, g, slope):
    def body(t, c):
        i, j = t // 8, t % 8
        at = pl.ds(tile_start(i, ROW_T), ROW_T)
        cols = pl.ds(pl.multiple_of(j * 256, 256), 256)
        u = dot(low[at, :], w[:, cols], 1, 0) + b1[:, cols]
        cdf, e = normal_cdf(u)
        g[at, cols] = (u * cdf).astype(BF16)
        slope[at, cols] = (cdf + u * e * 0.3989422804014327).astype(BF16)
        return c
    lax.fori_loop(0, 32, body, 0)


def fwd_fc2(g, w, tab, x2, x3):
    def body(i, c):
        at = pl.ds(pl.multiple_of(i * 656, 16), 656)
        for j in range(2):
            cols = slice(256 * j, 256 * j + 256)
            x3[at, cols] = x2[at, cols] + dot(g[at, :], w[:, cols], 1, 0) + row(tab, 7, j)
        return c
    lax.fori_loop(0, 2, body, 0)


def fwd_kernel(x, sz, tab, b1, wqkv, wproj, w1, w2,
               x3, n1, inv1, h1, q, p, v, s, rel, a_low, n2, inv2, h2, g, slope,
               x1, f):
    fwd_conv1(x, sz, tab, x1)
    norm_phase(x1, tab, 0, 1, n1, h1, inv1)
    fwd_qkv(h1, wqkv, tab, q, p, v)
    fwd_softmax(p, sz)
    fwd_attn(q, p, v, s, f)
    fwd_conv3(v, q, f, sz, tab, rel, f)
    fwd_proj(f, wproj, tab, x1, a_low)
    norm_phase(x1, tab, 2, 3, n2, h2, inv2)
    fwd_fc1(h2, w1, b1, g, slope)
    fwd_fc2(g, w2, tab, x1, x3)


RES = (
    ("n1", (R, D), BF16), ("inv1", (R, 128), F32), ("h1", (R, D), BF16),
    ("q", (4, RP, 128), F32), ("p", (4, RP, 128), F32), ("v", (4, RP, 128), F32),
    ("s", (2 * NI, 256, 256), BF16), ("rel", (4, R, 128), F32), ("a", (R, D), BF16),
    ("n2", (R, D), BF16), ("inv2", (R, 128), F32), ("h2", (R, D), BF16),
    ("g", (R, FF), BF16), ("slope", (R, FF), BF16))


def vspec(n):
    return [pl.BlockSpec(memory_space=pltpu.VMEM)] * n


PARAMS = pltpu.CompilerParams(vmem_limit_bytes=67043328)


def fwd_layer(x, sz, tab, b1, wqkv, wproj, w1, w2):
    outs = [jax.ShapeDtypeStruct((R, D), F32)] + [jax.ShapeDtypeStruct(sh, dt) for _, sh, dt in RES]
    return pl.pallas_call(
        fwd_kernel, out_shape=outs, in_specs=vspec(8), out_specs=vspec(len(outs)),
        scratch_shapes=[pltpu.VMEM((R, D), F32), pltpu.VMEM((4, RP, 128), F32)],
        compiler_params=PARAMS, name="block_fwd",
    )(x, sz, tab, b1, wqkv, wproj, w1, w2)


def add_rows(ref, row, val):
    total = val[0:8]
    for i in range(1, val.shape[0] // 8):
        total = total + val[8 * i:8 * i + 8]
    ref[8 * row:8 * row + 8, :] += total


def bwd_du(dx, w2, slope, dm, gb1):
    def cast(i, c):
        at = pl.ds(pl.multiple_of(i * 32, 16), 32)
        dm[at, :] = dx[at, :].astype(BF16)
        return c
    lax.fori_loop(0, 41, cast, 0)

    def body(t, c):
        i, j = t // 8, t % 8
        at = pl.ds(pl.multiple_of(i * 656, 16), 656)
        cols = pl.ds(pl.multiple_of(j * 256, 256), 256)
        d = dot(dm[at, :], w2[cols, :], 1, 1) * slope[at, cols].astype(F32)
        slope[at, cols] = d.astype(BF16)
        total = d[0:8]
        for k in range(1, 82):
            total = total + d[8 * k:8 * k + 8]
        keep = jnp.where(i == 0, 0.0, 1.0)
        gb1[:, cols] = gb1[:, cols] * keep + total
        return c
    gb1[...] = jnp.zeros_like(gb1)
    lax.fori_loop(0, 16, body, 0)


def norm_back_phase(up, hat, inv_ref, tab, gain, res, out_low, sums, rg, rs, rb):
    def body(i, c):
        at = pl.ds(pl.multiple_of(i * 32, 16), 32)
        u = up[at, :]
        n = hat[at, :].astype(F32)
        e = u * row(tab, gain)
        m1 = jnp.mean(e, axis=-1, keepdims=True)
        m2 = jnp.mean(e * n, axis=-1, keepdims=True)
        inv = inv_ref[at, 0:1]
        d = res[at, :] + inv * (e - m1 - n * m2)
        res[at, :] = d
        add_rows(sums, rg, u * n)
        add_rows(sums, rs, u)
        if out_low is not None:
            out_low[at, :] = d.astype(BF16)
        return c
    lax.fori_loop(0, 41, body, 0)


def mm_nt(a, w, out, split=False):
    def body(i, c):
        at = pl.ds(pl.multiple_of(i * 656, 16), 656)
        for j in range(2):
            val = dot(a[at, :], w[256 * j:256 * j + 256, :], 1, 1)
            if split:
                put2(out, at, j, val)
            else:
                out[at, 256 * j:256 * j + 256] = val
        return c
    lax.fori_loop(0, 2, body, 0)


def wgrad(left, right, out):
    wide_left = left.shape[1] > 512
    blocks = max(left.shape[1], right.shape[1]) // 512
    for j in range(blocks):
        cols = slice(512 * j, 512 * j + 512)
        if wide_left:
            out[cols, :] = dot(left[:, cols], right[...], 0, 0).astype(BF16)
        else:
            out[:, cols] = dot(left[...], right[:, cols], 0, 0).astype(BF16)


def bwd_attn1(q, p, v, s, da, dq, dv, dk):
    def body(t, c):
        i, half = t // 2, t % 2
        df = (img_load(da, i, half) * 0.125).astype(BF16)
        qi = img_load(q, i, half).astype(BF16)
        dsum = jnp.where(head_mask(), dot(qi, df, 0, 0), 0.0).astype(BF16)
        img_store(dq, i, half, dot(df, s[t], 1, 1))
        pi = img_load(p, i, half).astype(BF16)
        img_store(dv, i, half, dot(pi, dsum, 1, 0))
        vi = img_load(v, i, half).astype(BF16)
        img_store(dk, i, half, dot(vi, dsum, 1, 1))
        return c
    lax.fori_loop(0, 2 * NI, body, 0)


def bwd_mix(q, p, v, rel, da, dq, dv, dk, dj, sz, tab, gsum, gtap):
    def body(radius, lg, ig):
        lane = lane_of(lg)
        size = sz[ds(8 * ig, 8), :]

        acc = {"r": None, "q": None, "s": [None] * 4, "n": 0}

        def first(at, ok):
            d = da[lg, at, :]
            qv = q[lg, at, :]
            if ok is None:
                dqv = dq[lg, at, :]
                da[lg, at, :] = jnp.zeros_like(d)
            else:
                d = jnp.where(ok, d, 0.0)
                dr = qv * d
                da[lg, at, :] = dr
                acc["r"] = dr if acc["r"] is None else acc["r"] + dr
                dqv = dq[lg, at, :] + rel[lg, at, :] * d
            dq[lg, at, :] = dqv
            acc["q"] = dqv if acc["q"] is None else acc["q"] + dqv
            t = p[lg, at, :] * dk[lg, at, :]
            j = acc["n"] % 4
            acc["s"][j] = t if acc["s"][j] is None else acc["s"][j] + t
            acc["n"] += 1
        each_pos(size, ig, first)
        dot_sum = (acc["s"][0] + acc["s"][1]) + (acc["s"][2] + acc["s"][3])

        def second(at, ok):
            dk[lg, at, :] = p[lg, at, :] * (dk[lg, at, :] - dot_sum)
        each_pos(size, ig, second)
        gsum[ds(8 * (8 + 8 * 0), 8), lane] += acc["r"]
        gsum[ds(8 * 4, 8), lane] += acc["q"]

        def load_grad(y):
            return [da[lg, cell(y, k, ig), :] for k in range(GRID)]

        def load_src(y):
            return [jnp.where(inside_at(size, y, k), v[lg, cell(y, k, ig), :], 0.0) for k in range(GRID)]

        def emit_tap(a, b, val):
            at = ds(8 * (TAPS + (a + 3) * 7 + b + 3), 8)
            gsum[at, lane] += val
        conv_kgrad(load_grad, load_src, radius, emit_tap)
        vs = [dv[lg, ds(8 * ig, 8), :]]

        def emit(y, out):
            for k in range(GRID):
                at = cell(y, k, ig)
                val = dv[lg, at, :] + jnp.where(inside_at(size, y, k), out[k], 0.0)
                dv[lg, at, :] = val
                vs[0] = vs[0] + val
        conv_pass(load_grad, lambda a, b: row8(tab, TAPS + (a + 3) * 7 + b + 3, lg), radius, emit, flip=True)
        gsum[ds(8 * 5, 8), lane] += vs[0]
    for_groups(body)

    def cast(i, c):
        at = pl.ds(pl.multiple_of(i * 32, 16), 32)
        for j, ref in enumerate((dq, dk, dv)):
            for g in range(4):
                dj[at, 512 * j + 128 * g:512 * j + 128 * g + 128] = ref[g, at, :].astype(BF16)
        return c
    lax.fori_loop(0, 41, cast, 0)


def bwd_conv1(x, dx1, dx, sz, tab, gsum):
    def body(i, c):
        lg, ig = i // 2, i % 2
        lane = lane_of(lg)
        size = sz[ds(8 * ig, 8), :]
        cls = ds(8 * ig, 8)
        dx[cls, lane] = dx1[cls, lane]

        def load_grad(y):
            return [jnp.where(inside_at(size, y, k), dx1[cell(y, k, ig), lane], 0.0) for k in range(GRID)]

        def load_src(y):
            return [jnp.where(inside_at(size, y, k), x[cell(y, k, ig), lane].astype(F32), 0.0) for k in range(GRID)]

        def emit_tap(a, b, val):
            at = ds(8 * (CPE + (a + 1) * 3 + b + 1), 8)
            gsum[at, lane] += val
        conv_kgrad(load_grad, load_src, 1, emit_tap)
        bias = [jnp.zeros((8, 128), F32)]

        def emit(y, out):
            for k in range(GRID):
                at = cell(y, k, ig)
                g = dx1[at, lane]
                ok = inside_at(size, y, k)
                bias[0] = bias[0] + jnp.where(ok, g, 0.0)
                dx[at, lane] = g + jnp.where(ok, out[k], 0.0)
        conv_pass(load_grad, lambda a, b: row8(tab, CPE + (a + 1) * 3 + b + 1, lg), 1, emit, flip=True)
        gsum[ds(8 * CPEB, 8), lane] += bias[0]
        return c
    lax.fori_loop(0, 8, body, 0)


def col_sum(src, gsum, row):
    def body(i, c):
        at = pl.ds(pl.multiple_of(i * 32, 16), 32)
        add_rows(gsum, row, src[at, :].astype(F32))
        return c
    lax.fori_loop(0, 41, body, 0)


def bwd_e_kernel(dx3, tab, wproj, w1, w2, a_low, n2, inv2, h2, g, slope,
                 dx2, da, gw1, gw2, gproj, gsum, gb1, dm, up):
    gsum[...] = jnp.zeros_like(gsum)
    dx2[...] = dx3[...]
    bwd_du(dx2, w2, slope, dm, gb1)
    col_sum(dm, gsum, 7)
    wgrad(g, dm, gw2)
    wgrad(h2, slope, gw1)
    mm_nt(slope, w1, up)
    norm_back_phase(up, n2, inv2, tab, 2, dx2, dm, gsum, 2, 3, None)
    col_sum(dm, gsum, 6)
    wgrad(a_low, dm, gproj)
    mm_nt(dm, wproj, da, True)
    da[:, R:RP, :] = jnp.zeros((4, RP - R, 128), F32)


def bwd_f_kernel(x, sz, tab, wqkv, n1, inv1, h1, q, p, v, s, rel, dx2, da, gsum_in,
                 dx, gqkv, gsum, dq, dk, dv, dj, up):
    gsum[...] = gsum_in[...]
    bwd_attn1(q, p, v, s, da, dq, dv, dk)
    bwd_mix(q, p, v, rel, da, dq, dv, dk, dj, sz, tab, gsum, None)
    wgrad(h1, dj, gqkv)
    mm_nt(dj, wqkv, up)
    norm_back_phase(up, n1, inv1, tab, 0, dx2, None, gsum, 0, 1, None)
    bwd_conv1(x, dx2, dx, sz, tab, gsum)


def bwd_layer(dx3, x, sz, tab, b1, wqkv, wproj, w1, w2, res):
    sd = jax.ShapeDtypeStruct
    r = dict(zip([n for n, _, _ in RES], res))
    dx2, da, gw1, gw2, gproj, gsum, gb1 = pl.pallas_call(
        bwd_e_kernel,
        out_shape=[sd((R, D), F32), sd((4, RP, 128), F32), sd((D, FF), BF16), sd((FF, D), BF16), sd((D, D), BF16), sd((8 * TROWS, D), F32), sd((8, FF), F32)],
        in_specs=vspec(11), out_specs=vspec(7),
        scratch_shapes=[pltpu.VMEM((R, D), BF16), pltpu.VMEM((R, D), F32)],
        compiler_params=PARAMS, name="block_bwd_e",
    )(dx3, tab, wproj, w1, w2, r["a"], r["n2"], r["inv2"], r["h2"], r["g"], r["slope"])
    dx, gqkv, gsum = pl.pallas_call(
        bwd_f_kernel,
        out_shape=[sd((R, D), F32), sd((D, 3 * D), BF16), sd((8 * TROWS, D), F32)],
        in_specs=vspec(15), out_specs=vspec(3),
        scratch_shapes=[pltpu.VMEM((4, RP, 128), F32)] * 3 + [pltpu.VMEM((R, 3 * D), BF16), pltpu.VMEM((R, D), F32)],
        compiler_params=PARAMS, name="block_bwd_f",
    )(x, sz, tab, wqkv, r["n1"], r["inv1"], r["h1"], r["q"], r["p"], r["v"], r["s"], r["rel"], dx2, da, gsum)
    return dx, gqkv, gproj, gw1, gw2, gsum, gb1


AXES = ("wide", "narrow")


def window_mask():
    channel = lax.broadcasted_iota(jnp.int32, (49, D), 1)
    tap = lax.broadcasted_iota(jnp.int32, (49, D), 0)
    head = channel // (D // HEADS)
    reach = jnp.where(head < 2, 1, jnp.where(head < 5, 2, 3))
    return ((jnp.abs(tap // 7 - 3) <= reach) & (jnp.abs(tap % 7 - 3) <= reach)).astype(F32)


def blocks_of(flat, rows, cols):
    return flat.reshape(rows, cols // D, D).transpose(1, 0, 2).reshape(rows * cols // D, D)


def pack(qkv, proj, fc1, fc2, small, n):
    per = D // n
    width = small.shape[0]
    pad = -width % D
    parts = [blocks_of(qkv, per, 3 * D), proj.reshape(per, D), blocks_of(fc1, per, FF), fc2.reshape(FF // n, D), jnp.pad(small, (0, pad)).reshape(-1, D)]
    return jnp.concatenate(parts)


def unpack(full, n, small_count):
    per = D // n

    def block(j):
        return full[:, j * per:(j + 1) * per].reshape(D, D)
    wqkv = jnp.concatenate([block(0), block(1), block(2)], axis=1)
    w1 = jnp.concatenate([block(4 + j) for j in range(4)], axis=1)
    w2 = full[:, 8 * per:8 * per + FF // n].reshape(FF, D)
    small = full[:, 8 * per + FF // n:].reshape(n, -1)[:, :small_count].reshape(-1)
    return wqkv, block(3), w1, w2, small


def pack_grads(gqkv, gproj, gw1, gw2, small, n):
    per = D // n
    width = small.shape[0] // n
    pad = -width % D
    cols = [gqkv[:, j * D:(j + 1) * D] for j in range(3)] + [gproj] + [gw1[:, j * D:(j + 1) * D] for j in range(4)]
    parts = [c.reshape(n, per, D) for c in cols] + [gw2.reshape(n, FF // n, D)]
    parts.append(jnp.pad(small.reshape(n, width), ((0, 0), (0, pad))).reshape(n, -1, D).astype(BF16))
    return jnp.concatenate(parts, axis=1)


def split_grads(shard, n, width):
    per = D // n

    def cols(first, count):
        return shard[first * per:(first + count) * per].reshape(count, per, D).transpose(1, 0, 2).reshape(-1)
    fc2 = shard[8 * per:8 * per + FF // n].reshape(-1)
    small = shard[8 * per + FF // n:].reshape(-1)[:width]
    return cols(0, 3), cols(3, 1), cols(4, 4), fc2, small


def tables(small):
    small = small.astype(F32)
    end = TABLE * D
    tb = small[:end].reshape(D, TABLE).T
    cpe = small[end + FF:].reshape(D, 10).T
    tab = jnp.concatenate([tb[:9], tb[9:] * window_mask(), cpe, jnp.zeros((TROWS - 68, D), F32)])
    return tab.reshape(TROWS, 4, 128).transpose(1, 0, 2), small[end:end + FF][None]


def small_grads(gsum, gb1):
    s = gsum.reshape(TROWS, 8, D).sum(1)
    tb = jnp.concatenate([s[:9], s[9:58] * window_mask()]).T
    return jnp.concatenate([tb.reshape(-1), gb1.sum(0), s[58:68].T.reshape(-1)])


def to_rows(a):
    return jnp.transpose(a, (1, 0, 2)).reshape(R, D)


def from_rows(a):
    return jnp.transpose(a.reshape(SLOT, NI, D), (1, 0, 2))


def shards(n, images, grid_sizes, qkv, proj, fc1, fc2, small, cotangent):
    layers = qkv.shape[0]
    width = small.shape[1]
    packed = [pack(qkv[l], proj[l], fc1[l], fc2[l], small[l], n) for l in range(layers)]
    slot = lax.broadcasted_iota(jnp.int32, (SLOT, 1), 0)
    cellno = jnp.maximum(slot - 1, 0)
    far = jnp.maximum(cellno // GRID, cellno % GRID)
    present = ((slot == 0) | (far < grid_sizes[None, :]))[:, :, None]
    sz = jnp.broadcast_to(grid_sizes[:, None], (NI, 128))
    x = to_rows(images)
    saved = []
    for l in range(layers):
        full = lax.all_gather(packed[l][None], AXES, axis=0, tiled=True)
        wqkv, wproj, w1, w2, vec = unpack(full, n, width)
        tab, b1 = tables(vec)
        out = fwd_layer(x, sz, tab, b1, wqkv, wproj, w1, w2)
        saved.append((x, tab, b1, wqkv, wproj, w1, w2, out[1:]))
        x = out[0]
    output = from_rows(jnp.where(present, x.reshape(SLOT, NI, D), 0.0).astype(BF16))
    dx = jnp.where(present, jnp.transpose(cotangent, (1, 0, 2)), 0).astype(F32).reshape(R, D)
    shares = [None] * layers
    for l in reversed(range(layers)):
        xin, tab, b1, wqkv, wproj, w1, w2, res = saved[l]
        dx, gqkv, gproj, gw1, gw2, gsum, gb1 = bwd_layer(dx, xin, sz, tab, b1, wqkv, wproj, w1, w2, res)
        g = pack_grads(gqkv, gproj, gw1, gw2, small_grads(gsum, gb1), n)
        shares[l] = split_grads(lax.psum_scatter(g, AXES, scatter_dimension=0, tiled=True)[0].astype(F32), n, width)
    grads = [jnp.stack([shares[l][i] for l in range(layers)]) for i in range(5)]
    return (output, from_rows(dx), *grads)


def solution(mesh):
    n = mesh.shape["wide"] * mesh.shape["narrow"]
    from jax.sharding import PartitionSpec as P
    rows, flat = P(AXES, None, None), P(None, AXES)
    return jax.shard_map(
        functools.partial(shards, n), mesh=mesh,
        in_specs=(rows, P(AXES), flat, flat, flat, flat, flat, rows),
        out_specs=(rows, rows, flat, flat, flat, flat, flat),
        check_vma=False)
```

time: 1640 us -> 835 us (0.51)
  other arithmetic: 516 us -> 25.2 us
  Pallas kernels: 0 us -> 312 us
  local copies, waits for them, and re-layouts: 309 us -> 56.1 us
  matrix products: 226 us -> 0 us
  blocking collectives: 170 us -> 0 us
  waiting for transfers between devices: 387 us -> 420 us
    unnamed x8 -> x4, waiting for transfers between devices: 387 us -> 0.07 us
    pallas_call x0 -> x6, Pallas kernels: none -> 312 us  [the longest x2 130 us: fwd_layer(): pl.pallas_call(fwd_kernel, out_shape=outs, in_specs=vspec(8), out_specs=v...]
    reduce_scatter x0 -> x2, waiting for transfers between devices: none -> 278 us  [shards(): lax.psum_scatter(g, AXES, scatter_dimension=0, tiled=True)[0].astype(F32)]
    all_gather x8 -> x0, other arithmetic: 278 us -> none  [the longest x2 91.8 us: shards(): lax.all_gather(fc2_weight[layer_index], ('wide', 'narrow'), axis=0, tiled...]
    dot_general x36 -> x0, matrix products: 226 us -> none  [the longest x8 58.6 us: back_dot(): lax.dot_general(left_rows, matrix, (((1,), (1,)), ((), ())), preferred_el...]
    all_gather x4 -> x0, blocking collectives: 170 us -> none  [the longest x2 88.4 us: shards(): lax.all_gather(proj_weight[layer_index], ('wide', 'narrow'), axis=0, tile...]
    reshape x48 -> x24, local copies, waits for them, and re-layouts: 159 us -> 4.23 us  [the longest x2 1.34 us: tables(): tab.reshape(TROWS, 4, 128).transpose(1, 0, 2)]
    all_gather x6 -> x2, waiting for transfers between devices: 0.03 us -> 142 us  [shards(): full = lax.all_gather(packed[l][None], AXES, axis=0, tiled=True)]
  transfers between devices with their start and end apart: 7 -> 4, of which waited for: 1 -> 4; matrix products, arithmetic and copies ran while one was open for 32% -> 2% of each run, Pallas kernels for 0% -> 0%
where the time goes in v1:
time: 835 us; the launch traced here: 829 us
  waiting for transfers between devices  420 us (50%)
  Pallas kernels  312 us (37%)
  local copies, waits for them, and re-layouts  56.1 us (7%)
  other arithmetic  25.2 us (3%)
  between operations  15.1 us (2%)
    reduce_scatter x2, waiting for transfers between devices, shards(): lax.psum_scatter(g, AXES, scatter_dimension=0, tiled=True)[0].astype(F32)  278 us
    all_gather x2, waiting for transfers between devices, shards(): full = lax.all_gather(packed[l][None], AXES, axis=0, tiled=True)  142 us
    pallas_call x2, Pallas kernels, fwd_layer(): pl.pallas_call(fwd_kernel, out_shape=outs, in_specs=vspec(8), out_specs=v...  130 us
    pallas_call x2, Pallas kernels, bwd_layer(): pl.pallas_call(bwd_f_kernel, out_shape=[sd((R, D), F32), sd((D, 3 * D), B...  110 us
    pallas_call x2, Pallas kernels, bwd_layer(): pl.pallas_call(bwd_e_kernel, out_shape=[sd((R, D), F32), sd((4, RP, 128),...  71.9 us
    unnamed x84, local copies, waits for them, and re-layouts  19.3 us
  transfers between devices with their start and end apart: 4, of which 4 were waited for; matrix products, arithmetic and copies ran while one was open for 2% of the time, Pallas kernels for 0%

profile of v1, /device:TPU:0, one launch (start us, length us, event | category | flops | bytes accessed | tf_op | source)
XLA Modules:
  0.0 829.2 jit_solution(945520424259391941)
XLA Ops:
  8.1 1.0 slice_reduce_fusion.6
  9.1 1.5 slice_reduce_fusion.4
  10.7 1.7 slice_reduce_fusion.1
  12.5 1.7 slice_reduce_fusion
  17.2 71.1 %all-gather.7.cloned.1.call-done = bf16[32,195,512]{2,1,0:T(8,128)(2,1)} async-done(((bf16[1,195,512]{2,1,0:T(8,128)(2,1)}), bf16[32,195,512]{2,1,0:T(8,128)(2,1)}) %all-gather.7.cloned.1.call-update) | async-done | bytes 6389776 | tf_op jit(solution)/shard_map/all_gather | solution.py:676
  89.9 70.7 %all-gather.9.cloned.1.call-done = bf16[32,195,512]{2,1,0:T(8,128)(2,1)} async-done(((bf16[1,195,512]{2,1,0:T(8,128)(2,1)}), bf16[32,195,512]{2,1,0:T(8,128)(2,1)}) %all-gather.9.cloned.1.call-update) | async-done | bytes 6389776 | tf_op jit(solution)/shard_map/all_gather | solution.py:676
  165.5 3.9 fusion.9
  169.4 1.3 pad_maximum_fusion.3.wqkv
  170.7 1.5 fusion.10
  172.2 1.2 pad_maximum_fusion.2.wqkv
  173.4 1.6 pad_maximum_fusion.1.w1
  175.1 1.6 pad_maximum_fusion.w1
  176.7 1.6 slice.325
  179.0 65.4 %block_fwd.2 = (f32[1312,512]{1,0:T(8,128)}, bf16[1312,512]{1,0:T(8,128)(2,1)}, f32[1312,128]{1,0:T(8,128)}, bf16[1312,512]{1,0:T(8,128)(2,1)}, f32[4,1536,128]{...) custom-call(bf16[1312,512]{1,0:T(8,128)(2,1)} %bitcast.136, ...), custom_call_target="tpu_custom_call" | custom-call | tf_op jit(solution)/shard_map/block_fwd/pallas_call | solution.py:338
  244.4 3.2 slice.341
  247.6 65.0 %block_fwd.3 = (f32[1312,512]{1,0:T(8,128)}, bf16[1312,512]{1,0:T(8,128)(2,1)}, f32[1312,128]{1,0:T(8,128)}, bf16[1312,512]{1,0:T(8,128)(2,1)}, f32[4,1536,128]{...) custom-call(f32[1312,512]{1,0:T(8,128)} %get-tuple-element.57.x, ...), custom_call_target="tpu_custom_call" | custom-call | tf_op jit(solution)/shard_map/block_fwd/pallas_call | solution.py:338
  312.6 3.7 bitcast_select_fusion
  316.3 2.1 bitcast_convert_fusion.dx3
  318.4 36.1 %block_bwd_e.2 = (f32[1312,512]{1,0:T(8,128)}, f32[4,1536,128]{2,1,0:T(8,128)}, bf16[512,2048]{1,0:T(8,128)(2,1)}, bf16[2048,512]{1,0:T(8,128)(2,1)}, bf16[512,5...) custom-call(f32[1312,512]{1,0:T(8,128)} %bitcast_convert_fusion.dx3, f32[4,72,128]{2,1,0:T(8,128)} %bitcast.144, ...), custom_call_target="tpu_custom_call" | custom-call | tf_op jit(solution)/shard_map/block_bwd_e/pallas_call | solution.py:569
  354.5 55.0 %block_bwd_f.2 = (f32[1312,512]{1,0:T(8,128)}, bf16[512,1536]{1,0:T(8,128)(2,1)}, f32[576,512]{1,0:T(8,128)}) custom-call(f32[1312,512]{1,0:T(8,128)} %get-tuple-element.57.x, s32[16,128]{1,0:T(8,128)} %broadcast_in_dim.58.sz, f32[4,72,128]{2,1,0:T(8,128)} %bitcast.145, bf16[512,1536]{1,0:T(8,128)(2,1)} %pad_maximum_fusion.3.wqkv, ...), custom_call_target="tpu_custom_call" | custom-call | tf_op jit(solution)/shard_map/block_bwd_f/pallas_call | solution.py:576
  409.5 1.6 bitcast_reduce_fusion
  412.3 1.5 reduce_sum.39
  413.8 35.8 %block_bwd_e.3 = (f32[1312,512]{1,0:T(8,128)}, f32[4,1536,128]{2,1,0:T(8,128)}, bf16[512,2048]{1,0:T(8,128)(2,1)}, bf16[2048,512]{1,0:T(8,128)(2,1)}, bf16[512,5...) custom-call(f32[1312,512]{1,0:T(8,128)} %get-tuple-element.84.dx3, f32[4,72,128]{2,1,0:T(8,128)} %bitcast.147, ...), custom_call_target="tpu_custom_call" | custom-call | tf_op jit(solution)/shard_map/block_bwd_e/pallas_call | solution.py:569
  449.6 55.1 %block_bwd_f.3 = (f32[1312,512]{1,0:T(8,128)}, bf16[512,1536]{1,0:T(8,128)(2,1)}, f32[576,512]{1,0:T(8,128)}) custom-call(bf16[1312,512]{1,0:T(8,128)(2,1)} %bitcast.137, s32[16,128]{1,0:T(8,128)} %broadcast_in_dim.58.sz, f32[4,72,128]{2,1,0:T(8,128)} %bitcast.148, bf16[512,1536]{1,0:T(8,128)(2,1)} %pad_maximum_fusion.2.wqkv, ...), custom_call_target="tpu_custom_call" | custom-call | tf_op jit(solution)/shard_map/block_bwd_f/pallas_call | solution.py:576
  504.7 1.7 bitcast_reduce_fusion.1
  506.4 1.0 fusion.2
  510.5 1.5 fusion.14
  519.1 1.6 constant_dynamic-update-slice_fusion.21
  530.5 1.5 constant_dynamic-update-slice_fusion.11
  532.7 133.9 %reduce-scatter.5.cloned.1.call-done = bf16[1,195,512]{2,1,0:T(8,128)(2,1)} async-done(((bf16[32,195,512]{2,1,0:T(8,128)(2,1)}), bf16[1,195,512]{2,1,0:T(8,128)(2,1)}) %reduce-scatter.5.cloned.1.call-update) | async-done | bytes 199696 | tf_op jit(solution)/shard_map/reduce_scatter | solution.py:689
  667.7 144.1 %reduce-scatter.3.cloned.1.call-done = bf16[1,195,512]{2,1,0:T(8,128)(2,1)} async-done(((bf16[32,195,512]{2,1,0:T(8,128)(2,1)}), bf16[1,195,512]{2,1,0:T(8,128)(2,1)}) %reduce-scatter.3.cloned.1.call-update) | async-done | bytes 199696 | tf_op jit(solution)/shard_map/reduce_scatter | solution.py:689
  811.7 1.0 convert_element_type.50
  (200 shorter events, 42.7 us)
Async XLA Ops:
  7.2 9.0 %copy-start.14 = (s32[16]{0:T(128)S(1)}, s32[16]{0:T(128)}, u32[]{:S(2)}) copy-start(s32[16]{0:T(128)} %param.9) | copy-start | bytes 196
  7.2 81.1 %all-gather.7.cloned.1.call-start = ((), (), s32[]{:S(2)}) async-start(), calls=%async_computation.4 | async-start | bytes 6758400 | tf_op jit(solution)/shard_map/all_gather | solution.py:676
  14.3 0.7 copy-start.9
  15.0 145.6 %all-gather.9.cloned.1.call-start = ((), (), s32[]{:S(2)}) async-start(), calls=%async_computation.5 | async-start | bytes 6758400 | tf_op jit(solution)/shard_map/all_gather | solution.py:676
  15.4 0.7 copy-start.10
  16.1 650.6 %reduce-scatter.5.cloned.1.call-start = ((), (), s32[]{:S(2)}) async-start(), calls=%async_computation.3 | async-start | bytes 6758400 | tf_op jit(solution)/shard_map/reduce_scatter | solution.py:689
  17.0 147.0 %copy-start.15 = (pred[512]{0:T(512)(128)(4,1)}, pred[512]{0:T(512)(128)(4,1)S(1)}, u32[]{:S(2)}) copy-start(pred[512]{0:T(512)(128)(4,1)S(1)} %fusion.7) | copy-start | bytes 1540
  17.1 147.0 %copy-start.16 = (s32[49]{0:T(128)}, s32[49]{0:T(128)S(1)}, u32[]{:S(2)}) copy-start(s32[49]{0:T(128)S(1)} %get-tuple-element.161) | copy-start | bytes 592
  17.1 147.0 %copy-start.17 = (s32[49]{0:T(128)}, s32[49]{0:T(128)S(1)}, u32[]{:S(2)}) copy-start(s32[49]{0:T(128)S(1)} %get-tuple-element.162) | copy-start | bytes 592
  17.1 147.0 %copy-start.18 = (s32[49]{0:T(128)}, s32[49]{0:T(128)S(1)}, u32[]{:S(2)}) copy-start(s32[49]{0:T(128)S(1)} %get-tuple-element.159) | copy-start | bytes 592
  17.1 147.0 %copy-start.19 = (s32[49]{0:T(128)}, s32[49]{0:T(128)S(1)}, u32[]{:S(2)}) copy-start(s32[49]{0:T(128)S(1)} %get-tuple-element.160) | copy-start | bytes 592
  17.1 147.0 %copy-start.20 = (pred[49]{0:T(512)(128)(4,1)}, pred[49]{0:T(512)(128)(4,1)S(1)}, u32[]{:S(2)}) copy-start(pred[49]{0:T(512)(128)(4,1)S(1)} %get-tuple-element.157) | copy-start | bytes 151
  17.1 147.0 %copy-start.21 = (pred[49]{0:T(512)(128)(4,1)}, pred[49]{0:T(512)(128)(4,1)S(1)}, u32[]{:S(2)}) copy-start(pred[49]{0:T(512)(128)(4,1)S(1)} %get-tuple-element.158) | copy-start | bytes 151
  17.2 147.0 %copy-start.12 = (s32[512]{0:T(512)}, s32[512]{0:T(512)S(1)}, u32[]{:S(2)}) copy-start(s32[512]{0:T(512)S(1)} %get-tuple-element.155) | copy-start | bytes 6148
  17.2 147.0 %copy-start.13 = (s32[512]{0:T(512)}, s32[512]{0:T(512)S(1)}, u32[]{:S(2)}) copy-start(s32[512]{0:T(512)S(1)} %get-tuple-element.156) | copy-start | bytes 6148
  164.8 5.9 slice-start
  165.5 5.2 slice-start.1
  411.1 0.6 copy-start.8
  504.7 7.3 copy-start.3
  512.0 2.8 copy-start.7
  513.9 5.2 copy-start.2
  521.4 0.8 copy-start.11
  521.4 1.8 copy-start.4
  521.5 290.3 %reduce-scatter.3.cloned.1.call-start = ((), (), s32[]{:S(2)}) async-start(), calls=%async_computation.2 | async-start | bytes 6758400 | tf_op jit(solution)/shard_map/reduce_scatter | solution.py:689
  523.3 2.7 copy-start.6
  523.3 3.6 copy-start.1
  527.0 3.5 copy-start
  811.7 5.9 copy-start.5
Sparse Core Ops, SparseCore 0:
  15.1 73.0 all-gather.6
  91.7 68.8 all-gather.8
  521.6 145.0 reduce-scatter.4
  668.8 142.8 reduce-scatter.2

commit v2 on v1

--- a/solution.py
+++ b/solution.py
@@ -14,7 +14,9 @@
 PADS = 96
 RP = PADS * NI
 RADII = (1, 2, 3, 3)
-TAPS, CPE, CPEB, TROWS = 9, 58, 67, 72
+AXES = ("wide", "narrow")
+WROWS = 192
+TAPS, CPE, CPEB, TROWS = 9, 64, 73, 80
 
 
 def ds(start, size, align=8):
@@ -166,15 +168,24 @@
     lax.fori_loop(0, 12, body, 0)
 
 
+def weight(g, block, first, count, cols):
+    at = ds(16 * block, 16, 16)
+    return jnp.concatenate([g[t % 2, t // 8, t // 4 % 2, t // 2 % 2, at, cols] for t in range(first // 16, (first + count) // 16)], axis=0)
+
+
+def weight2(g, chunk, cols):
+    return jnp.concatenate([g[i % 2, chunk // 2, chunk % 2, i // 2, 128:192, cols] for i in range(4)], axis=0)
+
+
 def fwd_qkv(low, w, tab, q, k, v):
     def body(i, c):
         at = pl.ds(tile_start(i, ROW_T), ROW_T)
         h = low[at, :]
         for j in range(2):
             cols = slice(256 * j, 256 * j + 256)
-            put2(q, at, j, dot(h, w[:, cols], 1, 0) + row(tab, 4, j))
-            put2(k, at, j, dot(h, w[:, 512 + 256 * j:768 + 256 * j], 1, 0))
-            put2(v, at, j, dot(h, w[:, 1024 + 256 * j:1280 + 256 * j], 1, 0) + row(tab, 5, j))
+            put2(q, at, j, dot(h, weight(w, 0, 0, D, cols), 1, 0) + row(tab, 4, j))
+            put2(k, at, j, dot(h, weight(w, 1, 0, D, cols), 1, 0))
+            put2(v, at, j, dot(h, weight(w, 2, 0, D, cols), 1, 0) + row(tab, 5, j))
         return c
     lax.fori_loop(0, 4, body, 0)
     tail = slice(R, RP)
@@ -275,7 +286,7 @@
         a_low[at, :] = low
         for j in range(2):
             cols = slice(256 * j, 256 * j + 256)
-            x1[at, cols] = x1[at, cols] + dot(low, w[:, cols], 1, 0) + row(tab, 6, j)
+            x1[at, cols] = x1[at, cols] + dot(low, weight(w, 3, 0, D, cols), 1, 0) + row(tab, 6, j)
         return c
     lax.fori_loop(0, 2, body, 0)
 
@@ -285,7 +296,9 @@
         i, j = t // 8, t % 8
         at = pl.ds(tile_start(i, ROW_T), ROW_T)
         cols = pl.ds(pl.multiple_of(j * 256, 256), 256)
-        u = dot(low[at, :], w[:, cols], 1, 0) + b1[:, cols]
+        half = pl.ds(pl.multiple_of(j % 2 * 256, 256), 256)
+        bias = jnp.concatenate([b1[pl.ds(2 * j, 1), :], b1[pl.ds(2 * j + 1, 1), :]], axis=1)
+        u = dot(low[at, :], weight(w, 4 + j // 2, 0, D, half), 1, 0) + bias
         cdf, e = normal_cdf(u)
         g[at, cols] = (u * cdf).astype(BF16)
         slope[at, cols] = (cdf + u * e * 0.3989422804014327).astype(BF16)
@@ -294,28 +307,35 @@
 
 
 def fwd_fc2(g, w, tab, x2, x3):
-    def body(i, c):
+    def body(i, _):
         at = pl.ds(pl.multiple_of(i * 656, 16), 656)
         for j in range(2):
             cols = slice(256 * j, 256 * j + 256)
-            x3[at, cols] = x2[at, cols] + dot(g[at, :], w[:, cols], 1, 0) + row(tab, 7, j)
-        return c
+            x3[at, cols] = x2[at, cols] + dot(g[at, :], jnp.concatenate([weight2(w, c, cols) for c in range(8)], axis=0), 1, 0) + row(tab, 7, j)
+        return _
     lax.fori_loop(0, 2, body, 0)
 
 
-def fwd_kernel(x, sz, tab, b1, wqkv, wproj, w1, w2,
-               x3, n1, inv1, h1, q, p, v, s, rel, a_low, n2, inv2, h2, g, slope,
-               x1, f):
+def fwd_phases(x, sz, tab, b1, w, x3, n1, inv1, h1, q, p, v, s, rel, a_low, n2, inv2, h2, g, slope, x1, f, tick=lambda: None):
     fwd_conv1(x, sz, tab, x1)
     norm_phase(x1, tab, 0, 1, n1, h1, inv1)
-    fwd_qkv(h1, wqkv, tab, q, p, v)
+    tick(0)
+    fwd_qkv(h1, w, tab, q, p, v)
+    tick(1)
     fwd_softmax(p, sz)
+    tick(2)
     fwd_attn(q, p, v, s, f)
+    tick(3)
     fwd_conv3(v, q, f, sz, tab, rel, f)
-    fwd_proj(f, wproj, tab, x1, a_low)
+    tick(4)
+    fwd_proj(f, w, tab, x1, a_low)
+    tick(5)
     norm_phase(x1, tab, 2, 3, n2, h2, inv2)
-    fwd_fc1(h2, w1, b1, g, slope)
-    fwd_fc2(g, w2, tab, x1, x3)
+    tick(6)
+    fwd_fc1(h2, w, b1, g, slope)
+    tick(7)
+    fwd_fc2(g, w, tab, x1, x3)
+    tick(8)
 
 
 RES = (
@@ -333,13 +353,237 @@
 PARAMS = pltpu.CompilerParams(vmem_limit_bytes=67043328)
 
 
-def fwd_layer(x, sz, tab, b1, wqkv, wproj, w1, w2):
+MESH = pl.DeviceIdType.MESH
+
+
+class Place:
+    def __init__(self, line):
+        w, m = lax.axis_index("wide"), lax.axis_index("narrow")
+        self.line = line
+        self.z, self.x, self.y, self.c = w // 2, w % 2, m // 2, m % 2
+
+    def dev(self, z=None, x=None, y=None, c=None):
+        z = self.z if z is None else z
+        x = self.x if x is None else x
+        y = self.y if y is None else y
+        c = self.c if c is None else c
+        return (z * 2 + x, y * 2 + c)
+
+    def neighbours(self):
+        n = self.line
+        return (self.dev(x=1 - self.x), self.dev(y=1 - self.y), self.dev(c=1 - self.c),
+                self.dev(z=lax.rem(self.z + 1, n)), self.dev(z=lax.rem(self.z + n - 1, n)))
+
+
+def greet(place):
+    barrier = pltpu.get_barrier_semaphore()
+    for who in place.neighbours():
+        pl.semaphore_signal(barrier, inc=1, device_id=who, device_id_type=MESH)
+    pl.semaphore_wait(barrier, 5)
+
+
+def remote(src, dst, send, recv, dev):
+    return pltpu.make_async_remote_copy(src_ref=src, dst_ref=dst, send_sem=send, recv_sem=recv, device_id=dev, device_id_type=MESH)
+
+
+def gather_ticks(place, g, rows, send, recv):
+    n, z, x, y, c = place.line, place.z, place.x, place.y, place.c
+    xs, ys, cs = 0, 1, 2
+
+    def swap(core, sem, mine, dev):
+        return remote(mine, mine, send.at[sem], recv.at[sem], dev)
+
+    def pair_x(whole):
+        part = g.at[1, :, x, :, rows] if whole else g.at[0, z, x, y, rows]
+        return swap(0, xs, part, place.dev(x=1 - x))
+
+    def pair_y(whole):
+        part = g.at[1, :, x, y, rows] if whole else g.at[0, z, :, y, rows]
+        return swap(0, ys, part, place.dev(y=1 - y))
+
+    def line(core, k):
+        def part(at):
+            at = jnp.clip(at, 0, n - 1)
+            return g.at[0, at, :, :, rows] if core == 0 else g.at[1, at, x, y, rows]
+        right = remote(part(z - k + 1), part(z - k + 1), send.at[2 + k], recv.at[2 + k], place.dev(z=jnp.minimum(z + 1, n - 1)))
+        left = remote(part(z + k - 1), part(z + k - 1), send.at[1 + n + k], recv.at[1 + n + k], place.dev(z=jnp.maximum(z - 1, 0)))
+        return (right, (z + 1 < n) & (z - k + 1 >= 0), z - k >= 0), (left, (z > 0) & (z + k - 1 < n), z + k < n)
+
+    def start_line(core, k):
+        for copy, sends, _ in line(core, k):
+            pl.when(sends)(copy.start)
+
+    def wait_line(core, k):
+        for copy, sends, gets in line(core, k):
+            pl.when(sends)(copy.wait_send)
+            pl.when(gets)(copy.wait_recv)
+
+    def both(copy):
+        copy.wait_send()
+        copy.wait_recv()
+
+    def core_copy(which):
+        return remote(g.at[which, :, :, :, rows], g.at[which, :, :, :, rows], send.at[cs], recv.at[cs], place.dev(c=1 - c))
+
+    first, second = [], []
+    first.append(lambda: pair_x(False).start())
+    first.append(lambda: (both(pair_x(False)), pair_y(False).start()))
+    first.append(lambda: (both(pair_y(False)), start_line(0, 1)))
+    for k in range(1, n - 1):
+        first.append(lambda k=k: (wait_line(0, k), start_line(0, k + 1)))
+    first.append(lambda: (wait_line(0, n - 1), core_copy(0).start()))
+    first.append(lambda: both(core_copy(0)))
+    second.append(lambda: start_line(1, 1))
+    for k in range(1, n - 1):
+        second.append(lambda k=k: (wait_line(1, k), start_line(1, k + 1)))
+    second.append(lambda: (wait_line(1, n - 1), pair_y(True).start()))
+    second.append(lambda: (both(pair_y(True)), pair_x(True).start()))
+    second.append(lambda: (both(pair_x(True)), core_copy(1).start()))
+    second.append(lambda: both(core_copy(1)))
+    assert len(first) == len(second)
+
+    def tick(a, b):
+        def run():
+            @pl.when(c == 0)
+            def _():
+                a()
+
+            @pl.when(c == 1)
+            def _():
+                b()
+        return run
+    return [tick(a, b) for a, b in zip(first, second)]
+
+
+def wave(lists):
+    for r in range(max(i + len(t) for i, t in enumerate(lists))):
+        for i, t in enumerate(lists):
+            if 0 <= r - i < len(t):
+                t[r - i]()
+
+
+def gather_kernel(line, chunks, shard, g, own, send, recv):
+    place = Place(line)
+    mine = pltpu.make_async_copy(shard, g.at[place.c, place.z, place.x, place.y], own)
+    mine.start()
+    greet(place)
+    mine.wait()
+    wave([gather_ticks(place, g, pl.ds(a, b - a), send.at[i], recv.at[i]) for i, (a, b) in enumerate(chunks)])
+
+
+def gather(shard, line, chunks, cid):
+    rows = shard.shape[0]
+    sems = pltpu.SemaphoreType.DMA((len(chunks), 3 + 2 * (line - 1) + 1))
+    return pl.pallas_call(
+        functools.partial(gather_kernel, line, chunks),
+        out_shape=jax.ShapeDtypeStruct((2, line, 2, 2, rows, D), BF16),
+        in_specs=[pl.BlockSpec(memory_space=pltpu.VMEM)], out_specs=pl.BlockSpec(memory_space=pltpu.VMEM),
+        scratch_shapes=[pltpu.SemaphoreType.DMA, sems, sems],
+        compiler_params=pltpu.CompilerParams(collective_id=cid, has_side_effects=True, vmem_limit_bytes=67043328),
+        name="gather_weights")(shard)
+
+
+def add_into(dst, src, out=None):
+    out = dst if out is None else out
+    out[...] = (dst[...].astype(F32) + src[...].astype(F32)).astype(out.dtype)
+
+
+def build_tables(gs, layer, tau, y, tab, b1):
+    for t in range(32):
+        tau[9 * t:9 * t + 9, :] = gs[t % 2, t // 8, t // 4 % 2, t // 2 % 2, 16 * layer:16 * layer + 9, :]
+    lane = lax.broadcasted_iota(jnp.int32, (8, 128), 1)
+
+    def run(base, step, width, b):
+        first, off = width * b // 128, width * b % 128
+        val = tau[pl.ds(base + first, 8, stride=step), :]
+        if off:
+            val = pltpu.roll(val, 128 - off, 1)
+            if off + width > 128:
+                more = pltpu.roll(tau[pl.ds(base + first + 1, 8, stride=step), :], 128 - off, 1)
+                val = jnp.where(lane < 128 - off, val, more)
+        return val
+    for b in range(64):
+        tb = run(0, 29, TABLE, b)
+        cpe = pltpu.roll(run(248, 5, 10, b), 64, 1)
+        y[8 * b:8 * b + 8, :] = jnp.where(lane < TABLE, tb, jnp.where((lane >= 64) & (lane < 74), cpe, 0.0))
+    r = lax.broadcasted_iota(jnp.int32, (D, D), 0)
+    c = lax.broadcasted_iota(jnp.int32, (D, D), 1)
+    place = jnp.where(c == 64 * (r % 8) + r // 8, 1.0, 0.0).astype(BF16)
+    table = dot(y[...].astype(BF16), place, 0, 0)[:TROWS]
+    tap = lax.broadcasted_iota(jnp.int32, (TROWS, D), 0) - TAPS
+    head = lax.broadcasted_iota(jnp.int32, (TROWS, D), 1) // 64
+    reach = jnp.where(head < 2, 1, jnp.where(head < 5, 2, 3))
+    ok = (tap < 0) | (tap >= 49) | ((jnp.abs(tap // 7 - 3) <= reach) & (jnp.abs(tap % 7 - 3) <= reach))
+    table = jnp.where(ok, table, 0.0)
+    for g in range(4):
+        tab[layer, g] = table[:, 128 * g:128 * g + 128]
+    b1[layer] = tau[232:248, :]
+
+
+CHUNKS = ((0, 64), (64, 128), (128, 192))
+
+
+def first_kernel(line, x, sz, shard0, shard1, small,
+                 x3, n1, inv1, h1, q, p, v, s, rel, a_low, n2, inv2, h2, g, slope, w0, w1, tab, b1,
+                 x1, f, gs, tau, y, own, send, recv):
+    place = Place(line)
+    here = (place.c, place.z, place.x, place.y)
+    puts = [pltpu.make_async_copy(src, dst.at[here], own.at[i]) for i, (src, dst) in enumerate(((shard0, w0), (shard1, w1), (small, gs)))]
+    for cp in puts:
+        cp.start()
+    greet(place)
+    for cp in puts:
+        cp.wait()
+    lists = [gather_ticks(place, gs, slice(None), send.at[0], recv.at[0])]
+    lists += [gather_ticks(place, w0, pl.ds(a, b - a), send.at[1 + i], recv.at[1 + i]) for i, (a, b) in enumerate(CHUNKS)]
+    lists += [gather_ticks(place, w1, pl.ds(a, b - a), send.at[4 + i], recv.at[4 + i]) for i, (a, b) in enumerate(CHUNKS)]
+    depth = len(lists[0])
+    rounds = []
+    for r in range(depth + len(lists) - 1):
+        rounds.append([t[r - i] for i, t in enumerate(lists) if 0 <= r - i < depth])
+    todo = iter(rounds)
+    done = [0]
+
+    def advance(upto):
+        while done[0] < upto:
+            for t in next(todo):
+                t()
+            done[0] += 1
+    advance(depth)
+    for layer in range(2):
+        build_tables(gs, layer, tau, y, tab, b1)
+    need = {0: depth + 1, 6: depth + 3}
+
+    def tick(i):
+        advance(min(max(done[0] + 1, need.get(i, 0)), len(rounds)))
+    fwd_phases(x, sz, tab.at[0], b1.at[0], w0, x3, n1, inv1, h1, q, p, v, s, rel, a_low, n2, inv2, h2, g, slope, x1, f, tick)
+    advance(len(rounds))
+
+
+def fwd_kernel(x, sz, tab, b1, w, *refs):
+    fwd_phases(x, sz, tab, b1, w, *refs, tick=lambda i: None)
+
+
+def fwd_first(line, x, sz, shard0, shard1, small):
+    sd = jax.ShapeDtypeStruct
+    pack = (2, line, 2, 2)
+    outs = [sd((R, D), F32)] + [sd(sh, dt) for _, sh, dt in RES] + [sd(pack + (WROWS, D), BF16)] * 2 + [sd((2, 4, TROWS, 128), F32), sd((2, 16, 128), F32)]
+    sems = pltpu.SemaphoreType.DMA((7, 3 + 2 * (line - 1) + 1))
+    return pl.pallas_call(
+        functools.partial(first_kernel, line), out_shape=outs, in_specs=vspec(5), out_specs=vspec(len(outs)),
+        scratch_shapes=[pltpu.VMEM((R, D), F32), pltpu.VMEM((4, RP, 128), F32), pltpu.VMEM(pack + (32, 128), F32), pltpu.VMEM((288, 128), F32),
+                        pltpu.VMEM((D, 128), F32), pltpu.SemaphoreType.DMA((3,)), sems, sems],
+        compiler_params=pltpu.CompilerParams(vmem_limit_bytes=67043328, collective_id=0, has_side_effects=True), name="first_fwd",
+    )(x, sz, shard0, shard1, small)
+
+
+def fwd_layer(x, sz, tab, b1, w):
     outs = [jax.ShapeDtypeStruct((R, D), F32)] + [jax.ShapeDtypeStruct(sh, dt) for _, sh, dt in RES]
     return pl.pallas_call(
-        fwd_kernel, out_shape=outs, in_specs=vspec(8), out_specs=vspec(len(outs)),
+        fwd_kernel, out_shape=outs, in_specs=vspec(5), out_specs=vspec(len(outs)),
         scratch_shapes=[pltpu.VMEM((R, D), F32), pltpu.VMEM((4, RP, 128), F32)],
         compiler_params=PARAMS, name="block_fwd",
-    )(x, sz, tab, b1, wqkv, wproj, w1, w2)
+    )(x, sz, tab, b1, w)
 
 
 def add_rows(ref, row, val):
@@ -360,7 +604,7 @@
         i, j = t // 8, t % 8
         at = pl.ds(pl.multiple_of(i * 656, 16), 656)
         cols = pl.ds(pl.multiple_of(j * 256, 256), 256)
-        d = dot(dm[at, :], w2[cols, :], 1, 1) * slope[at, cols].astype(F32)
+        d = dot(dm[at, :], weight2(w2, j, slice(None)), 1, 1) * slope[at, cols].astype(F32)
         slope[at, cols] = d.astype(BF16)
         total = d[0:8]
         for k in range(1, 82):
@@ -391,11 +635,12 @@
     lax.fori_loop(0, 41, body, 0)
 
 
-def mm_nt(a, w, out, split=False):
+def mm_nt(a, g, first, blocks, out, split=False):
     def body(i, c):
         at = pl.ds(pl.multiple_of(i * 656, 16), 656)
         for j in range(2):
-            val = dot(a[at, :], w[256 * j:256 * j + 256, :], 1, 1)
+            w = jnp.concatenate([weight(g, first + b, 256 * j, 256, slice(None)) for b in range(blocks)], axis=1)
+            val = dot(a[at, :], w, 1, 1)
             if split:
                 put2(out, at, j, val)
             else:
@@ -536,54 +781,51 @@
     lax.fori_loop(0, 41, body, 0)
 
 
-def bwd_e_kernel(dx3, tab, wproj, w1, w2, a_low, n2, inv2, h2, g, slope,
+def bwd_e_kernel(dx3, tab, w, a_low, n2, inv2, h2, g, slope,
                  dx2, da, gw1, gw2, gproj, gsum, gb1, dm, up):
     gsum[...] = jnp.zeros_like(gsum)
     dx2[...] = dx3[...]
-    bwd_du(dx2, w2, slope, dm, gb1)
+    bwd_du(dx2, w, slope, dm, gb1)
     col_sum(dm, gsum, 7)
     wgrad(g, dm, gw2)
     wgrad(h2, slope, gw1)
-    mm_nt(slope, w1, up)
+    mm_nt(slope, w, 4, 4, up)
     norm_back_phase(up, n2, inv2, tab, 2, dx2, dm, gsum, 2, 3, None)
     col_sum(dm, gsum, 6)
     wgrad(a_low, dm, gproj)
-    mm_nt(dm, wproj, da, True)
+    mm_nt(dm, w, 3, 1, da, True)
     da[:, R:RP, :] = jnp.zeros((4, RP - R, 128), F32)
 
 
-def bwd_f_kernel(x, sz, tab, wqkv, n1, inv1, h1, q, p, v, s, rel, dx2, da, gsum_in,
+def bwd_f_kernel(x, sz, tab, w, n1, inv1, h1, q, p, v, s, rel, dx2, da, gsum_in,
                  dx, gqkv, gsum, dq, dk, dv, dj, up):
     gsum[...] = gsum_in[...]
     bwd_attn1(q, p, v, s, da, dq, dv, dk)
     bwd_mix(q, p, v, rel, da, dq, dv, dk, dj, sz, tab, gsum, None)
     wgrad(h1, dj, gqkv)
-    mm_nt(dj, wqkv, up)
+    mm_nt(dj, w, 0, 3, up)
     norm_back_phase(up, n1, inv1, tab, 0, dx2, None, gsum, 0, 1, None)
     bwd_conv1(x, dx2, dx, sz, tab, gsum)
 
 
-def bwd_layer(dx3, x, sz, tab, b1, wqkv, wproj, w1, w2, res):
+def bwd_layer(dx3, x, sz, tab, w, res):
     sd = jax.ShapeDtypeStruct
     r = dict(zip([n for n, _, _ in RES], res))
     dx2, da, gw1, gw2, gproj, gsum, gb1 = pl.pallas_call(
         bwd_e_kernel,
         out_shape=[sd((R, D), F32), sd((4, RP, 128), F32), sd((D, FF), BF16), sd((FF, D), BF16), sd((D, D), BF16), sd((8 * TROWS, D), F32), sd((8, FF), F32)],
-        in_specs=vspec(11), out_specs=vspec(7),
+        in_specs=vspec(9), out_specs=vspec(7),
         scratch_shapes=[pltpu.VMEM((R, D), BF16), pltpu.VMEM((R, D), F32)],
         compiler_params=PARAMS, name="block_bwd_e",
-    )(dx3, tab, wproj, w1, w2, r["a"], r["n2"], r["inv2"], r["h2"], r["g"], r["slope"])
+    )(dx3, tab, w, r["a"], r["n2"], r["inv2"], r["h2"], r["g"], r["slope"])
     dx, gqkv, gsum = pl.pallas_call(
         bwd_f_kernel,
         out_shape=[sd((R, D), F32), sd((D, 3 * D), BF16), sd((8 * TROWS, D), F32)],
         in_specs=vspec(15), out_specs=vspec(3),
         scratch_shapes=[pltpu.VMEM((4, RP, 128), F32)] * 3 + [pltpu.VMEM((R, 3 * D), BF16), pltpu.VMEM((R, D), F32)],
         compiler_params=PARAMS, name="block_bwd_f",
-    )(x, sz, tab, wqkv, r["n1"], r["inv1"], r["h1"], r["q"], r["p"], r["v"], r["s"], r["rel"], dx2, da, gsum)
+    )(x, sz, tab, w, r["n1"], r["inv1"], r["h1"], r["q"], r["p"], r["v"], r["s"], r["rel"], dx2, da, gsum)
     return dx, gqkv, gproj, gw1, gw2, gsum, gb1
-
-
-AXES = ("wide", "narrow")
 
 
 def window_mask():
@@ -598,24 +840,18 @@
     return flat.reshape(rows, cols // D, D).transpose(1, 0, 2).reshape(rows * cols // D, D)
 
 
-def pack(qkv, proj, fc1, fc2, small, n):
+def pack(qkv, proj, fc1, fc2, n):
     per = D // n
-    width = small.shape[0]
-    pad = -width % D
-    parts = [blocks_of(qkv, per, 3 * D), proj.reshape(per, D), blocks_of(fc1, per, FF), fc2.reshape(FF // n, D), jnp.pad(small, (0, pad)).reshape(-1, D)]
-    return jnp.concatenate(parts)
-
-
-def unpack(full, n, small_count):
+    return jnp.concatenate([blocks_of(qkv, per, 3 * D), proj.reshape(per, D), blocks_of(fc1, per, FF), fc2.reshape(FF // n, D)])
+
+
+def whole_weights(packed, small, n):
     per = D // n
-
-    def block(j):
-        return full[:, j * per:(j + 1) * per].reshape(D, D)
-    wqkv = jnp.concatenate([block(0), block(1), block(2)], axis=1)
-    w1 = jnp.concatenate([block(4 + j) for j in range(4)], axis=1)
-    w2 = full[:, 8 * per:8 * per + FF // n].reshape(FF, D)
-    small = full[:, 8 * per + FF // n:].reshape(n, -1)[:, :small_count].reshape(-1)
-    return wqkv, block(3), w1, w2, small
+    full = lax.all_gather(packed[None], AXES, axis=0, tiled=True)
+    vec = lax.all_gather(small, AXES, axis=0, tiled=True)
+    parts = [full[:, j * per:(j + 1) * per].reshape(32, D // 32, D) for j in range(8)] + [full[:, 8 * per:].reshape(32, FF // 32, D)]
+    w = jnp.concatenate(parts, axis=1).reshape(4, 2, 2, 2, WROWS, D).transpose(3, 0, 1, 2, 4, 5)
+    return w, *tables(vec)
 
 
 def pack_grads(gqkv, gproj, gw1, gw2, small, n):
@@ -643,14 +879,14 @@
     end = TABLE * D
     tb = small[:end].reshape(D, TABLE).T
     cpe = small[end + FF:].reshape(D, 10).T
-    tab = jnp.concatenate([tb[:9], tb[9:] * window_mask(), cpe, jnp.zeros((TROWS - 68, D), F32)])
-    return tab.reshape(TROWS, 4, 128).transpose(1, 0, 2), small[end:end + FF][None]
+    tab = jnp.concatenate([tb[:9], tb[9:] * window_mask(), jnp.zeros((CPE - TABLE, D), F32), cpe, jnp.zeros((TROWS - CPE - 10, D), F32)])
+    return tab.reshape(TROWS, 4, 128).transpose(1, 0, 2), small[end:end + FF].reshape(16, 128)
 
 
 def small_grads(gsum, gb1):
     s = gsum.reshape(TROWS, 8, D).sum(1)
     tb = jnp.concatenate([s[:9], s[9:58] * window_mask()]).T
-    return jnp.concatenate([tb.reshape(-1), gb1.sum(0), s[58:68].T.reshape(-1)])
+    return jnp.concatenate([tb.reshape(-1), gb1.sum(0), s[CPE:CPE + 10].T.reshape(-1)])
 
 
 def to_rows(a):
@@ -664,7 +900,7 @@
 def shards(n, images, grid_sizes, qkv, proj, fc1, fc2, small, cotangent):
     layers = qkv.shape[0]
     width = small.shape[1]
-    packed = [pack(qkv[l], proj[l], fc1[l], fc2[l], small[l], n) for l in range(layers)]
+    packed = [pack(qkv[l], proj[l], fc1[l], fc2[l], n) for l in range(layers)]
     slot = lax.broadcasted_iota(jnp.int32, (SLOT, 1), 0)
     cellno = jnp.maximum(slot - 1, 0)
     far = jnp.maximum(cellno // GRID, cellno % GRID)
@@ -672,19 +908,27 @@
     sz = jnp.broadcast_to(grid_sizes[:, None], (NI, 128))
     x = to_rows(images)
     saved = []
+    if n == 32 and layers == 2:
+        flat = jnp.pad(small.astype(F32).reshape(2, 9, 128), ((0, 0), (0, 7), (0, 0))).reshape(32, 128)
+        out = fwd_first(4, x, sz, packed[0], packed[1], flat)
+        count = 1 + len(RES)
+        w0, w1, tab, b1 = out[count:]
+        held = [(w0, tab[0], b1[0]), (w1, tab[1], b1[1])]
+    else:
+        held = [whole_weights(packed[l], small[l], n) for l in range(layers)]
+        out = None
     for l in range(layers):
-        full = lax.all_gather(packed[l][None], AXES, axis=0, tiled=True)
-        wqkv, wproj, w1, w2, vec = unpack(full, n, width)
-        tab, b1 = tables(vec)
-        out = fwd_layer(x, sz, tab, b1, wqkv, wproj, w1, w2)
-        saved.append((x, tab, b1, wqkv, wproj, w1, w2, out[1:]))
+        w, tab, b1 = held[l]
+        if l or out is None:
+            out = fwd_layer(x, sz, tab, b1, w)
+        saved.append((x, tab, w, out[1:1 + len(RES)]))
         x = out[0]
     output = from_rows(jnp.where(present, x.reshape(SLOT, NI, D), 0.0).astype(BF16))
     dx = jnp.where(present, jnp.transpose(cotangent, (1, 0, 2)), 0).astype(F32).reshape(R, D)
     shares = [None] * layers
     for l in reversed(range(layers)):
-        xin, tab, b1, wqkv, wproj, w1, w2, res = saved[l]
-        dx, gqkv, gproj, gw1, gw2, gsum, gb1 = bwd_layer(dx, xin, sz, tab, b1, wqkv, wproj, w1, w2, res)
+        xin, tab, w, res = saved[l]
+        dx, gqkv, gproj, gw1, gw2, gsum, gb1 = bwd_layer(dx, xin, sz, tab, w, res)
         g = pack_grads(gqkv, gproj, gw1, gw2, small_grads(gsum, gb1), n)
         shares[l] = split_grads(lax.psum_scatter(g, AXES, scatter_dimension=0, tiled=True)[0].astype(F32), n, width)
     grads = [jnp.stack([shares[l][i] for l in range(layers)]) for i in range(5)]

time: 835 us -> 756 us (0.905)
  waiting for transfers between devices: 420 us -> 278 us
  Pallas kernels: 312 us -> 383 us
    all_gather x2 -> x0, waiting for transfers between devices: 142 us -> none  [shards(): full = lax.all_gather(packed[l][None], AXES, axis=0, tiled=True)]
    pallas_call x2, Pallas kernels: 130 us -> 196 us  [the longest x1 131 us: fwd_first(): pl.pallas_call(functools.partial(first_kernel, line), out_shape=outs, in_...]
    slice x19 -> x4, local copies, waits for them, and re-layouts: 20.2 us -> 5.97 us  [shards(): packed = [pack(qkv[l], proj[l], fc1[l], fc2[l], n) for l in range(layers)]]
    unnamed x84 -> x46, local copies, waits for them, and re-layouts: 19.3 us -> 22.6 us
  transfers between devices with their start and end apart: 4 -> 2, of which waited for: 4 -> 2; matrix products, arithmetic and copies ran while one was open for 2% -> 2% of each run, Pallas kernels for 0% -> 0%
where the time goes in v2:
time: 756 us; the launch traced here: 750 us
  Pallas kernels  383 us (51%)
  waiting for transfers between devices  278 us (37%)
  local copies, waits for them, and re-layouts  50.2 us (7%)
  other arithmetic  24.2 us (3%)
  between operations  14.9 us (2%)
    reduce_scatter x2, waiting for transfers between devices, shards(): lax.psum_scatter(g, AXES, scatter_dimension=0, tiled=True)[0].astype(F32)  278 us
    pallas_call x1, Pallas kernels, fwd_first(): pl.pallas_call(functools.partial(first_kernel, line), out_shape=outs, in_...  131 us
    pallas_call x2, Pallas kernels, bwd_layer(): pl.pallas_call(bwd_f_kernel, out_shape=[sd((R, D), F32), sd((D, 3 * D), B...  113 us
    pallas_call x2, Pallas kernels, bwd_layer(): pl.pallas_call(bwd_e_kernel, out_shape=[sd((R, D), F32), sd((4, RP, 128),...  73.4 us
    pallas_call x1, Pallas kernels, fwd_layer(): pl.pallas_call(fwd_kernel, out_shape=outs, in_specs=vspec(5), out_specs=v...  65.3 us
    unnamed x46, local copies, waits for them, and re-layouts  22.6 us
  transfers between devices with their start and end apart: 2, of which 2 were waited for; matrix products, arithmetic and copies ran while one was open for 2% of the time, Pallas kernels for 0%

profile of v2, /device:TPU:0, one launch (start us, length us, event | category | flops | bytes accessed | tf_op | source)
XLA Modules:
  0.0 749.6 jit_solution(5093004617052638367)
XLA Ops:
  11.5 1.7 slice_reduce_fusion
  13.3 1.7 slice_reduce_fusion.1
  15.1 1.0 slice_reduce_fusion.6
  16.1 1.5 slice_reduce_fusion.4
  20.0 1.3 broadcast_in_dim.40.sz
  21.3 130.6 %first_fwd.1 = (f32[1312,512]{1,0:T(8,128)}, bf16[1312,512]{1,0:T(8,128)(2,1)}, f32[1312,128]{1,0:T(8,128)}, bf16[1312,512]{1,0:T(8,128)(2,1)}, f32[4,1536,128]{...) custom-call(bf16[1312,512]{1,0:T(8,128)(2,1)} %bitcast.93, ...), custom_call_target="tpu_custom_call" | custom-call | tf_op jit(solution)/shard_map/first_fwd/pallas_call | solution.py:572
  151.9 1.7 slice_bitcast_fusion
  153.7 1.3 slice_bitcast_fusion.8.b1
  155.0 65.3 %block_fwd.1 = (f32[1312,512]{1,0:T(8,128)}, bf16[1312,512]{1,0:T(8,128)(2,1)}, f32[1312,128]{1,0:T(8,128)}, bf16[1312,512]{1,0:T(8,128)(2,1)}, f32[4,1536,128]{...) custom-call(f32[1312,512]{1,0:T(8,128)} %get-tuple-element.61.x, ...), custom_call_target="tpu_custom_call" | custom-call | tf_op jit(solution)/shard_map/block_fwd/pallas_call | solution.py:582
  220.3 3.7 bitcast_select_fusion
  224.0 2.0 bitcast_convert_fusion.dx3
  226.0 36.7 %block_bwd_e.2 = (f32[1312,512]{1,0:T(8,128)}, f32[4,1536,128]{2,1,0:T(8,128)}, bf16[512,2048]{1,0:T(8,128)(2,1)}, bf16[2048,512]{1,0:T(8,128)(2,1)}, bf16[512,5...) custom-call(f32[1312,512]{1,0:T(8,128)} %bitcast_convert_fusion.dx3, f32[4,80,128]{2,1,0:T(8,128)} %get-tuple-element.138.tab, ...), custom_call_target="tpu_custom_call" | custom-call | tf_op jit(solution)/shard_map/block_bwd_e/pallas_call | solution.py:814
  262.7 56.8 %block_bwd_f.2 = (f32[1312,512]{1,0:T(8,128)}, bf16[512,1536]{1,0:T(8,128)(2,1)}, f32[640,512]{1,0:T(8,128)}) custom-call(f32[1312,512]{1,0:T(8,128)} %get-tuple-element.61.x, s32[16,128]{1,0:T(8,128)} %broadcast_in_dim.40.sz, f32[4,80,128]{2,1,0:T(8,128)} %get-tuple-element.138.tab, bf16[2,4,2,2,192,512]{5,4,3,2,1,0:T(8,128)(2,1)} %get-tuple-element.64.w, ...), custom_call_target="tpu_custom_call" | custom-call | tf_op jit(solution)/shard_map/block_bwd_f/pallas_call | solution.py:821
  319.4 1.8 bitcast_reduce_fusion
  321.9 2.4 fusion.12
  325.2 1.3 fusion.10
  327.5 36.6 %block_bwd_e.3 = (f32[1312,512]{1,0:T(8,128)}, f32[4,1536,128]{2,1,0:T(8,128)}, bf16[512,2048]{1,0:T(8,128)(2,1)}, bf16[2048,512]{1,0:T(8,128)(2,1)}, bf16[512,5...) custom-call(f32[1312,512]{1,0:T(8,128)} %get-tuple-element.92.dx3, f32[4,80,128]{2,1,0:T(8,128)} %get-tuple-element.137.tab, ...), custom_call_target="tpu_custom_call" | custom-call | tf_op jit(solution)/shard_map/block_bwd_e/pallas_call | solution.py:814
  364.1 56.5 %block_bwd_f.3 = (f32[1312,512]{1,0:T(8,128)}, bf16[512,1536]{1,0:T(8,128)(2,1)}, f32[640,512]{1,0:T(8,128)}) custom-call(bf16[1312,512]{1,0:T(8,128)(2,1)} %bitcast.94, s32[16,128]{1,0:T(8,128)} %broadcast_in_dim.40.sz, f32[4,80,128]{2,1,0:T(8,128)} %get-tuple-element.137.tab, bf16[2,4,2,2,192,512]{5,4,3,2,1,0:T(8,128)(2,1)} %get-tuple-element.66.w, ...), custom_call_target="tpu_custom_call" | custom-call | tf_op jit(solution)/shard_map/block_bwd_f/pallas_call | solution.py:821
  420.6 1.8 bitcast_reduce_fusion.1
  422.5 1.6 fusion.2
  427.0 1.9 constant_dynamic-update-slice_fusion.18
  428.9 1.9 constant_dynamic-update-slice_fusion.17
  430.8 1.9 constant_dynamic-update-slice_fusion.16
  432.7 1.9 constant_dynamic-update-slice_fusion.15
  434.6 1.9 constant_dynamic-update-slice_fusion.14
  438.3 1.5 constant_dynamic-update-slice_fusion.11
  441.7 1.5 fusion.11
  450.2 1.6 constant_dynamic-update-slice_fusion.1
  452.6 133.5 %reduce-scatter.5.cloned.1.call-done = bf16[1,195,512]{2,1,0:T(8,128)(2,1)} async-done(((bf16[32,195,512]{2,1,0:T(8,128)(2,1)}), bf16[1,195,512]{2,1,0:T(8,128)(2,1)}) %reduce-scatter.5.cloned.1.call-update) | async-done | bytes 199696 | tf_op jit(solution)/shard_map/reduce_scatter | solution.py:933
  586.0 1.0 convert_element_type.34
  587.0 144.1 %reduce-scatter.3.cloned.1.call-done = bf16[1,195,512]{2,1,0:T(8,128)(2,1)} async-done(((bf16[32,195,512]{2,1,0:T(8,128)(2,1)}), bf16[1,195,512]{2,1,0:T(8,128)(2,1)}) %reduce-scatter.3.cloned.1.call-update) | async-done | bytes 199696 | tf_op jit(solution)/shard_map/reduce_scatter | solution.py:933
  731.2 1.0 convert_element_type.32
  (118 shorter events, 33.5 us)
Async XLA Ops:
  7.2 578.9 %reduce-scatter.5.cloned.1.call-start = ((), (), s32[]{:S(2)}) async-start(), calls=%async_computation.3 | async-start | bytes 6758400 | tf_op jit(solution)/shard_map/reduce_scatter | solution.py:933
  319.4 5.7 copy-start.3
  321.2 0.6 copy-start.7
  420.6 15.9 %copy-start.5 = (bf16[512,512]{1,0:T(8,128)(2,1)S(1)}, bf16[512,512]{1,0:T(8,128)(2,1)}, u32[]{:S(2)}) copy-start(bf16[512,512]{1,0:T(8,128)(2,1)} %get-tuple-element.128) | copy-start | bytes 1572868
  420.6 16.8 %copy-start.4 = (bf16[512,512]{1,0:T(8,128)(2,1)S(1)}, bf16[512,512]{1,0:T(8,128)(2,1)}, u32[]{:S(2)}) copy-start(bf16[512,512]{1,0:T(8,128)(2,1)} %get-tuple-element.127) | copy-start | bytes 1572868
  420.6 17.6 %copy-start.2 = (bf16[2048,512]{1,0:T(8,128)(2,1)S(1)}, bf16[2048,512]{1,0:T(8,128)(2,1)}, u32[]{:S(2)}) copy-start(bf16[2048,512]{1,0:T(8,128)(2,1)} %get-tuple-element.112) | copy-start | bytes 6291460
  438.3 2.7 copy-start.9
  438.3 2.8 copy-start.8
  440.6 5.2 copy-start.6
  440.6 6.0 copy-start.1
  440.6 290.6 %reduce-scatter.3.cloned.1.call-start = ((), (), s32[]{:S(2)}) async-start(), calls=%async_computation.2 | async-start | bytes 6758400 | tf_op jit(solution)/shard_map/reduce_scatter | solution.py:933
  444.8 5.4 copy-start
Sparse Core Ops, SparseCore 0:
  440.7 145.3 reduce-scatter.4
  588.3 142.7 reduce-scatter.2

commit v3 on v2

--- a/solution.py
+++ b/solution.py
@@ -253,7 +253,7 @@
         pi = img_load(p, i, half).astype(BF16)
         vi = img_load(v, i, half).astype(BF16)
         summ = jnp.where(head_mask(), dot(pi, vi, 0, 0), 0.0).astype(BF16)
-        s[t] = summ
+        s[t] = (summ[0:64] + summ[64:128]) + (summ[128:192] + summ[192:256])
         qi = img_load(q, i, half).astype(BF16)
         img_store(f, i, half, dot(qi, summ, 1, 0) * 0.125)
         return c
@@ -316,32 +316,37 @@
     lax.fori_loop(0, 2, body, 0)
 
 
-def fwd_phases(x, sz, tab, b1, w, x3, n1, inv1, h1, q, p, v, s, rel, a_low, n2, inv2, h2, g, slope, x1, f, tick=lambda: None):
-    fwd_conv1(x, sz, tab, x1)
-    norm_phase(x1, tab, 0, 1, n1, h1, inv1)
-    tick(0)
+def fwd_phases(x, sz, tab, b1, w, x3, n1, inv1, h1, q, p, v, s, rel, a_low, n2, inv2, h2, g, slope, x1, f, tick, need):
     fwd_qkv(h1, w, tab, q, p, v)
-    tick(1)
+    tick()
     fwd_softmax(p, sz)
-    tick(2)
+    tick()
     fwd_attn(q, p, v, s, f)
-    tick(3)
+    tick()
     fwd_conv3(v, q, f, sz, tab, rel, f)
-    tick(4)
+    tick()
     fwd_proj(f, w, tab, x1, a_low)
-    tick(5)
     norm_phase(x1, tab, 2, 3, n2, h2, inv2)
-    tick(6)
+    tick.upto(need)
     fwd_fc1(h2, w, b1, g, slope)
-    tick(7)
+    tick()
     fwd_fc2(g, w, tab, x1, x3)
-    tick(8)
+
+
+class Idle:
+    def __call__(self):
+        pass
+
+    def upto(self, count):
+        pass
+
+    finish = __call__
 
 
 RES = (
     ("n1", (R, D), BF16), ("inv1", (R, 128), F32), ("h1", (R, D), BF16),
     ("q", (4, RP, 128), F32), ("p", (4, RP, 128), F32), ("v", (4, RP, 128), F32),
-    ("s", (2 * NI, 256, 256), BF16), ("rel", (4, R, 128), F32), ("a", (R, D), BF16),
+    ("s", (2 * NI, 64, 256), BF16), ("rel", (4, R, 128), F32), ("a", (R, D), BF16),
     ("n2", (R, D), BF16), ("inv2", (R, 128), F32), ("h2", (R, D), BF16),
     ("g", (R, FF), BF16), ("slope", (R, FF), BF16))
 
@@ -369,123 +374,183 @@
         c = self.c if c is None else c
         return (z * 2 + x, y * 2 + c)
 
-    def neighbours(self):
-        n = self.line
-        return (self.dev(x=1 - self.x), self.dev(y=1 - self.y), self.dev(c=1 - self.c),
-                self.dev(z=lax.rem(self.z + 1, n)), self.dev(z=lax.rem(self.z + n - 1, n)))
+    def off(self, k):
+        return lax.rem(self.z + self.line + k, self.line)
 
 
 def greet(place):
     barrier = pltpu.get_barrier_semaphore()
-    for who in place.neighbours():
+    far = [place.dev(z=place.off(k)) for k in range(1, place.line)]
+    near = [place.dev(x=1 - place.x), place.dev(y=1 - place.y), place.dev(c=1 - place.c)]
+    for who in far + near:
         pl.semaphore_signal(barrier, inc=1, device_id=who, device_id_type=MESH)
-    pl.semaphore_wait(barrier, 5)
+    pl.semaphore_wait(barrier, place.line + 2)
 
 
 def remote(src, dst, send, recv, dev):
     return pltpu.make_async_remote_copy(src_ref=src, dst_ref=dst, send_sem=send, recv_sem=recv, device_id=dev, device_id_type=MESH)
 
 
+def both(copy):
+    copy.wait_send()
+    copy.wait_recv()
+
+
+def by_core(place, a, b):
+    def run():
+        @pl.when(place.c == 0)
+        def _():
+            a()
+
+        @pl.when(place.c == 1)
+        def _():
+            b()
+    return run
+
+
 def gather_ticks(place, g, rows, send, recv):
+    n, z, x, y = place.line, place.z, place.x, place.y
+
+    def lines():
+        mine = g.at[place.c, z, x, y, rows]
+        return [remote(mine, mine, send.at[k - 1], recv.at[k - 1], place.dev(z=place.off(k))) for k in range(1, n)]
+
+    def line_waits():
+        for k, cp in enumerate(lines()):
+            cp.wait_send()
+            got = g.at[place.c, place.off(-k - 1), x, y, rows]
+            remote(got, got, send.at[k], recv.at[k], place.dev(z=place.off(1))).wait_recv()
+
+    def parts(core):
+        if core == 0:
+            return (g.at[0, :, x, y, rows], g.at[0, :, x, :, rows]), (g.at[0, :, x, y, rows], g.at[0, :, x, 1 - y, rows], g.at[0, :, 1 - x, :, rows])
+        return (g.at[1, :, x, y, rows], g.at[1, :, :, y, rows]), (g.at[1, :, x, y, rows], g.at[1, :, 1 - x, y, rows], g.at[1, :, :, 1 - y, rows])
+
+    def swap(core, i):
+        part = parts(core)[0][i]
+        over_y = (core == 0) == (i == 0)
+        return remote(part, part, send.at[n - 1 + i], recv.at[n - 1 + i], place.dev(y=1 - y) if over_y else place.dev(x=1 - x))
+
+    def hand(core, i):
+        part = parts(core)[1][i]
+        return remote(part, part, send.at[n + 1 + i], recv.at[n + 1 + i], place.dev(c=1 - place.c))
+
+    def steps(core):
+        def last():
+            for i in range(3):
+                hand(core, i).wait_send()
+                hand(1 - core, i).wait_recv()
+        return [lambda: None,
+                lambda: (swap(core, 0).start(), hand(core, 0).start()),
+                lambda: (both(swap(core, 0)), swap(core, 1).start(), hand(core, 1).start()),
+                lambda: (both(swap(core, 1)), hand(core, 2).start()),
+                last]
+    ticks = [by_core(place, a, b) for a, b in zip(steps(0), steps(1))]
+
+    def first():
+        for cp in lines():
+            cp.start()
+
+    def second():
+        line_waits()
+        ticks[1]()
+    return [first, second] + ticks[2:]
+
+
+def add_blocks(pairs):
+    for dst, src in pairs:
+        dst[...] = (dst[...].astype(F32) + src[...].astype(F32)).astype(dst.dtype)
+
+
+def scatter_ticks(place, g, rows, cbuf, pbuf, sbuf, zbuf, out, send, recv):
     n, z, x, y, c = place.line, place.z, place.x, place.y, place.c
-    xs, ys, cs = 0, 1, 2
-
-    def swap(core, sem, mine, dev):
-        return remote(mine, mine, send.at[sem], recv.at[sem], dev)
-
-    def pair_x(whole):
-        part = g.at[1, :, x, :, rows] if whole else g.at[0, z, x, y, rows]
-        return swap(0, xs, part, place.dev(x=1 - x))
-
-    def pair_y(whole):
-        part = g.at[1, :, x, y, rows] if whole else g.at[0, z, :, y, rows]
-        return swap(0, ys, part, place.dev(y=1 - y))
-
-    def line(core, k):
-        def part(at):
-            at = jnp.clip(at, 0, n - 1)
-            return g.at[0, at, :, :, rows] if core == 0 else g.at[1, at, x, y, rows]
-        right = remote(part(z - k + 1), part(z - k + 1), send.at[2 + k], recv.at[2 + k], place.dev(z=jnp.minimum(z + 1, n - 1)))
-        left = remote(part(z + k - 1), part(z + k - 1), send.at[1 + n + k], recv.at[1 + n + k], place.dev(z=jnp.maximum(z - 1, 0)))
-        return (right, (z + 1 < n) & (z - k + 1 >= 0), z - k >= 0), (left, (z > 0) & (z + k - 1 < n), z + k < n)
-
-    def start_line(core, k):
-        for copy, sends, _ in line(core, k):
-            pl.when(sends)(copy.start)
-
-    def wait_line(core, k):
-        for copy, sends, gets in line(core, k):
-            pl.when(sends)(copy.wait_send)
-            pl.when(gets)(copy.wait_recv)
-
-    def both(copy):
-        copy.wait_send()
-        copy.wait_recv()
-
-    def core_copy(which):
-        return remote(g.at[which, :, :, :, rows], g.at[which, :, :, :, rows], send.at[cs], recv.at[cs], place.dev(c=1 - c))
-
-    first, second = [], []
-    first.append(lambda: pair_x(False).start())
-    first.append(lambda: (both(pair_x(False)), pair_y(False).start()))
-    first.append(lambda: (both(pair_y(False)), start_line(0, 1)))
-    for k in range(1, n - 1):
-        first.append(lambda k=k: (wait_line(0, k), start_line(0, k + 1)))
-    first.append(lambda: (wait_line(0, n - 1), core_copy(0).start()))
-    first.append(lambda: both(core_copy(0)))
-    second.append(lambda: start_line(1, 1))
-    for k in range(1, n - 1):
-        second.append(lambda k=k: (wait_line(1, k), start_line(1, k + 1)))
-    second.append(lambda: (wait_line(1, n - 1), pair_y(True).start()))
-    second.append(lambda: (both(pair_y(True)), pair_x(True).start()))
-    second.append(lambda: (both(pair_x(True)), core_copy(1).start()))
-    second.append(lambda: both(core_copy(1)))
-    assert len(first) == len(second)
-
-    def tick(a, b):
+
+    def cores():
+        return remote(g.at[1 - c, :, :, :, rows], cbuf, send.at[0], recv.at[0], place.dev(c=1 - c))
+
+    def swaps(core):
+        over_x, over_y = place.dev(x=1 - x), place.dev(y=1 - y)
+        if core == 0:
+            return (remote(g.at[0, :, 1 - x, :, rows], pbuf, send.at[1], recv.at[1], over_x),
+                    remote(g.at[0, :, x, 1 - y, rows], sbuf, send.at[2], recv.at[2], over_y))
+        return (remote(g.at[1, :, :, 1 - y, rows], pbuf, send.at[1], recv.at[1], over_y),
+                remote(g.at[1, :, 1 - x, y, rows], sbuf, send.at[2], recv.at[2], over_x))
+
+    def lines():
+        return [remote(g.at[c, place.off(k), x, y, rows], zbuf.at[k - 1], send.at[2 + k], recv.at[2 + k], place.dev(z=place.off(k))) for k in range(1, n)]
+
+    def start_cores():
+        cores().start()
+
+    def add_cores():
+        both(cores())
+
+        def body(t, carry):
+            add_blocks([(g.at[c, t // 4, t // 2 % 2, t % 2, rows], cbuf.at[t // 4, t // 2 % 2, t % 2])])
+            return carry
+        lax.fori_loop(0, 4 * n, body, 0)
+
+    def step1(core):
         def run():
-            @pl.when(c == 0)
-            def _():
-                a()
-
-            @pl.when(c == 1)
-            def _():
-                b()
+            add_cores()
+            swaps(core)[0].start()
         return run
-    return [tick(a, b) for a, b in zip(first, second)]
-
-
-def wave(lists):
-    for r in range(max(i + len(t) for i, t in enumerate(lists))):
-        for i, t in enumerate(lists):
-            if 0 <= r - i < len(t):
-                t[r - i]()
-
-
-def gather_kernel(line, chunks, shard, g, own, send, recv):
-    place = Place(line)
-    mine = pltpu.make_async_copy(shard, g.at[place.c, place.z, place.x, place.y], own)
-    mine.start()
-    greet(place)
-    mine.wait()
-    wave([gather_ticks(place, g, pl.ds(a, b - a), send.at[i], recv.at[i]) for i, (a, b) in enumerate(chunks)])
-
-
-def gather(shard, line, chunks, cid):
-    rows = shard.shape[0]
-    sems = pltpu.SemaphoreType.DMA((len(chunks), 3 + 2 * (line - 1) + 1))
-    return pl.pallas_call(
-        functools.partial(gather_kernel, line, chunks),
-        out_shape=jax.ShapeDtypeStruct((2, line, 2, 2, rows, D), BF16),
-        in_specs=[pl.BlockSpec(memory_space=pltpu.VMEM)], out_specs=pl.BlockSpec(memory_space=pltpu.VMEM),
-        scratch_shapes=[pltpu.SemaphoreType.DMA, sems, sems],
-        compiler_params=pltpu.CompilerParams(collective_id=cid, has_side_effects=True, vmem_limit_bytes=67043328),
-        name="gather_weights")(shard)
-
-
-def add_into(dst, src, out=None):
-    out = dst if out is None else out
-    out[...] = (dst[...].astype(F32) + src[...].astype(F32)).astype(out.dtype)
+
+    def step2(core):
+        def run():
+            both(swaps(core)[0])
+
+            def body(t, carry):
+                dst = g.at[0, t // 2, x, t % 2, rows] if core == 0 else g.at[1, t // 2, t % 2, y, rows]
+                add_blocks([(dst, pbuf.at[t // 2, t % 2])])
+                return carry
+            lax.fori_loop(0, 2 * n, body, 0)
+            swaps(core)[1].start()
+        return run
+
+    def step3(core):
+        def run():
+            both(swaps(core)[1])
+
+            def body(t, carry):
+                add_blocks([(g.at[core, t, x, y, rows], sbuf.at[t])])
+                return carry
+            lax.fori_loop(0, n, body, 0)
+            for cp in lines():
+                cp.start()
+        return run
+
+    def finish():
+        for cp in lines():
+            both(cp)
+        total = g[c, z, x, y, rows].astype(F32)
+        for k in range(n - 1):
+            total = total + zbuf[k].astype(F32)
+        out[...] = total
+    return [start_cores] + [by_core(place, s(0), s(1)) for s in (step1, step2, step3)] + [finish]
+
+
+def scatter_bufs(line, rows, width, dtype):
+    return [pltpu.VMEM(shape + (rows, width), dtype) for shape in ((line, 2, 2), (line, 2), (line,), (line - 1,))]
+
+
+class Ticker:
+    def __init__(self, lists):
+        depth = max(i + len(t) for i, t in lists)
+        self.rounds = [[t[r - i] for i, t in lists if 0 <= r - i < len(t)] for r in range(depth)]
+        self.done = 0
+
+    def upto(self, count):
+        while self.done < min(count, len(self.rounds)):
+            for t in self.rounds[self.done]:
+                t()
+            self.done += 1
+
+    def __call__(self):
+        self.upto(self.done + 1)
+
+    def finish(self):
+        self.upto(len(self.rounds))
 
 
 def build_tables(gs, layer, tau, y, tab, b1):
@@ -520,7 +585,19 @@
     b1[layer] = tau[232:248, :]
 
 
-CHUNKS = ((0, 64), (64, 128), (128, 192))
+FIRST = ((0, 64), (64, 128), (128, 192))
+SECOND = ((64, 128), (128, 192))
+
+
+def sem_rows(line, count):
+    return pltpu.SemaphoreType.DMA((count, line + 4))
+
+
+def put_own(pairs, sems):
+    copies = [pltpu.make_async_copy(src, dst, sems.at[i]) for i, (src, dst) in enumerate(pairs)]
+    for cp in copies:
+        cp.start()
+    return copies
 
 
 def first_kernel(line, x, sz, shard0, shard1, small,
@@ -528,61 +605,103 @@
                  x1, f, gs, tau, y, own, send, recv):
     place = Place(line)
     here = (place.c, place.z, place.x, place.y)
-    puts = [pltpu.make_async_copy(src, dst.at[here], own.at[i]) for i, (src, dst) in enumerate(((shard0, w0), (shard1, w1), (small, gs)))]
-    for cp in puts:
-        cp.start()
+    puts = put_own(((shard0, w0.at[here]), (shard1.at[0:64], w1.at[here]), (small, gs.at[here])), own)
     greet(place)
     for cp in puts:
         cp.wait()
-    lists = [gather_ticks(place, gs, slice(None), send.at[0], recv.at[0])]
-    lists += [gather_ticks(place, w0, pl.ds(a, b - a), send.at[1 + i], recv.at[1 + i]) for i, (a, b) in enumerate(CHUNKS)]
-    lists += [gather_ticks(place, w1, pl.ds(a, b - a), send.at[4 + i], recv.at[4 + i]) for i, (a, b) in enumerate(CHUNKS)]
-    depth = len(lists[0])
-    rounds = []
-    for r in range(depth + len(lists) - 1):
-        rounds.append([t[r - i] for i, t in enumerate(lists) if 0 <= r - i < depth])
-    todo = iter(rounds)
-    done = [0]
-
-    def advance(upto):
-        while done[0] < upto:
-            for t in next(todo):
-                t()
-            done[0] += 1
-    advance(depth)
-    for layer in range(2):
-        build_tables(gs, layer, tau, y, tab, b1)
-    need = {0: depth + 1, 6: depth + 3}
-
-    def tick(i):
-        advance(min(max(done[0] + 1, need.get(i, 0)), len(rounds)))
-    fwd_phases(x, sz, tab.at[0], b1.at[0], w0, x3, n1, inv1, h1, q, p, v, s, rel, a_low, n2, inv2, h2, g, slope, x1, f, tick)
-    advance(len(rounds))
-
-
-def fwd_kernel(x, sz, tab, b1, w, *refs):
-    fwd_phases(x, sz, tab, b1, w, *refs, tick=lambda i: None)
+    tiny = Ticker([(0, gather_ticks(place, gs, slice(None), send.at[0], recv.at[0]))])
+    lists = [(i, gather_ticks(place, w0, pl.ds(a, b - a), send.at[1 + i], recv.at[1 + i])) for i, (a, b) in enumerate(FIRST)]
+    lists.append((3, gather_ticks(place, w1, slice(None), send.at[4], recv.at[4])))
+    tick = Ticker(lists)
+    tiny()
+    tick()
+    tiny()
+    tiny()
+    tick()
+    tiny()
+    tiny()
+    build_tables(gs, 0, tau, y, tab, b1)
+    tick()
+    fwd_conv1(x, sz, tab.at[0], x1)
+    tick()
+    norm_phase(x1, tab.at[0], 0, 1, n1, h1, inv1)
+    build_tables(gs, 1, tau, y, tab, b1)
+    tick.upto(5)
+    fwd_phases(x, sz, tab.at[0], b1.at[0], w0, x3, n1, inv1, h1, q, p, v, s, rel, a_low, n2, inv2, h2, g, slope, x1, f, tick, 7)
+    tick.finish()
+
+
+def second_kernel(line, x, sz, tab, b1, w_in, shard,
+                  x3, n1, inv1, h1, q, p, v, s, rel, a_low, n2, inv2, h2, g, slope, w, x1, f, own, load, send, recv):
+    place = Place(line)
+    here = (place.c, place.z, place.x, place.y)
+    got = pltpu.make_async_copy(w_in, w.at[:, :, :, :, 0:64], load)
+    got.start()
+    puts = put_own(((shard.at[64:WROWS], w.at[here + (pl.ds(64, 128),)]),), own)
+    greet(place)
+    for cp in puts:
+        cp.wait()
+    tick = Ticker([(i, gather_ticks(place, w, pl.ds(a, b - a), send.at[i], recv.at[i])) for i, (a, b) in enumerate(SECOND)])
+    tick()
+    fwd_conv1(x, sz, tab, x1)
+    tick()
+    norm_phase(x1, tab, 0, 1, n1, h1, inv1)
+    got.wait()
+    fwd_phases(x, sz, tab, b1, w, x3, n1, inv1, h1, q, p, v, s, rel, a_low, n2, inv2, h2, g, slope, x1, f, tick, 6)
+
+
+def fwd_kernel(x, sz, tab, b1, w, x3, n1, inv1, h1, q, p, v, s, rel, a_low, n2, inv2, h2, g, slope, x1, f):
+    fwd_conv1(x, sz, tab, x1)
+    norm_phase(x1, tab, 0, 1, n1, h1, inv1)
+    fwd_phases(x, sz, tab, b1, w, x3, n1, inv1, h1, q, p, v, s, rel, a_low, n2, inv2, h2, g, slope, x1, f, Idle(), 0)
+
+
+def sd(shape, dtype):
+    return jax.ShapeDtypeStruct(shape, dtype)
+
+
+def comm_params(cid):
+    return pltpu.CompilerParams(vmem_limit_bytes=67043328, collective_id=cid, has_side_effects=True)
+
+
+def packed(line, rows, width=D, dtype=BF16):
+    return sd((2, line, 2, 2, rows, width), dtype)
+
+
+ANY = pl.BlockSpec(memory_space=pl.ANY)
+
+
+def fwd_outs():
+    return [sd((R, D), F32)] + [sd(sh, dt) for _, sh, dt in RES]
+
+
+FWD_SCRATCH = [pltpu.VMEM((R, D), F32), pltpu.VMEM((4, RP, 128), F32)]
 
 
 def fwd_first(line, x, sz, shard0, shard1, small):
-    sd = jax.ShapeDtypeStruct
-    pack = (2, line, 2, 2)
-    outs = [sd((R, D), F32)] + [sd(sh, dt) for _, sh, dt in RES] + [sd(pack + (WROWS, D), BF16)] * 2 + [sd((2, 4, TROWS, 128), F32), sd((2, 16, 128), F32)]
-    sems = pltpu.SemaphoreType.DMA((7, 3 + 2 * (line - 1) + 1))
+    outs = fwd_outs() + [packed(line, WROWS), packed(line, 64), sd((2, 4, TROWS, 128), F32), sd((2, 16, 128), F32)]
     return pl.pallas_call(
         functools.partial(first_kernel, line), out_shape=outs, in_specs=vspec(5), out_specs=vspec(len(outs)),
-        scratch_shapes=[pltpu.VMEM((R, D), F32), pltpu.VMEM((4, RP, 128), F32), pltpu.VMEM(pack + (32, 128), F32), pltpu.VMEM((288, 128), F32),
-                        pltpu.VMEM((D, 128), F32), pltpu.SemaphoreType.DMA((3,)), sems, sems],
-        compiler_params=pltpu.CompilerParams(vmem_limit_bytes=67043328, collective_id=0, has_side_effects=True), name="first_fwd",
+        scratch_shapes=FWD_SCRATCH + [pltpu.VMEM((2, line, 2, 2, 32, 128), F32), pltpu.VMEM((288, 128), F32), pltpu.VMEM((D, 128), F32),
+                                      pltpu.SemaphoreType.DMA((3,)), sem_rows(line, 5), sem_rows(line, 5)],
+        compiler_params=comm_params(0), name="first_fwd",
     )(x, sz, shard0, shard1, small)
 
 
+def fwd_second(line, x, sz, tab, b1, w_in, shard):
+    outs = fwd_outs() + [packed(line, WROWS)]
+    return pl.pallas_call(
+        functools.partial(second_kernel, line), out_shape=outs, in_specs=vspec(4) + [ANY] + vspec(1), out_specs=vspec(len(outs)),
+        scratch_shapes=FWD_SCRATCH + [pltpu.SemaphoreType.DMA((1,)), pltpu.SemaphoreType.DMA, sem_rows(line, 2), sem_rows(line, 2)],
+        compiler_params=comm_params(1), name="second_fwd",
+    )(x, sz, tab, b1, w_in, shard)
+
+
 def fwd_layer(x, sz, tab, b1, w):
-    outs = [jax.ShapeDtypeStruct((R, D), F32)] + [jax.ShapeDtypeStruct(sh, dt) for _, sh, dt in RES]
+    outs = fwd_outs()
     return pl.pallas_call(
         fwd_kernel, out_shape=outs, in_specs=vspec(5), out_specs=vspec(len(outs)),
-        scratch_shapes=[pltpu.VMEM((R, D), F32), pltpu.VMEM((4, RP, 128), F32)],
-        compiler_params=PARAMS, name="block_fwd",
+        scratch_shapes=FWD_SCRATCH, compiler_params=PARAMS, name="block_fwd",
     )(x, sz, tab, b1, w)
 
 
@@ -590,7 +709,8 @@
     total = val[0:8]
     for i in range(1, val.shape[0] // 8):
         total = total + val[8 * i:8 * i + 8]
-    ref[8 * row:8 * row + 8, :] += total
+    for g in range(4):
+        ref[g, 8 * row:8 * row + 8, :] += total[:, 128 * g:128 * g + 128]
 
 
 def bwd_du(dx, w2, slope, dm, gb1):
@@ -616,17 +736,17 @@
     lax.fori_loop(0, 16, body, 0)
 
 
-def norm_back_phase(up, hat, inv_ref, tab, gain, res, out_low, sums, rg, rs, rb):
+def norm_back_phase(up, hat, inv_ref, tab, gain, res, out, out_low, sums, rg, rs, split=False):
     def body(i, c):
         at = pl.ds(pl.multiple_of(i * 32, 16), 32)
-        u = up[at, :]
+        u = jnp.concatenate([up[g, at, :] for g in range(4)], axis=1) if split else up[at, :]
         n = hat[at, :].astype(F32)
         e = u * row(tab, gain)
         m1 = jnp.mean(e, axis=-1, keepdims=True)
         m2 = jnp.mean(e * n, axis=-1, keepdims=True)
         inv = inv_ref[at, 0:1]
         d = res[at, :] + inv * (e - m1 - n * m2)
-        res[at, :] = d
+        out[at, :] = d
         add_rows(sums, rg, u * n)
         add_rows(sums, rs, u)
         if out_low is not None:
@@ -649,24 +769,29 @@
     lax.fori_loop(0, 2, body, 0)
 
 
-def wgrad(left, right, out):
-    wide_left = left.shape[1] > 512
-    blocks = max(left.shape[1], right.shape[1]) // 512
-    for j in range(blocks):
-        cols = slice(512 * j, 512 * j + 512)
-        if wide_left:
-            out[cols, :] = dot(left[:, cols], right[...], 0, 0).astype(BF16)
-        else:
-            out[:, cols] = dot(left[...], right[:, cols], 0, 0).astype(BF16)
+def wgrad(left, right, gr, first):
+    for j in range(right.shape[1] // 512):
+        tile = dot(left[...], right[:, 512 * j:512 * j + 512], 0, 0).astype(BF16)
+        for t in range(32):
+            gr[t % 2, t // 8, t // 4 % 2, t // 2 % 2, first + 16 * j:first + 16 * j + 16, :] = tile[16 * t:16 * t + 16]
+
+
+def wgrad2(left, right, gr, first):
+    for j in range(4):
+        tile = dot(left[:, 512 * j:512 * j + 512], right[...], 0, 0).astype(BF16)
+        for i in range(8):
+            gr[i % 2, j, i // 4, i // 2 % 2, first:first + 64, :] = tile[64 * i:64 * i + 64]
 
 
 def bwd_attn1(q, p, v, s, da, dq, dv, dk):
     def body(t, c):
         i, half = t // 2, t % 2
         df = (img_load(da, i, half) * 0.125).astype(BF16)
+        wide = s[t]
+        wide = jnp.where(head_mask(), jnp.concatenate([wide] * 4, axis=0), jnp.zeros((), BF16))
         qi = img_load(q, i, half).astype(BF16)
         dsum = jnp.where(head_mask(), dot(qi, df, 0, 0), 0.0).astype(BF16)
-        img_store(dq, i, half, dot(df, s[t], 1, 1))
+        img_store(dq, i, half, dot(df, wide, 1, 1))
         pi = img_load(p, i, half).astype(BF16)
         img_store(dv, i, half, dot(pi, dsum, 1, 0))
         vi = img_load(v, i, half).astype(BF16)
@@ -675,7 +800,7 @@
     lax.fori_loop(0, 2 * NI, body, 0)
 
 
-def bwd_mix(q, p, v, rel, da, dq, dv, dk, dj, sz, tab, gsum, gtap):
+def bwd_mix(q, p, v, rel, da, dq, dv, dk, sz, tab, gsum):
     def body(radius, lg, ig):
         lane = lane_of(lg)
         size = sz[ds(8 * ig, 8), :]
@@ -706,8 +831,8 @@
         def second(at, ok):
             dk[lg, at, :] = p[lg, at, :] * (dk[lg, at, :] - dot_sum)
         each_pos(size, ig, second)
-        gsum[ds(8 * (8 + 8 * 0), 8), lane] += acc["r"]
-        gsum[ds(8 * 4, 8), lane] += acc["q"]
+        gsum[lg, 64:72, :] += acc["r"]
+        gsum[lg, 32:40, :] += acc["q"]
 
         def load_grad(y):
             return [da[lg, cell(y, k, ig), :] for k in range(GRID)]
@@ -717,7 +842,7 @@
 
         def emit_tap(a, b, val):
             at = ds(8 * (TAPS + (a + 3) * 7 + b + 3), 8)
-            gsum[at, lane] += val
+            gsum[lg, at, :] += val
         conv_kgrad(load_grad, load_src, radius, emit_tap)
         vs = [dv[lg, ds(8 * ig, 8), :]]
 
@@ -728,9 +853,11 @@
                 dv[lg, at, :] = val
                 vs[0] = vs[0] + val
         conv_pass(load_grad, lambda a, b: row8(tab, TAPS + (a + 3) * 7 + b + 3, lg), radius, emit, flip=True)
-        gsum[ds(8 * 5, 8), lane] += vs[0]
-    for_groups(body)
-
+        gsum[lg, 40:48, :] += vs[0]
+    return body
+
+
+def bwd_cast(dq, dk, dv, dj):
     def cast(i, c):
         at = pl.ds(pl.multiple_of(i * 32, 16), 32)
         for j, ref in enumerate((dq, dk, dv)):
@@ -756,7 +883,7 @@
 
         def emit_tap(a, b, val):
             at = ds(8 * (CPE + (a + 1) * 3 + b + 1), 8)
-            gsum[at, lane] += val
+            gsum[lg, at, :] += val
         conv_kgrad(load_grad, load_src, 1, emit_tap)
         bias = [jnp.zeros((8, 128), F32)]
 
@@ -768,7 +895,7 @@
                 bias[0] = bias[0] + jnp.where(ok, g, 0.0)
                 dx[at, lane] = g + jnp.where(ok, out[k], 0.0)
         conv_pass(load_grad, lambda a, b: row8(tab, CPE + (a + 1) * 3 + b + 1, lg), 1, emit, flip=True)
-        gsum[ds(8 * CPEB, 8), lane] += bias[0]
+        gsum[lg, 8 * CPEB:8 * CPEB + 8, :] += bias[0]
         return c
     lax.fori_loop(0, 8, body, 0)
 
@@ -781,51 +908,213 @@
     lax.fori_loop(0, 41, body, 0)
 
 
-def bwd_e_kernel(dx3, tab, w, a_low, n2, inv2, h2, g, slope,
-                 dx2, da, gw1, gw2, gproj, gsum, gb1, dm, up):
+def build_small(gsum, gb1, y, tau, gsm):
+    r = lax.broadcasted_iota(jnp.int32, (D, D), 0)
+    c = lax.broadcasted_iota(jnp.int32, (D, D), 1)
+    place = jnp.where(c == 64 * (r % 8) + r // 8, 1.0, 0.0).astype(BF16)
+    table = jnp.concatenate([sum(gsum[g, pl.ds(i, TROWS, stride=8), :] for i in range(8)) for g in range(4)], axis=1)
+    tap = lax.broadcasted_iota(jnp.int32, (TROWS, D), 0) - TAPS
+    head = lax.broadcasted_iota(jnp.int32, (TROWS, D), 1) // 64
+    reach = jnp.where(head < 2, 1, jnp.where(head < 5, 2, 3))
+    ok = (tap < 0) | (tap >= 49) | ((jnp.abs(tap // 7 - 3) <= reach) & (jnp.abs(tap % 7 - 3) <= reach))
+    table = jnp.where(ok, table, 0.0)
+    table = jnp.concatenate([table, jnp.zeros((128 - TROWS, D), F32)])
+    hi = table.astype(BF16)
+    mid = (table - hi.astype(F32)).astype(BF16)
+    y[...] = dot(place, hi, 1, 1) + dot(place, mid, 1, 1)
+    lane = lax.broadcasted_iota(jnp.int32, (8, 128), 1)
+
+    def lay(base, step, width, start):
+        for j in range(step):
+            out = None
+            for b in range(128 * j // width, min(64, -(-128 * (j + 1) // width))):
+                first = width * b - 128 * j
+                val = y[8 * b:8 * b + 8, :]
+                shift = (first - start) % 128
+                if shift:
+                    val = pltpu.roll(val, shift, 1)
+                out = val if out is None else jnp.where(lane >= first, val, out)
+            tau[pl.ds(base + j, 8, stride=step), :] = out
+    lay(0, 29, TABLE, 0)
+    lay(248, 5, 10, CPE)
+    for i in range(16):
+        tau[232 + i:233 + i, :] = jnp.sum(gb1[:, 128 * i:128 * i + 128], axis=0, keepdims=True)
+    for t in range(32):
+        gsm[t % 2, t // 8, t // 4 % 2, t // 2 % 2, 0:9, :] = tau[9 * t:9 * t + 9, :]
+        gsm[t % 2, t // 8, t // 4 % 2, t // 2 % 2, 9:16, :] = jnp.zeros((7, 128), F32)
+
+
+def e_phases(dx3, tab, w, a_low, n2, inv2, h2, g, slope_in, dx2, da, gfc, gsum, gb1, dm, up, slope, load, tick):
+    got = pltpu.make_async_copy(slope_in, slope, load)
+    got.start()
     gsum[...] = jnp.zeros_like(gsum)
-    dx2[...] = dx3[...]
-    bwd_du(dx2, w, slope, dm, gb1)
+    got.wait()
+    bwd_du(dx3, w, slope, dm, gb1)
     col_sum(dm, gsum, 7)
-    wgrad(g, dm, gw2)
-    wgrad(h2, slope, gw1)
+    tick()
+    wgrad2(g, dm, gfc, 80)
+    tick()
+    wgrad(h2, slope, gfc, 16)
+    tick()
     mm_nt(slope, w, 4, 4, up)
-    norm_back_phase(up, n2, inv2, tab, 2, dx2, dm, gsum, 2, 3, None)
+    tick()
+    norm_back_phase(up, n2, inv2, tab, 2, dx3, dx2, dm, gsum, 2, 3)
     col_sum(dm, gsum, 6)
-    wgrad(a_low, dm, gproj)
+    tick()
+    wgrad(a_low, dm, gfc, 0)
     mm_nt(dm, w, 3, 1, da, True)
     da[:, R:RP, :] = jnp.zeros((4, RP - R, 128), F32)
 
 
-def bwd_f_kernel(x, sz, tab, w, n1, inv1, h1, q, p, v, s, rel, dx2, da, gsum_in,
-                 dx, gqkv, gsum, dq, dk, dv, dj, up):
-    gsum[...] = gsum_in[...]
+def e_kernel(dx3, tab, w, a_low, n2, inv2, h2, g, slope_in, dx2, da, gfc, gsum, gb1, dm, up, slope, load):
+    e_phases(dx3, tab, w, a_low, n2, inv2, h2, g, slope_in, dx2, da, gfc, gsum, gb1, dm, up, slope, load, Idle())
+
+
+def e_kernel_comm(line, dx3, tab, w, a_low, n2, inv2, h2, g, slope_in, gq_in, gs_in, dx2, da, gfc, gsum, gb1, out_q, out_s,
+                  dm, up, slope, load, gq, gs, loads, *rest):
+    qb, sb, (send, recv) = rest[:4], rest[4:8], rest[8:]
+    place = Place(line)
+    copies = put_own(((gq_in, gq), (gs_in, gs)), loads)
+    greet(place)
+    for cp in copies:
+        cp.wait()
+    tick = Ticker([(0, scatter_ticks(place, gq, slice(None), *qb, out_q, send.at[0], recv.at[0])),
+                   (0, scatter_ticks(place, gs, slice(None), *sb, out_s, send.at[1], recv.at[1]))])
+    tick()
+    e_phases(dx3, tab, w, a_low, n2, inv2, h2, g, slope_in, dx2, da, gfc, gsum, gb1, dm, up, slope, load, tick)
+    tick.finish()
+
+
+def f_phases(x, sz, tab, wq, n1, inv1, h1, q, p, v, s, rel, dx2, da, gsum, dx, gq, dq, dk, dv, dj, dx1, tick):
     bwd_attn1(q, p, v, s, da, dq, dv, dk)
-    bwd_mix(q, p, v, rel, da, dq, dv, dk, dj, sz, tab, gsum, None)
-    wgrad(h1, dj, gqkv)
-    mm_nt(dj, w, 0, 3, up)
-    norm_back_phase(up, n1, inv1, tab, 0, dx2, None, gsum, 0, 1, None)
-    bwd_conv1(x, dx2, dx, sz, tab, gsum)
-
-
-def bwd_layer(dx3, x, sz, tab, w, res):
-    sd = jax.ShapeDtypeStruct
+    tick()
+    body = bwd_mix(q, p, v, rel, da, dq, dv, dk, sz, tab, gsum)
+    for radius, base, count in ((1, 0, 2), (2, 1, 2), (3, 2, 2), (3, 3, 2)):
+        def run(i, c, radius=radius, base=base):
+            body(radius, base, i)
+            return c
+        lax.fori_loop(0, count, run, 0)
+        tick()
+    bwd_cast(dq, dk, dv, dj)
+    wgrad(h1, dj, gq, 0)
+    tick()
+    mm_nt(dj, wq, 0, 3, dq, True)
+    norm_back_phase(dq, n1, inv1, tab, 0, dx2, dx1, None, gsum, 0, 1, True)
+    tick()
+    bwd_conv1(x, dx1, dx, sz, tab, gsum)
+
+
+def f_kernel(x, sz, tab, wq, n1, inv1, h1, q, p, v, s, rel, dx2, da_in, gsum_in, gb1, dx, gq, gsm, dq, dk, dv, dj, dx1, da, gsum, y, tau, loads):
+    copies = put_own(((da_in, da), (gsum_in, gsum)), loads)
+    for cp in copies:
+        cp.wait()
+    f_phases(x, sz, tab, wq, n1, inv1, h1, q, p, v, s, rel, dx2, da, gsum, dx, gq, dq, dk, dv, dj, dx1, Idle())
+    build_small(gsum, gb1, y, tau, gsm)
+
+
+GFC = ((0, 80), (80, 144))
+
+
+def f_kernel_comm(line, last, x, sz, tab, w_in, n1, inv1, h1, q, p, v, s, rel, dx2, da_in, gsum_in, gb1, gfc_in, *refs):
+    refs = list(refs)
+    if last:
+        dx, out_fc, out_q, out_s = refs[:4]
+        refs = refs[4:]
+        gq, gsm = refs.pop(), refs.pop()
+    else:
+        dx, out_fc, gq, gsm = refs[:4]
+        refs = refs[4:]
+    dq, dk, dv, dj, dx1, da, gsum, y, tau, wq, gfc, loads, send, recv = refs[:14]
+    bufs = refs[14:]
+    place = Place(line)
+    copies = put_own(((gfc_in, gfc), (da_in, da), (gsum_in, gsum), (w_in.at[:, :, :, :, 0:48], wq)), loads)
+    greet(place)
+    for cp in copies:
+        cp.wait()
+    lists = []
+    for i, (a, b) in enumerate(GFC):
+        lists.append((i, scatter_ticks(place, gfc, pl.ds(a, b - a), *bufs[4 * i:4 * i + 4], out_fc.at[pl.ds(a, b - a)], send.at[i], recv.at[i])))
+    tick = Ticker(lists)
+    tick()
+    if not last:
+        f_phases(x, sz, tab, wq, n1, inv1, h1, q, p, v, s, rel, dx2, da, gsum, dx, gq, dq, dk, dv, dj, dx1, tick)
+        tick.finish()
+        build_small(gsum, gb1, y, tau, gsm)
+        return
+    end = Ticker([(0, scatter_ticks(place, gq, slice(None), *bufs[8:12], out_q, send.at[2], recv.at[2]))])
+
+    class Steps(Idle):
+        calls = 0
+
+        def __call__(self):
+            Steps.calls += 1
+            if Steps.calls < 6:
+                tick()
+            else:
+                tick.finish()
+                end()
+    f_phases(x, sz, tab, wq, n1, inv1, h1, q, p, v, s, rel, dx2, da, gsum, dx, gq, dq, dk, dv, dj, dx1, Steps())
+    end()
+    build_small(gsum, gb1, y, tau, gsm)
+    fin = Ticker([(0, scatter_ticks(place, gsm, slice(None), *bufs[12:16], out_s, send.at[3], recv.at[3]))])
+    fin()
+    end.finish()
+    fin.finish()
+
+
+E_OUTS = [sd((R, D), F32), sd((4, RP, 128), F32), packed(4, 144), sd((4, 8 * TROWS, 128), F32), sd((8, FF), F32)]
+E_SCRATCH = [pltpu.VMEM((R, D), BF16), pltpu.VMEM((R, D), F32), pltpu.VMEM((R, FF), BF16), pltpu.SemaphoreType.DMA]
+F_SCRATCH = [pltpu.VMEM((4, RP, 128), F32)] * 3 + [pltpu.VMEM((R, 3 * D), BF16), pltpu.VMEM((R, D), F32), pltpu.VMEM((4, RP, 128), F32),
+             pltpu.VMEM((4, 8 * TROWS, 128), F32), pltpu.VMEM((D, 128), F32), pltpu.VMEM((288, 128), F32)]
+
+
+def bwd_e(dx3, tab, w, res):
     r = dict(zip([n for n, _, _ in RES], res))
-    dx2, da, gw1, gw2, gproj, gsum, gb1 = pl.pallas_call(
-        bwd_e_kernel,
-        out_shape=[sd((R, D), F32), sd((4, RP, 128), F32), sd((D, FF), BF16), sd((FF, D), BF16), sd((D, D), BF16), sd((8 * TROWS, D), F32), sd((8, FF), F32)],
-        in_specs=vspec(9), out_specs=vspec(7),
-        scratch_shapes=[pltpu.VMEM((R, D), BF16), pltpu.VMEM((R, D), F32)],
-        compiler_params=PARAMS, name="block_bwd_e",
+    return pl.pallas_call(
+        e_kernel, out_shape=E_OUTS, in_specs=vspec(8) + [ANY], out_specs=vspec(5), scratch_shapes=E_SCRATCH, compiler_params=PARAMS, name="block_bwd_e",
     )(dx3, tab, w, r["a"], r["n2"], r["inv2"], r["h2"], r["g"], r["slope"])
-    dx, gqkv, gsum = pl.pallas_call(
-        bwd_f_kernel,
-        out_shape=[sd((R, D), F32), sd((D, 3 * D), BF16), sd((8 * TROWS, D), F32)],
-        in_specs=vspec(15), out_specs=vspec(3),
-        scratch_shapes=[pltpu.VMEM((4, RP, 128), F32)] * 3 + [pltpu.VMEM((R, 3 * D), BF16), pltpu.VMEM((R, D), F32)],
-        compiler_params=PARAMS, name="block_bwd_f",
-    )(x, sz, tab, w, r["n1"], r["inv1"], r["h1"], r["q"], r["p"], r["v"], r["s"], r["rel"], dx2, da, gsum)
-    return dx, gqkv, gproj, gw1, gw2, gsum, gb1
+
+
+def bwd_e_comm(line, cid, dx3, tab, w, res, gq, gs):
+    r = dict(zip([n for n, _, _ in RES], res))
+    return pl.pallas_call(
+        functools.partial(e_kernel_comm, line), out_shape=E_OUTS + [sd((48, D), F32), sd((16, 128), F32)],
+        in_specs=vspec(8) + [ANY] * 3, out_specs=vspec(7),
+        scratch_shapes=E_SCRATCH + [pltpu.VMEM((2, line, 2, 2, 48, D), BF16), pltpu.VMEM((2, line, 2, 2, 16, 128), F32), pltpu.SemaphoreType.DMA((2,))]
+        + scatter_bufs(line, 48, D, BF16) + scatter_bufs(line, 16, 128, F32) + [sem_rows(line, 2)] * 2,
+        compiler_params=comm_params(cid), name="comm_bwd_e",
+    )(dx3, tab, w, r["a"], r["n2"], r["inv2"], r["h2"], r["g"], r["slope"], gq, gs)
+
+
+def f_args(r, x, sz, tab, w, dx2, da, gsum, gb1):
+    return (x, sz, tab, w, r["n1"], r["inv1"], r["h1"], r["q"], r["p"], r["v"], r["s"], r["rel"], dx2, da, gsum, gb1)
+
+
+def bwd_f(x, sz, tab, w, res, dx2, da, gsum, gb1):
+    r = dict(zip([n for n, _, _ in RES], res))
+    return pl.pallas_call(
+        f_kernel, out_shape=[sd((R, D), F32), packed(4, 48), packed(4, 16, 128, F32)],
+        in_specs=vspec(13) + [ANY] * 2 + vspec(1), out_specs=vspec(3),
+        scratch_shapes=F_SCRATCH + [pltpu.SemaphoreType.DMA((2,))], compiler_params=PARAMS, name="block_bwd_f",
+    )(*f_args(r, x, sz, tab, w[:, :, :, :, 0:48], dx2, da, gsum, gb1))
+
+
+def bwd_f_comm(line, cid, last, x, sz, tab, w, res, dx2, da, gsum, gb1, gfc):
+    r = dict(zip([n for n, _, _ in RES], res))
+    grads = [pltpu.VMEM((2, line, 2, 2, 16, 128), F32), pltpu.VMEM((2, line, 2, 2, 48, D), BF16)]
+    outs = [sd((R, D), F32), sd((144, D), F32)]
+    outs += [sd((48, D), F32), sd((16, 128), F32)] if last else [packed(line, 48), packed(line, 16, 128, F32)]
+    scratch = F_SCRATCH + [pltpu.VMEM((2, line, 2, 2, 48, D), BF16), pltpu.VMEM((2, line, 2, 2, 144, D), BF16), pltpu.SemaphoreType.DMA((4,)),
+                           sem_rows(line, 4), sem_rows(line, 4)]
+    for a, b in GFC:
+        scratch += scatter_bufs(line, b - a, D, BF16)
+    if last:
+        scratch += scatter_bufs(line, 48, D, BF16) + scatter_bufs(line, 16, 128, F32) + grads
+    return pl.pallas_call(
+        functools.partial(f_kernel_comm, line, last), out_shape=outs,
+        in_specs=vspec(3) + [ANY] + vspec(9) + [ANY] * 2 + vspec(1) + [ANY], out_specs=vspec(4),
+        scratch_shapes=scratch, compiler_params=comm_params(cid), name="last_bwd_f" if last else "comm_bwd_f",
+    )(*f_args(r, x, sz, tab, w, dx2, da, gsum, gb1), gfc)
 
 
 def window_mask():
@@ -854,24 +1143,26 @@
     return w, *tables(vec)
 
 
-def pack_grads(gqkv, gproj, gw1, gw2, small, n):
+def share_by_xla(gfc, gq, gsm, n):
     per = D // n
-    width = small.shape[0] // n
-    pad = -width % D
-    cols = [gqkv[:, j * D:(j + 1) * D] for j in range(3)] + [gproj] + [gw1[:, j * D:(j + 1) * D] for j in range(4)]
-    parts = [c.reshape(n, per, D) for c in cols] + [gw2.reshape(n, FF // n, D)]
-    parts.append(jnp.pad(small.reshape(n, width), ((0, 0), (0, pad))).reshape(n, -1, D).astype(BF16))
-    return jnp.concatenate(parts, axis=1)
-
-
-def split_grads(shard, n, width):
-    per = D // n
-
+
+    def rows(a):
+        return a.transpose(1, 2, 3, 0, 4, 5).reshape((32,) + a.shape[4:])
+    gq, gfc, gsm = rows(gq), rows(gfc), rows(gsm)
+    every = jnp.concatenate([gq, gfc[:, :80]], axis=1)
+    parts = [every[:, 16 * j:16 * j + 16].reshape(n, per, D) for j in range(8)] + [gfc[:, 80:].reshape(n, FF // n, D)]
+    vec = gsm[:, :9].reshape(n, -1)
+    width = vec.shape[1]
+    parts.append(jnp.pad(vec, ((0, 0), (0, -width % D))).reshape(n, -1, D).astype(BF16))
+    share = lax.psum_scatter(jnp.concatenate(parts, axis=1), AXES, scatter_dimension=0, tiled=True)[0].astype(F32)
+    mats = split_shares(share[:8 * per + FF // n], per)
+    return (*mats, share[8 * per + FF // n:].reshape(-1)[:width])
+
+
+def split_shares(share, per):
     def cols(first, count):
-        return shard[first * per:(first + count) * per].reshape(count, per, D).transpose(1, 0, 2).reshape(-1)
-    fc2 = shard[8 * per:8 * per + FF // n].reshape(-1)
-    small = shard[8 * per + FF // n:].reshape(-1)[:width]
-    return cols(0, 3), cols(3, 1), cols(4, 4), fc2, small
+        return share[first * per:(first + count) * per].reshape(count, per, D).transpose(1, 0, 2).reshape(-1)
+    return cols(0, 3), cols(3, 1), cols(4, 4), share[8 * per:].reshape(-1)
 
 
 def tables(small):
@@ -883,12 +1174,6 @@
     return tab.reshape(TROWS, 4, 128).transpose(1, 0, 2), small[end:end + FF].reshape(16, 128)
 
 
-def small_grads(gsum, gb1):
-    s = gsum.reshape(TROWS, 8, D).sum(1)
-    tb = jnp.concatenate([s[:9], s[9:58] * window_mask()]).T
-    return jnp.concatenate([tb.reshape(-1), gb1.sum(0), s[CPE:CPE + 10].T.reshape(-1)])
-
-
 def to_rows(a):
     return jnp.transpose(a, (1, 0, 2)).reshape(R, D)
 
@@ -900,7 +1185,7 @@
 def shards(n, images, grid_sizes, qkv, proj, fc1, fc2, small, cotangent):
     layers = qkv.shape[0]
     width = small.shape[1]
-    packed = [pack(qkv[l], proj[l], fc1[l], fc2[l], n) for l in range(layers)]
+    packed_w = [pack(qkv[l], proj[l], fc1[l], fc2[l], n) for l in range(layers)]
     slot = lax.broadcasted_iota(jnp.int32, (SLOT, 1), 0)
     cellno = jnp.maximum(slot - 1, 0)
     far = jnp.maximum(cellno // GRID, cellno % GRID)
@@ -908,29 +1193,37 @@
     sz = jnp.broadcast_to(grid_sizes[:, None], (NI, 128))
     x = to_rows(images)
     saved = []
-    if n == 32 and layers == 2:
+    dy = jnp.where(present, jnp.transpose(cotangent, (1, 0, 2)), 0).astype(F32).reshape(R, D)
+    count = 1 + len(RES)
+    if n == 32 and layers == 2 and width == 1152:
+        line = n // 8
         flat = jnp.pad(small.astype(F32).reshape(2, 9, 128), ((0, 0), (0, 7), (0, 0))).reshape(32, 128)
-        out = fwd_first(4, x, sz, packed[0], packed[1], flat)
-        count = 1 + len(RES)
-        w0, w1, tab, b1 = out[count:]
-        held = [(w0, tab[0], b1[0]), (w1, tab[1], b1[1])]
+        out0 = fwd_first(line, x, sz, packed_w[0], packed_w[1], flat)
+        w0, w1a, tab, b1 = out0[count:]
+        x1, res0 = out0[0], out0[1:count]
+        out1 = fwd_second(line, x1, sz, tab[1], b1[1], w1a, packed_w[1])
+        last, res1, w1 = out1[0], out1[1:count], out1[count]
+        dx2, da, gfc1, gsum, gb1 = bwd_e(dy, tab[1], w1, res1)
+        dx, sfc1, gq1, gsm1 = bwd_f_comm(line, 2, False, x1, sz, tab[1], w1, res1, dx2, da, gsum, gb1, gfc1)
+        dx2, da, gfc0, gsum, gb1, sq1, ss1 = bwd_e_comm(line, 3, dx, tab[0], w0, res0, gq1, gsm1)
+        dx, sfc0, sq0, ss0 = bwd_f_comm(line, 4, True, x, sz, tab[0], w0, res0, dx2, da, gsum, gb1, gfc0)
+        shares = [(*split_shares(jnp.concatenate([q, fc]), D // n), s[:9].reshape(-1)) for q, fc, s in ((sq0, sfc0, ss0), (sq1, sfc1, ss1))]
     else:
-        held = [whole_weights(packed[l], small[l], n) for l in range(layers)]
-        out = None
-    for l in range(layers):
-        w, tab, b1 = held[l]
-        if l or out is None:
-            out = fwd_layer(x, sz, tab, b1, w)
-        saved.append((x, tab, w, out[1:1 + len(RES)]))
-        x = out[0]
-    output = from_rows(jnp.where(present, x.reshape(SLOT, NI, D), 0.0).astype(BF16))
-    dx = jnp.where(present, jnp.transpose(cotangent, (1, 0, 2)), 0).astype(F32).reshape(R, D)
-    shares = [None] * layers
-    for l in reversed(range(layers)):
-        xin, tab, w, res = saved[l]
-        dx, gqkv, gproj, gw1, gw2, gsum, gb1 = bwd_layer(dx, xin, sz, tab, w, res)
-        g = pack_grads(gqkv, gproj, gw1, gw2, small_grads(gsum, gb1), n)
-        shares[l] = split_grads(lax.psum_scatter(g, AXES, scatter_dimension=0, tiled=True)[0].astype(F32), n, width)
+        held = [whole_weights(packed_w[l], small[l], n) for l in range(layers)]
+        last = x
+        for l in range(layers):
+            w, tab, b1 = held[l]
+            out = fwd_layer(last, sz, tab, b1, w)
+            saved.append((last, tab, w, out[1:count]))
+            last = out[0]
+        shares = [None] * layers
+        dx = dy
+        for l in reversed(range(layers)):
+            xin, tab, w, res = saved[l]
+            dx2, da, gfc, gsum, gb1 = bwd_e(dx, tab, w, res)
+            dx, gq, gsm = bwd_f(xin, sz, tab, w, res, dx2, da, gsum, gb1)
+            shares[l] = share_by_xla(gfc, gq, gsm, n)
+    output = from_rows(jnp.where(present, last.reshape(SLOT, NI, D), 0.0).astype(BF16))
     grads = [jnp.stack([shares[l][i] for l in range(layers)]) for i in range(5)]
     return (output, from_rows(dx), *grads)
 

time: 756 us -> 506 us (0.67)
  waiting for transfers between devices: 278 us -> 0 us
  Pallas kernels: 383 us -> 469 us
  local copies, waits for them, and re-layouts: 50.2 us -> 20.9 us
  between operations: 14.9 us -> 1.07 us
  other arithmetic: 24.2 us -> 11.9 us
    reduce_scatter x2 -> x0, waiting for transfers between devices: 278 us -> none  [shards(): lax.psum_scatter(g, AXES, scatter_dimension=0, tiled=True)[0].astype(F32)]
    pallas_call x5, Pallas kernels: 252 us -> 352 us  [the longest x2 185 us: bwd_f_comm(): pl.pallas_call(functools.partial(f_kernel_comm, line, last), out_shape=ou...]
    unnamed x46 -> x17, local copies, waits for them, and re-layouts: 22.6 us -> 6.8 us
    pallas_call x1, Pallas kernels: 131 us -> 117 us  [fwd_first(): pl.pallas_call(functools.partial(first_kernel, line), out_shape=outs, in_...]
    slice x16 -> x4, local copies, waits for them, and re-layouts: 16.7 us -> 5.97 us  [shards(): packed_w = [pack(qkv[l], proj[l], fc1[l], fc2[l], n) for l in range(layers)]]
  transfers between devices with their start and end apart: 2 -> 0, of which waited for: 2 -> 0; matrix products, arithmetic and copies ran while one was open for 2% -> 0% of each run, Pallas kernels for 0% -> 0%
where the time goes in v3:
time: 506 us; the launch traced here: 503 us
  Pallas kernels  469 us (93%)
  local copies, waits for them, and re-layouts  20.9 us (4%)
  other arithmetic  11.9 us (2%)
    pallas_call x2, Pallas kernels, bwd_f_comm(): pl.pallas_call(functools.partial(f_kernel_comm, line, last), out_shape=ou...  185 us
    pallas_call x1, Pallas kernels, fwd_first(): pl.pallas_call(functools.partial(first_kernel, line), out_shape=outs, in_...  117 us
    pallas_call x1, Pallas kernels, fwd_second(): pl.pallas_call(functools.partial(second_kernel, line), out_shape=outs, in...  78.7 us
    pallas_call x1, Pallas kernels, bwd_e_comm(): pl.pallas_call(functools.partial(e_kernel_comm, line), out_shape=E_OUTS +...  50.5 us
    pallas_call x1, Pallas kernels, bwd_e(): pl.pallas_call(e_kernel, out_shape=E_OUTS, in_specs=vspec(8) + [ANY], out...  37.5 us

profile of v3, /device:TPU:0, one launch (start us, length us, event | category | flops | bytes accessed | tf_op | source)
XLA Modules:
  0.0 503.0 jit_solution(13252192695836611601)
XLA Ops:
  0.7 0.7 compare_or_fusion
  1.4 1.3 broadcast_in_dim.31.sz
  2.7 0.7 reshape.148
  3.4 0.6 bitcast_convert_fusion.1.small
  4.1 0.7 copy.31
  4.8 1.0 slice_reduce_fusion.6
  5.8 1.5 slice_reduce_fusion.4
  7.5 1.7 slice_reduce_fusion.1
  9.3 1.7 slice_reduce_fusion
  11.1 0.8 pad_maximum_fusion.2
  11.9 117.5 %first_fwd.1 = (f32[1312,512]{1,0:T(8,128)}, bf16[1312,512]{1,0:T(8,128)(2,1)}, f32[1312,128]{1,0:T(8,128)}, bf16[1312,512]{1,0:T(8,128)(2,1)}, f32[4,1536,128]{...) custom-call(bf16[1312,512]{1,0:T(8,128)(2,1)} %bitcast.75, ...), custom_call_target="tpu_custom_call" | custom-call | tf_op jit(solution)/shard_map/first_fwd/pallas_call | solution.py:683
  129.4 1.7 slice_bitcast_fusion
  131.1 1.3 slice_bitcast_fusion.8.b1
  132.4 78.7 %second_fwd.1 = (f32[1312,512]{1,0:T(8,128)}, bf16[1312,512]{1,0:T(8,128)(2,1)}, f32[1312,128]{1,0:T(8,128)}, bf16[1312,512]{1,0:T(8,128)(2,1)}, f32[4,1536,128]...) custom-call(f32[1312,512]{1,0:T(8,128)} %get-tuple-element.62.x, ...), custom_call_target="tpu_custom_call" | custom-call | tf_op jit(solution)/shard_map/second_fwd/pallas_call | solution.py:693
  211.1 3.7 bitcast_select_fusion
  214.8 2.0 bitcast_convert_fusion.dx3
  216.8 37.5 %block_bwd_e.1 = (f32[1312,512]{1,0:T(8,128)}, f32[4,1536,128]{2,1,0:T(8,128)}, bf16[2,4,2,2,144,512]{5,4,3,2,1,0:T(8,128)(2,1)}, f32[4,640,128]{2,1,0:T(8,128)}, f32[8,2048]{1,0:T(8,128)}) custom-call(f32[1312,512]{1,0:T(8,128)} %bitcast_convert_fusion.dx3, f32[4,80,128]{2,1,0:T(8,128)} %get-tuple-element.126.tab, ...), custom_call_target="tpu_custom_call" | custom-call | tf_op jit(solution)/shard_map/block_bwd_e/pallas_call | solution.py:1073
  254.3 80.1 %comm_bwd_f.1 = (f32[1312,512]{1,0:T(8,128)}, f32[144,512]{1,0:T(8,128)}, bf16[2,4,2,2,48,512]{5,4,3,2,1,0:T(8,128)(2,1)}, f32[2,4,2,2,16,128]{5,4,3,2,1,0:T(8,128)}) custom-call(f32[1312,512]{1,0:T(8,128)} %get-tuple-element.62.x, s32[16,128]{1,0:T(8,128)} %broadcast_in_dim.31.sz, f32[4,80,128]{2,1,0:T(8,128)} %get-tuple-element.126.tab, ...), custom_call_target="tpu_custom_call" | custom-call | tf_op jit(solution)/shard_map/comm_bwd_f/pallas_call | solution.py:1113
  334.4 50.5 %comm_bwd_e.1 = (f32[1312,512]{1,0:T(8,128)}, f32[4,1536,128]{2,1,0:T(8,128)}, bf16[2,4,2,2,144,512]{5,4,3,2,1,0:T(8,128)(2,1)}, f32[4,640,128]{2,1,0:T(8,128)},...) custom-call(f32[1312,512]{1,0:T(8,128)} %get-tuple-element.96.dx3, ...), custom_call_target="tpu_custom_call" | custom-call | tf_op jit(solution)/shard_map/comm_bwd_e/pallas_call | solution.py:1080
  385.0 104.9 %last_bwd_f.1 = (f32[1312,512]{1,0:T(8,128)}, f32[144,512]{1,0:T(8,128)}, f32[48,512]{1,0:T(8,128)}, f32[16,128]{1,0:T(8,128)}) custom-call(bf16[1312,512]{1,0:T(8,128)(2,1)} %bitcast.76, s32[16,128]{1,0:T(8,128)} %broadcast_in_dim.31.sz, f32[4,80,128]{2,1,0:T(8,128)} %get-tuple-element.125.tab, bf16[2,4,2,2,192,512]{5,4,3,2,1,0:T(8,128)(2,1)} %get-tuple-element.67.w.w_in, ...), custom_call_target="tpu_custom_call" | custom-call | tf_op jit(solution)/shard_map/last_bwd_f/pallas_call | solution.py:1113
  489.9 0.7 slice_bitcast_fusion.7
  490.6 0.7 slice_bitcast_fusion.6
  492.0 1.1 copy.51
  493.2 0.8 slice_bitcast_fusion.5
  494.0 1.0 slice_bitcast_fusion.3
  495.4 0.8 slice_bitcast_fusion.4
  496.2 1.0 slice_bitcast_fusion.2
  497.3 0.9 pad_maximum_fusion.1
  498.5 0.9 pad_maximum_fusion
  499.5 0.7 pad_maximum_fusion.5
  500.4 0.9 pad_maximum_fusion.4
  501.3 1.5 copy.55
  (33 shorter events, 2.2 us)
Async XLA Ops:
  489.9 10.3 %copy-start.1 = (f32[48,512]{1,0:T(8,128)S(1)}, f32[48,512]{1,0:T(8,128)}, u32[]{:S(2)}) copy-start(f32[48,512]{1,0:T(8,128)} %get-tuple-element.112) | copy-start | bytes 294916
  492.0 9.3 %copy-start = (f32[1312,512]{1,0:T(8,128)S(1)}, f32[1312,512]{1,0:T(8,128)}, u32[]{:S(2)}) copy-start(f32[1312,512]{1,0:T(8,128)} %get-tuple-element.110) | copy-start | bytes 8060932

commit v4 on v1

v4 whole, which is shorter than its diff:
```python
import functools
import jax
import jax.numpy as jnp
from jax import lax
from jax.experimental import pallas as pl
from jax.experimental.pallas import tpu as pltpu

F32, BF16 = jnp.float32, jnp.bfloat16
D, FF, HEADS, GRID, SLOT = 512, 2048, 8, 9, 82
TABLE = 58
EPS = 1e-6
NI = 16
R = SLOT * NI
PADS = 96
RP = PADS * NI
RADII = (1, 2, 3, 3)
AXES = ("wide", "narrow")
WROWS = 192
TAPS, CPE, CPEB, TROWS = 9, 64, 73, 80


def ds(start, size, align=8):
    if not isinstance(start, int):
        start = pl.multiple_of(start, align)
    return pl.ds(start, size)


def row8(ref, i, lg):
    return ref[lg, pl.ds(i, 8, stride=0), :]


def row(tab, i, j=None):
    parts = range(4) if j is None else (2 * j, 2 * j + 1)
    return jnp.concatenate([tab[g, i:i + 1, :] for g in parts], axis=1)


def put2(ref, at, j, val):
    ref[2 * j, at, :] = val[:, :128]
    ref[2 * j + 1, at, :] = val[:, 128:]


def cell(y, x, ig):
    return ds((1 + GRID * y + x) * NI + 8 * ig, 8)


def inside_at(sz, y, x):
    return sz > max(y, x)


PROW = GRID * NI
PADDED = ((GRID + 6) * PROW, 128)


def at_cell(y, x, ig):
    return pl.ds(pl.multiple_of((1 + GRID * y + x) * NI + 8 * ig, 8), 8)


def at_padded(y, x, ig):
    return pl.ds(pl.multiple_of((y + 3) * PROW + x * NI + 8 * ig, 8), 8)


def rows_loop(fn, init):
    return lax.fori_loop(0, GRID, fn, init)


def groups(fn):
    def run(ig, c):
        fn(ig)
        return c
    lax.fori_loop(0, 2, run, 0)


def lane_groups(fn):
    fn(1, 0)
    fn(2, 1)

    def run(i, c):
        fn(3, i + 2)
        return c
    lax.fori_loop(0, 2, run, 0)


def conv_pass(src, load_tap, radius, ig, emit, init, flip=False):
    span = range(-radius, radius + 1)

    def body(y, carry):
        acc = [None] * GRID
        for a in span:
            line = [src[at_padded(y - a if flip else y + a, x, ig), :] for x in range(GRID)]
            for b in span:
                tap = load_tap(a, b)
                for x in range(GRID):
                    xx = x - b if flip else x + b
                    if 0 <= xx < GRID:
                        term = line[xx] * tap
                        acc[x] = term if acc[x] is None else acc[x] + term
        return emit(y, acc, carry)
    return rows_loop(body, init)


def conv_kgrad(grad, src, radius, emit):
    span = range(-radius, radius + 1)
    rows = list(span)
    for part in (rows[:4], rows[4:]):
        if not part:
            continue

        def body(t, acc):
            y, ig = t // 2, t % 2
            acc = list(acc)
            up = [grad[at_padded(y, x, ig), :] for x in range(GRID)]
            for i, a in enumerate(part):
                line = [src[at_padded(y + a, x, ig), :] for x in range(GRID)]
                for j, b in enumerate(span):
                    k = i * len(span) + j
                    for x in range(GRID):
                        if 0 <= x + b < GRID:
                            acc[k] = acc[k] + up[x] * line[x + b]
            return tuple(acc)
        zero = jnp.zeros((8, 128), F32)
        sums = lax.fori_loop(0, 2 * GRID, body, (zero,) * (len(part) * len(span)))
        for i, a in enumerate(part):
            for j, b in enumerate(span):
                emit(a, b, sums[i * len(span) + j])


def zero_padded(ref):
    ref[...] = jnp.zeros(PADDED, F32)


def fill_padded(dst, src, lg, sz):
    def body(t, c):
        y, ig = t // 2, t % 2
        size = sz[ds(8 * ig, 8), :]
        for x in range(GRID):
            dst[at_padded(y, x, ig), :] = jnp.where(size > jnp.maximum(y, x), src[lg, at_cell(y, x, ig), :], 0.0)
        return c
    lax.fori_loop(0, 2 * GRID, body, 0)


def norm_rows(x):
    mean = jnp.mean(x, axis=-1, keepdims=True)
    cen = x - mean
    inv = lax.rsqrt(jnp.mean(cen * cen, axis=-1, keepdims=True) + EPS)
    return cen * inv, inv


def dot(a, b, ca, cb):
    return lax.dot_general(a, b, (((ca,), (cb,)), ((), ())), preferred_element_type=F32)


def head_mask():
    r = lax.broadcasted_iota(jnp.int32, (256, 256), 0) // 64
    c = lax.broadcasted_iota(jnp.int32, (256, 256), 1) // 64
    return r == c


def by_tiles(fn):
    def body(i, c):
        fn(pl.ds(pl.multiple_of(i * 256, 256), 256))
        return c
    lax.fori_loop(0, R // 256, body, 0)
    if R % 256:
        fn(pl.ds(R // 256 * 256, R % 256))


def full(ref, at):
    return jnp.concatenate([ref[g, at, :] for g in range(4)], axis=1)


def spread(ref, at, val):
    for g in range(4):
        ref[g, at, :] = val[:, 128 * g:128 * g + 128]


def fwd_conv1(x, sz, tab, x1, pv):
    def one(lg, c):
        fill_padded(pv, x, lg, sz)

        def group(ig):
            size = sz[ds(8 * ig, 8), :]
            x1[lg, ds(8 * ig, 8), :] = x[lg, ds(8 * ig, 8), :]
            bias = row8(tab, CPEB, lg)

            def emit(y, acc, carry):
                for k in range(GRID):
                    at = at_cell(y, k, ig)
                    x1[lg, at, :] = x[lg, at, :] + jnp.where(size > jnp.maximum(y, k), acc[k] + bias, 0.0)
                return carry
            conv_pass(pv, lambda a, b: row8(tab, CPE + (a + 1) * 3 + b + 1, lg), 1, ig, emit, 0)
        groups(group)
        return c
    lax.fori_loop(0, 4, one, 0)


def norm_phase(src, tab, gain, shift, hat, low, inv_ref):
    def fn(at):
        n, inv = norm_rows(full(src, at))
        hat[at, :] = n.astype(BF16)
        low[at, :] = (n * row(tab, gain) + row(tab, shift)).astype(BF16)
        inv_ref[at, :] = jnp.broadcast_to(inv, (n.shape[0], 128))
    by_tiles(fn)


def weight(g, block, first, count, cols):
    at = ds(16 * block, 16, 16)
    return jnp.concatenate([g[t % 2, t // 8, t // 4 % 2, t // 2 % 2, at, cols] for t in range(first // 16, (first + count) // 16)], axis=0)


def weight2(g, chunk, cols):
    return jnp.concatenate([g[i % 2, chunk, i // 4, i // 2 % 2, 128:192, cols] for i in range(8)], axis=0)


def halves(fn):
    def body(i, c):
        fn(pl.ds(pl.multiple_of(i * (R // 2), 16), R // 2))
        return c
    lax.fori_loop(0, 2, body, 0)


def zero_tail(ref):
    ref[:, R:RP, :] = jnp.zeros((4, RP - R, 128), F32)


def fwd_qkv(low, w, tab, q, k, v):
    def fn(at):
        h = low[at, :]
        for b, (ref, bias) in enumerate(((q, 4), (k, None), (v, 5))):
            for j in range(2):
                val = dot(h, weight(w, b, 0, D, slice(256 * j, 256 * j + 256)), 1, 0)
                put2(ref, at, j, val if bias is None else val + row(tab, bias, j))
    halves(fn)
    for ref in (q, k, v):
        zero_tail(ref)


def each_pos(size, ig, fn):
    fn(ds(8 * ig, 8), None)
    for y in range(GRID):
        for x in range(GRID):
            fn(cell(y, x, ig), inside_at(size, y, x))


def fwd_softmax(k, sz):
    def body(i, c):
        lg, ig = i // 2, i % 2
        size = sz[ds(8 * ig, 8), :]
        best = [None] * 4
        cnt = [0]

        def first(at, ok):
            val = k[lg, at, :]
            if ok is not None:
                val = jnp.where(ok, val, -1e30)
            j = cnt[0] % 4
            best[j] = val if best[j] is None else jnp.maximum(best[j], val)
            cnt[0] += 1
        each_pos(size, ig, first)
        top = jnp.maximum(jnp.maximum(best[0], best[1]), jnp.maximum(best[2], best[3]))
        total = [None] * 4
        cnt[0] = 0

        def second(at, ok):
            val = jnp.exp(k[lg, at, :] - top)
            if ok is not None:
                val = jnp.where(ok, val, 0.0)
            k[lg, at, :] = val
            j = cnt[0] % 4
            total[j] = val if total[j] is None else total[j] + val
            cnt[0] += 1
        each_pos(size, ig, second)
        scale = 1.0 / ((total[0] + total[1]) + (total[2] + total[3]))

        def third(at, ok):
            k[lg, at, :] = k[lg, at, :] * scale
        each_pos(size, ig, third)
        return c
    lax.fori_loop(0, 8, body, 0)


def img_load(ref, i, half):
    return jnp.concatenate([ref[2 * half + j, pl.ds(i, PADS, stride=NI), :] for j in range(2)], axis=1)


def img_store(ref, i, half, val):
    for j in range(2):
        ref[2 * half + j, pl.ds(i, PADS, stride=NI), :] = val[:, 128 * j:128 * j + 128]


def fwd_attn(q, p, v, s, f, first, count):
    def body(t, c):
        i, half = t // 2, t % 2
        pi = img_load(p, i, half).astype(BF16)
        vi = img_load(v, i, half).astype(BF16)
        summ = jnp.where(head_mask(), dot(pi, vi, 0, 0), 0.0).astype(BF16)
        s[t] = (summ[0:64] + summ[64:128]) + (summ[128:192] + summ[192:256])
        qi = img_load(q, i, half).astype(BF16)
        img_store(f, i, half, dot(qi, summ, 1, 0) * 0.125)
        return c
    lax.fori_loop(0, count, lambda t, c: body(t + first, c), 0, unroll=8)


def fwd_conv3(v, q, f, sz, tab, rel, pv, radius, lg):
    fill_padded(pv, v, lg, sz)
    bias = row8(tab, 8, lg)

    def group(ig):
        size = sz[ds(8 * ig, 8), :]

        def emit(y, acc, carry):
            for k in range(GRID):
                at = at_cell(y, k, ig)
                r = acc[k] + bias
                rel[lg, at, :] = r
                f[lg, at, :] = f[lg, at, :] + jnp.where(size > jnp.maximum(y, k), q[lg, at, :] * r, 0.0)
            return carry
        conv_pass(pv, lambda a, b: row8(tab, TAPS + (a + 3) * 7 + b + 3, lg), radius, ig, emit, 0)
    groups(group)


def fwd_proj(att, w, tab, x1, a_low):
    def fn(at):
        low = full(att, at).astype(BF16)
        a_low[at, :] = low
        for j in range(2):
            res = jnp.concatenate([x1[2 * j, at, :], x1[2 * j + 1, at, :]], axis=1)
            put2(x1, at, j, res + dot(low, weight(w, 3, 0, D, slice(256 * j, 256 * j + 256)), 1, 0) + row(tab, 6, j))
    halves(fn)


def normal_cdf(u):
    t = 1.0 / (1.0 + jnp.abs(u) * (0.3275911 * 0.7071067811865476))
    e = jnp.exp(-0.5 * u * u)
    poly = t * (0.5 * 0.254829592 + t * (0.5 * -0.284496736 + t * (0.5 * 1.421413741 + t * (0.5 * -1.453152027 + t * (0.5 * 1.061405429)))))
    tail = poly * e
    return jnp.where(u >= 0, 1.0 - tail, tail), e


def fwd_fc1(low, w, b1, g, slope, first, count):
    def body(j, c):
        cols = pl.ds(pl.multiple_of(j * 512, 512), 512)
        bias = jnp.concatenate([b1[pl.ds(4 * j + i, 1), :] for i in range(4)], axis=1)
        u = dot(low[...], weight(w, 4 + j, 0, D, slice(None)), 1, 0) + bias
        cdf, e = normal_cdf(u)
        g[:, cols] = (u * cdf).astype(BF16)
        slope[:, cols] = (cdf + u * e * 0.3989422804014327).astype(BF16)
        return c
    lax.fori_loop(0, count, lambda j, c: body(j + first, c), 0)


def fwd_fc2(g, w, tab, x1):
    def fn(at):
        for j in range(2):
            cols = slice(256 * j, 256 * j + 256)
            res = jnp.concatenate([x1[2 * j, at, :], x1[2 * j + 1, at, :]], axis=1)
            put2(x1, at, j, res + dot(g[at, :], jnp.concatenate([weight2(w, c, cols) for c in range(4)], axis=0), 1, 0) + row(tab, 7, j))
    halves(fn)


def fold_rows(val):
    parts = [val[8 * i:8 * i + 8] for i in range(val.shape[0] // 8)]
    while len(parts) > 1:
        parts = [a + b for a, b in zip(parts[::2], parts[1::2])] + parts[len(parts) // 2 * 2:]
    return parts[0]


def add_rows(ref, row, val):
    total = jnp.sum(fold_rows(val), axis=0, keepdims=True)
    for g in range(4):
        ref[g, row:row + 1, :] += total[:, 128 * g:128 * g + 128]


def add_sum(ref, lg, row, val):
    ref[lg, row:row + 1, :] += jnp.sum(val, axis=0, keepdims=True)


def bwd_cast_sum(dx, low, gsum, row):
    def fn(at):
        val = full(dx, at).astype(BF16)
        low[at, :] = val
        add_rows(gsum, row, val.astype(F32))
    by_tiles(fn)


def bwd_du(dm, w, slope, gb1):
    def body(j, c):
        cols = pl.ds(pl.multiple_of(j * 512, 512), 512)
        d = dot(dm[...], weight2(w, j, slice(None)), 1, 1) * slope[:, cols].astype(F32)
        slope[:, cols] = d.astype(BF16)
        gb1[:, cols] = fold_rows(d)
        return c
    lax.fori_loop(0, 4, body, 0)


def norm_back_phase(up, hat, inv_ref, tab, gain, res, out_low, sums, rg, rs, rb):
    def fn(at):
        u = full(up, at)
        n = hat[at, :].astype(F32)
        e = u * row(tab, gain)
        m1 = jnp.mean(e, axis=-1, keepdims=True)
        m2 = jnp.mean(e * n, axis=-1, keepdims=True)
        d = full(res, at) + inv_ref[at, 0:1] * (e - m1 - n * m2)
        spread(res, at, d)
        add_rows(sums, rg, u * n)
        add_rows(sums, rs, u)
        if out_low is not None:
            low = d.astype(BF16)
            out_low[at, :] = low
            add_rows(sums, rb, low.astype(F32))
    by_tiles(fn)


def mm_nt(a, cols, g, first, blocks, out):
    def fn(at):
        for j in range(2):
            w = jnp.concatenate([weight(g, first + b, 256 * j, 256, slice(None)) for b in range(blocks)], axis=1)
            put2(out, at, j, dot(a[at, cols], w, 1, 1))
    halves(fn)


def wgrad(left, right, gr, first, blocks):
    for j in range(blocks):
        tile = dot(left[...], right[:, 512 * j:512 * j + 512], 0, 0).astype(BF16)
        for t in range(32):
            gr[t % 2, t // 8, t // 4 % 2, t // 2 % 2, first + 16 * j:first + 16 * j + 16, :] = tile[16 * t:16 * t + 16]


def wgrad2(left, right, gr, first):
    for j in range(4):
        tile = dot(left[:, 512 * j:512 * j + 512], right[...], 0, 0).astype(BF16)
        for i in range(8):
            gr[i % 2, j, i // 4, i // 2 % 2, first:first + 64, :] = tile[64 * i:64 * i + 64]


def bwd_attn1(q, p, v, s, da, dq, dv, dk, first, count):
    def body(t, c):
        i, half = t // 2, t % 2
        df = (img_load(da, i, half) * 0.125).astype(BF16)
        wide = s[t]
        wide = jnp.where(head_mask(), jnp.concatenate([wide] * 4, axis=0), jnp.zeros((), BF16))
        qi = img_load(q, i, half).astype(BF16)
        dsum = jnp.where(head_mask(), dot(qi, df, 0, 0), 0.0).astype(BF16)
        img_store(dq, i, half, dot(df, wide, 1, 1))
        pi = img_load(p, i, half).astype(BF16)
        img_store(dv, i, half, dot(pi, dsum, 1, 0))
        vi = img_load(v, i, half).astype(BF16)
        img_store(dk, i, half, dot(vi, dsum, 1, 1))
        return c
    lax.fori_loop(0, count, lambda t, c: body(t + first, c), 0, unroll=8)


def bwd_mix(q, p, v, rel, da, dq, dv, dk, sz, tab, gsum, pv, pr, radius, lg):
    fill_padded(pv, v, lg, sz)

    def group(ig):
        size = sz[ds(8 * ig, 8), :]
        cls = ds(8 * ig, 8)
        dqc = dq[lg, cls, :]

        def first(y, carry):
            rs, qs, ps = carry
            for x in range(GRID):
                at = at_cell(y, x, ig)
                d = jnp.where(size > jnp.maximum(y, x), da[lg, at, :], 0.0)
                dr = q[lg, at, :] * d
                pr[at_padded(y, x, ig), :] = dr
                dqv = dq[lg, at, :] + rel[lg, at, :] * d
                dq[lg, at, :] = dqv
                rs, qs, ps = rs + dr, qs + dqv, ps + p[lg, at, :] * dk[lg, at, :]
            return rs, qs, ps
        rs, qs, ps = rows_loop(first, (jnp.zeros((8, 128), F32), dqc, p[lg, cls, :] * dk[lg, cls, :]))
        add_sum(gsum, lg, 8, rs)
        add_sum(gsum, lg, 4, qs)
        dk[lg, cls, :] = p[lg, cls, :] * (dk[lg, cls, :] - ps)

        def second(y, carry):
            for x in range(GRID):
                at = at_cell(y, x, ig)
                dk[lg, at, :] = p[lg, at, :] * (dk[lg, at, :] - ps)
            return carry
        rows_loop(second, 0)

        def emit(y, acc, total):
            for x in range(GRID):
                at = at_cell(y, x, ig)
                val = dv[lg, at, :] + jnp.where(size > jnp.maximum(y, x), acc[x], 0.0)
                dv[lg, at, :] = val
                total = total + val
            return total
        add_sum(gsum, lg, 5, conv_pass(pr, lambda a, b: row8(tab, TAPS + (a + 3) * 7 + b + 3, lg), radius, ig, emit, dv[lg, cls, :], True))
    groups(group)

    def emit_tap(a, b, val):
        add_sum(gsum, lg, TAPS + (a + 3) * 7 + b + 3, val)
    conv_kgrad(pr, pv, radius, emit_tap)


def bwd_cast(dq, dk, dv, dj):
    def fn(at):
        for j, ref in enumerate((dq, dk, dv)):
            dj[at, 512 * j:512 * j + 512] = full(ref, at).astype(BF16)
    by_tiles(fn)


def bwd_conv1(x, dx1, dx, sz, tab, gsum, pv, pr):
    def one(lg, c):
        fill_padded(pv, x, lg, sz)
        fill_padded(pr, dx1, lg, sz)

        def group(ig):
            size = sz[ds(8 * ig, 8), :]
            cls = ds(8 * ig, 8)
            dx[lg, cls, :] = dx1[lg, cls, :]

            def emit(y, acc, total):
                for k in range(GRID):
                    at = at_cell(y, k, ig)
                    total = total + pr[at_padded(y, k, ig), :]
                    dx[lg, at, :] = dx1[lg, at, :] + jnp.where(size > jnp.maximum(y, k), acc[k], 0.0)
                return total
            add_sum(gsum, lg, CPEB, conv_pass(pr, lambda a, b: row8(tab, CPE + (a + 1) * 3 + b + 1, lg), 1, ig, emit, jnp.zeros((8, 128), F32), True))
        groups(group)

        def emit_tap(a, b, val):
            add_sum(gsum, lg, CPE + (a + 1) * 3 + b + 1, val)
        conv_kgrad(pr, pv, 1, emit_tap)
        return c
    lax.fori_loop(0, 4, one, 0)


MESH = pl.DeviceIdType.MESH


class Place:
    def __init__(self, line):
        w, m = lax.axis_index("wide"), lax.axis_index("narrow")
        self.line = line
        self.z, self.x, self.y, self.c = w // 2, w % 2, m // 2, m % 2

    def dev(self, z=None, x=None, y=None, c=None):
        z = self.z if z is None else z
        x = self.x if x is None else x
        y = self.y if y is None else y
        c = self.c if c is None else c
        return (z * 2 + x, y * 2 + c)

    def off(self, k):
        return lax.rem(self.z + self.line + k, self.line)


def greet(place):
    barrier = pltpu.get_barrier_semaphore()
    far = [place.dev(z=place.off(k)) for k in range(1, place.line)]
    near = [place.dev(x=1 - place.x), place.dev(y=1 - place.y), place.dev(c=1 - place.c)]
    for who in far + near:
        pl.semaphore_signal(barrier, inc=1, device_id=who, device_id_type=MESH)
    pl.semaphore_wait(barrier, place.line + 2)


def remote(src, dst, send, recv, dev):
    return pltpu.make_async_remote_copy(src_ref=src, dst_ref=dst, send_sem=send, recv_sem=recv, device_id=dev, device_id_type=MESH)


def both(copy):
    copy.wait_send()
    copy.wait_recv()


def by_core(place, a, b):
    def run():
        @pl.when(place.c == 0)
        def _():
            a()

        @pl.when(place.c == 1)
        def _():
            b()
    return run


def gather_ticks(place, g, rows, send, recv):
    n, z, x, y = place.line, place.z, place.x, place.y

    def lines():
        mine = g.at[place.c, z, x, y, rows]
        return [remote(mine, mine, send.at[k - 1], recv.at[k - 1], place.dev(z=place.off(k))) for k in range(1, n)]

    def line_waits():
        for k, cp in enumerate(lines()):
            cp.wait_send()
            got = g.at[place.c, place.off(-k - 1), x, y, rows]
            remote(got, got, send.at[k], recv.at[k], place.dev(z=place.off(1))).wait_recv()

    def parts(core):
        if core == 0:
            return (g.at[0, :, x, y, rows], g.at[0, :, x, :, rows]), (g.at[0, :, x, y, rows], g.at[0, :, x, 1 - y, rows], g.at[0, :, 1 - x, :, rows])
        return (g.at[1, :, x, y, rows], g.at[1, :, :, y, rows]), (g.at[1, :, x, y, rows], g.at[1, :, 1 - x, y, rows], g.at[1, :, :, 1 - y, rows])

    def swap(core, i):
        part = parts(core)[0][i]
        over_y = (core == 0) == (i == 0)
        return remote(part, part, send.at[n - 1 + i], recv.at[n - 1 + i], place.dev(y=1 - y) if over_y else place.dev(x=1 - x))

    def hand(core, i):
        part = parts(core)[1][i]
        return remote(part, part, send.at[n + 1 + i], recv.at[n + 1 + i], place.dev(c=1 - place.c))

    def steps(core):
        def last():
            for i in range(3):
                hand(core, i).wait_send()
                hand(1 - core, i).wait_recv()
        return [lambda: None,
                lambda: (swap(core, 0).start(), hand(core, 0).start()),
                lambda: (both(swap(core, 0)), swap(core, 1).start(), hand(core, 1).start()),
                lambda: (both(swap(core, 1)), hand(core, 2).start()),
                last]
    ticks = [by_core(place, a, b) for a, b in zip(steps(0), steps(1))]

    def first():
        for cp in lines():
            cp.start()

    def second():
        line_waits()
        ticks[1]()
    return [first, second] + ticks[2:]


def add_blocks(pairs):
    for dst, src in pairs:
        dst[...] = (dst[...].astype(F32) + src[...].astype(F32)).astype(dst.dtype)


def scatter_ticks(place, g, rows, cbuf, pbuf, sbuf, zbuf, out, send, recv):
    n, z, x, y, c = place.line, place.z, place.x, place.y, place.c

    def cores():
        return remote(g.at[1 - c, :, :, :, rows], cbuf, send.at[0], recv.at[0], place.dev(c=1 - c))

    def swaps(core):
        over_x, over_y = place.dev(x=1 - x), place.dev(y=1 - y)
        if core == 0:
            return (remote(g.at[0, :, 1 - x, :, rows], pbuf, send.at[1], recv.at[1], over_x),
                    remote(g.at[0, :, x, 1 - y, rows], sbuf, send.at[2], recv.at[2], over_y))
        return (remote(g.at[1, :, :, 1 - y, rows], pbuf, send.at[1], recv.at[1], over_y),
                remote(g.at[1, :, 1 - x, y, rows], sbuf, send.at[2], recv.at[2], over_x))

    def lines():
        return [remote(g.at[c, place.off(k), x, y, rows], zbuf.at[k - 1], send.at[2 + k], recv.at[2 + k], place.dev(z=place.off(k))) for k in range(1, n)]

    def start_cores():
        cores().start()

    def add_cores():
        both(cores())

        def body(t, carry):
            add_blocks([(g.at[c, t // 4, t // 2 % 2, t % 2, rows], cbuf.at[t // 4, t // 2 % 2, t % 2])])
            return carry
        lax.fori_loop(0, 4 * n, body, 0)

    def step1(core):
        def run():
            add_cores()
            swaps(core)[0].start()
        return run

    def step2(core):
        def run():
            both(swaps(core)[0])

            def body(t, carry):
                dst = g.at[0, t // 2, x, t % 2, rows] if core == 0 else g.at[1, t // 2, t % 2, y, rows]
                add_blocks([(dst, pbuf.at[t // 2, t % 2])])
                return carry
            lax.fori_loop(0, 2 * n, body, 0)
            swaps(core)[1].start()
        return run

    def step3(core):
        def run():
            both(swaps(core)[1])

            def body(t, carry):
                add_blocks([(g.at[core, t, x, y, rows], sbuf.at[t])])
                return carry
            lax.fori_loop(0, n, body, 0)
            for cp in lines():
                cp.start()
        return run

    def finish():
        for cp in lines():
            both(cp)
        total = g[c, z, x, y, rows].astype(F32)
        for k in range(n - 1):
            total = total + zbuf[k].astype(F32)
        out[...] = total
    return [start_cores] + [by_core(place, s(0), s(1)) for s in (step1, step2, step3)] + [finish]


def scatter_bufs(line, rows, width, dtype):
    return [pltpu.VMEM(shape + (rows, width), dtype) for shape in ((line, 2, 2), (line, 2), (line,), (line - 1,))]


STEPS = 5


class Ticker:
    def __init__(self, lists):
        depth = max(i for i, _ in lists) + STEPS
        self.rounds = [[(lambda make=make, at=r - i: make()[at]()) for i, make in lists if 0 <= r - i < STEPS] for r in range(depth)]
        self.done = 0

    def upto(self, count):
        while self.done < min(count, len(self.rounds)):
            for t in self.rounds[self.done]:
                t()
            self.done += 1

    def __call__(self):
        self.upto(self.done + 1)

    def finish(self):
        self.upto(len(self.rounds))


def build_tables(gs, layer, tau, y, tab, b1):
    for t in range(32):
        tau[9 * t:9 * t + 9, :] = gs[t % 2, t // 8, t // 4 % 2, t // 2 % 2, 16 * layer:16 * layer + 9, :]
    lane = lax.broadcasted_iota(jnp.int32, (8, 128), 1)

    def run(base, step, width, b):
        first, off = width * b // 128, width * b % 128
        val = tau[pl.ds(base + first, 8, stride=step), :]
        if off:
            val = pltpu.roll(val, 128 - off, 1)
            if off + width > 128:
                more = pltpu.roll(tau[pl.ds(base + first + 1, 8, stride=step), :], 128 - off, 1)
                val = jnp.where(lane < 128 - off, val, more)
        return val
    for b in range(64):
        tb = run(0, 29, TABLE, b)
        cpe = pltpu.roll(run(248, 5, 10, b), 64, 1)
        y[8 * b:8 * b + 8, :] = jnp.where(lane < TABLE, tb, jnp.where((lane >= 64) & (lane < 74), cpe, 0.0))
    r = lax.broadcasted_iota(jnp.int32, (D, D), 0)
    c = lax.broadcasted_iota(jnp.int32, (D, D), 1)
    place = jnp.where(c == 64 * (r % 8) + r // 8, 1.0, 0.0).astype(BF16)
    table = dot(y[...].astype(BF16), place, 0, 0)[:TROWS]
    tap = lax.broadcasted_iota(jnp.int32, (TROWS, D), 0) - TAPS
    head = lax.broadcasted_iota(jnp.int32, (TROWS, D), 1) // 64
    reach = jnp.where(head < 2, 1, jnp.where(head < 5, 2, 3))
    ok = (tap < 0) | (tap >= 49) | ((jnp.abs(tap // 7 - 3) <= reach) & (jnp.abs(tap % 7 - 3) <= reach))
    table = jnp.where(ok, table, 0.0)
    for g in range(4):
        tab[layer, g] = table[:, 128 * g:128 * g + 128]
    b1[layer] = tau[232:248, :]


def build_small(gsum, gb1, y, tau, gsm):
    r = lax.broadcasted_iota(jnp.int32, (D, D), 0)
    c = lax.broadcasted_iota(jnp.int32, (D, D), 1)
    place = jnp.where(c == 64 * (r % 8) + r // 8, 1.0, 0.0).astype(BF16)
    table = full(gsum, slice(None))
    tap = lax.broadcasted_iota(jnp.int32, (TROWS, D), 0) - TAPS
    head = lax.broadcasted_iota(jnp.int32, (TROWS, D), 1) // 64
    reach = jnp.where(head < 2, 1, jnp.where(head < 5, 2, 3))
    ok = (tap < 0) | (tap >= 49) | ((jnp.abs(tap // 7 - 3) <= reach) & (jnp.abs(tap % 7 - 3) <= reach))
    table = jnp.where(ok, table, 0.0)
    table = jnp.concatenate([table, jnp.zeros((128 - TROWS, D), F32)])
    hi = table.astype(BF16)
    mid = (table - hi.astype(F32)).astype(BF16)
    y[...] = dot(place, hi, 1, 1) + dot(place, mid, 1, 1)
    lane = lax.broadcasted_iota(jnp.int32, (8, 128), 1)

    def lay(base, step, width, start):
        for j in range(step):
            out = None
            for b in range(128 * j // width, min(64, -(-128 * (j + 1) // width))):
                first = width * b - 128 * j
                val = y[8 * b:8 * b + 8, :]
                shift = (first - start) % 128
                if shift:
                    val = pltpu.roll(val, shift, 1)
                out = val if out is None else jnp.where(lane >= first, val, out)
            tau[pl.ds(base + j, 8, stride=step), :] = out
    lay(0, 29, TABLE, 0)
    lay(248, 5, 10, CPE)
    for i in range(16):
        tau[232 + i:233 + i, :] = jnp.sum(gb1[:, 128 * i:128 * i + 128], axis=0, keepdims=True)
    for t in range(32):
        gsm[t % 2, t // 8, t // 4 % 2, t // 2 % 2, 0:9, :] = tau[9 * t:9 * t + 9, :]
        gsm[t % 2, t // 8, t // 4 % 2, t // 2 % 2, 9:16, :] = jnp.zeros((7, 128), F32)


def sd(shape, dtype):
    return jax.ShapeDtypeStruct(shape, dtype)


def packed(rows, width=D, dtype=BF16):
    return sd((2, 4, 2, 2, rows, width), dtype)


ANY = pl.BlockSpec(memory_space=pl.ANY)
VM = pl.BlockSpec(memory_space=pltpu.VMEM)
L4 = ((4, RP, 128), F32)
WIDE = ((R, FF), BF16)
LOW = ((R, D), BF16)
INV = ((R, 128), F32)
SUMM = ((2 * NI, 64, 256), BF16)
REL = ((4, R, 128), F32)
PARK = (("q", L4), ("p", L4), ("v", L4), ("rel", REL), ("s", SUMM))
PARK0 = PARK + (("n1", LOW), ("h1", LOW), ("inv1", INV), ("a", LOW), ("n2", LOW), ("h2", LOW), ("inv2", INV), ("g", WIDE), ("slope", WIDE))
GATHERS = ((0, 64), (64, 128), (128, 192))
PIECES = ((0, 48), (48, 64), (64, 128), (128, 192))
SCATTERS = ((0, 80), (80, 144))


def cell_reach():
    cell_no = lax.broadcasted_iota(jnp.int32, (SLOT, 128), 0) - 1
    y = jnp.zeros((SLOT, 128), jnp.int32)
    for k in range(1, GRID):
        y = y + jnp.where(cell_no >= GRID * k, 1, 0)
    return jnp.where(cell_no < 0, -1, jnp.maximum(y, cell_no - GRID * y))


def take_images(src, dst, sz=None):
    reach = cell_reach() if sz is not None else None

    def body(i, c):
        for g in range(4):
            val = src[i, :, 128 * g:128 * g + 128].astype(F32)
            if sz is not None:
                val = jnp.where(reach < sz[pl.ds(i, 1), :], val, 0.0)
            dst[g, pl.ds(i, SLOT, stride=NI), :] = val
        return c
    lax.fori_loop(0, NI, body, 0)


def give_images(src, dst, sz=None):
    reach = cell_reach() if sz is not None else None

    def body(i, c):
        for g in range(4):
            val = src[g, pl.ds(i, SLOT, stride=NI), :]
            if sz is not None:
                val = jnp.where(reach < sz[pl.ds(i, 1), :], val, 0.0)
            dst[i, :, 128 * g:128 * g + 128] = val.astype(dst.dtype)
        return c
    lax.fori_loop(0, NI, body, 0)


class Copies:
    def __init__(self, sems):
        self.sems, self.used, self.open = sems, 0, {}

    def start(self, name, src, dst):
        at = self.used
        self.used += 1
        self.open[name] = lambda: pltpu.make_async_copy(src, dst, self.sems.at[at])
        self.open[name]().start()

    def wait(self, *names):
        for name in names:
            self.open.pop(name)().wait()

    def wait_all(self, prefix):
        for name in [n for n in self.open if n.startswith(prefix)]:
            self.wait(name)


class Idle:
    def __call__(self):
        pass

    def upto(self, count):
        pass

    def finish(self):
        pass


COPIES = 80
ROWS6 = (slice(None),) * 4


def step_kernel(comm, names, *refs):
    r = dict(zip(names, refs))
    cps = Copies(r["copy_sems"])
    sz, W, tab, b1 = r["sz"], r["W"], r["tab"], r["b1"]
    gsum, gb1, gfc, gq, gsm, tau = r["gsum"], r["gb1"], r["gfc"], r["gq"], r["gsm"], r["tau"]
    whbm = (r["w0"], r["w1"])
    n1, h1, inv1, a_low = r["n1"], r["h1"], r["inv1"], r["a"]
    xa, xb, da, dxb = r["xa"], r["xb"], r["da"], r["dxb"]
    pv, pr = r["pv"], r["pr"]
    y = pv.at[pl.ds(3 * PROW, D)]
    zero_padded(pv)
    zero_padded(pr)
    scope = pl.run_scoped

    def vm(*shapes):
        return [pltpu.VMEM(*sh) for sh in shapes]

    def load_piece(layer, i):
        a, b = PIECES[i]
        cps.start(f"W{i}", whbm[layer].at[ROWS6 + (pl.ds(a, b - a),)], W.at[ROWS6 + (pl.ds(a, b - a),)])

    STAGE = pltpu.VMEM((NI, SLOT, D), BF16)

    if comm:
        place = Place(4)
        here = (place.c, place.z, place.x, place.y)
        cps.start("own0", r["shard0"], r["w0"].at[here])
        cps.start("own1", r["shard1"], r["w1"].at[here])
        cps.start("own2", r["small"], r["gs"].at[here])
        greet(place)
        cps.wait("own2")
        send, recv = r["ag_send"], r["ag_recv"]
        tiny = Ticker([(0, lambda: gather_ticks(Place(4), r["gs"], slice(None), send.at[0], recv.at[0]))])
        lists = []
        for layer in range(2):
            for i, (a, b) in enumerate(GATHERS):
                n = 3 * layer + i
                lists.append((n, lambda n=n, layer=layer, a=a, b=b: gather_ticks(Place(4), whbm[layer], pl.ds(a, b - a), send.at[1 + n], recv.at[1 + n])))
        tick = Ticker(lists)
        tiny()
        cps.wait("own0", "own1")
        tick()
        tiny()

        def begin(stage):
            cps.start("images", r["images"], stage)
            cps.wait("images")
            take_images(stage, xa)
        scope(begin, STAGE)
        tiny()
        tick()
        tiny()
        tiny()
        build_tables(r["gs"], 0, tau, y, tab, b1)
        tick()
    else:
        tick = Idle()

        def begin(stage):
            cps.start("images", r["images"], stage)
            cps.wait("images")
            take_images(stage, xa)
        scope(begin, STAGE)

    def forward(layer, xin, x1, keep):
        t = tab.at[layer]
        fwd_conv1(xin, sz, t, x1, pv)
        tick()
        norm_phase(x1, t, 0, 1, n1, h1, inv1)
        if layer == 0:
            if comm:
                build_tables(r["gs"], 1, tau, y, tab, b1)
            tick.upto(5)
            load_piece(0, 0)
            load_piece(0, 1)
            for name in ("n1", "h1", "inv1"):
                cps.start("out0" + name, r[name], r["park0" + name])
        cps.wait("W0")

        def attention(q, p, v, rel, f, s):
            def park(name, ref):
                cps.start(f"park{layer}{name}", ref, r[f"park{layer}{name}"])
            fwd_qkv(h1, W, t, q, p, v)
            if layer == 0:
                tick.upto(8)
                load_piece(1, 0)
            else:
                tick()
            park("q", q)
            park("v", v)
            fwd_softmax(p, sz)
            park("p", p)
            tick()
            fwd_attn(q, p, v, s, f, 0, 16)
            tick()
            fwd_attn(q, p, v, s, f, 16, 16)
            park("s", s)
            tick()
            fwd_conv3(v, q, f, sz, t, rel, pv, 1, 0)
            fwd_conv3(v, q, f, sz, t, rel, pv, 2, 1)
            tick()

            def wide(i, c):
                fwd_conv3(v, q, f, sz, t, rel, pv, 3, i)
                return c
            lax.fori_loop(0, 2, lambda i, c: wide(i + 2, c), 0)
            tick()
            park("rel", rel)
            cps.wait("W1")
            fwd_proj(f, W, t, x1, a_low)
            cps.wait_all(f"park{layer}")
        scope(attention, *vm(L4, L4, L4, REL, L4, SUMM))
        if layer == 0:
            cps.start("out0a", a_low, r["park0a"])

        def mlp(g, slope, n2, h2, inv2, dm):
            norm_phase(x1, t, 2, 3, n2, h2, inv2)
            if layer == 0:
                tick.upto(6)
                load_piece(0, 2)
                tick.upto(7)
                load_piece(0, 3)
            else:
                tick.upto(9)
                load_piece(1, 2)
                tick.finish()
                load_piece(1, 3)
            cps.wait("W2")
            fwd_fc1(h2, W, b1.at[layer], g, slope, 0, 2)
            tick()
            fwd_fc1(h2, W, b1.at[layer], g, slope, 2, 2)
            if layer == 0:
                for name, ref in (("g", g), ("slope", slope), ("n2", n2), ("h2", h2), ("inv2", inv2)):
                    cps.start("out0" + name, ref, r["park0" + name])
            cps.wait("W3")
            fwd_fc2(g, W, t, x1)
            if layer == 0:
                tick()
                load_piece(1, 1)
                cps.wait_all("out0")
            else:
                keep(g, slope, n2, h2, inv2, dm)
        scope(mlp, *vm(WIDE, WIDE, LOW, LOW, INV, LOW))

    def first_half(layer, dx, da, g, slope, n2, h2, inv2, dm, tick):
        t = tab.at[layer]
        gsum[...] = jnp.zeros_like(gsum)
        bwd_cast_sum(dx, dm, gsum, 7)
        if layer == 0:
            cps.wait("in0slope", "W3")
        bwd_du(dm, W, slope, gb1)
        tick()
        if layer == 0:
            cps.wait("in0g")
        wgrad2(g, dm, gfc, 80)
        tick()
        if layer == 0:
            cps.wait("in0h2", "W2")
        wgrad(h2, slope, gfc, 16, 4)
        tick()
        mm_nt(slope, slice(None), W, 4, 4, da)
        if layer == 0:
            cps.wait("in0n2", "in0inv2", "in0a", "W1")
        norm_back_phase(da, n2, inv2, t, 2, dx, dm, gsum, 2, 3, 6)
        tick()
        wgrad(a_low, dm, gfc, 0, 1)
        mm_nt(dm, slice(None), W, 3, 1, da)
        zero_tail(da)
        tick()

    def second_half(layer, xin, dx, da, dv, tick, mid, end):
        t = tab.at[layer]

        def run(q, p, v, rel, dq, dk, s, dj):
            for name, ref in (("q", q), ("p", p), ("v", v), ("s", s), ("rel", rel)):
                cps.start(f"in{layer}" + name, r[f"park{layer}{name}"], ref)
            tick()
            cps.wait(*(f"in{layer}" + n for n in ("q", "p", "v", "s")))
            bwd_attn1(q, p, v, s, da, dq, dv, dk, 0, 16)
            tick()
            bwd_attn1(q, p, v, s, da, dq, dv, dk, 16, 16)
            tick()
            cps.wait(f"in{layer}rel")
            bwd_mix(q, p, v, rel, da, dq, dv, dk, sz, t, gsum, pv, pr, 1, 0)
            tick()
            bwd_mix(q, p, v, rel, da, dq, dv, dk, sz, t, gsum, pv, pr, 2, 1)
            tick()

            def wide(i, c):
                bwd_mix(q, p, v, rel, da, dq, dv, dk, sz, t, gsum, pv, pr, 3, i)
                return c
            lax.fori_loop(0, 2, lambda i, c: wide(i + 2, c), 0)
            tick()
            bwd_cast(dq, dk, dv, dj)
            if layer == 0:
                cps.wait("W0", "in0h1")
            wgrad(h1, dj, gq, 0, 3)
            mid()
            mm_nt(dj, slice(0, 1536), W, 0, 3, dq)
            if layer == 0:
                cps.wait("in0n1", "in0inv1")
            norm_back_phase(dq, n1, inv1, t, 0, dx, None, gsum, 0, 1, None)
        scope(run, *vm(L4, L4, L4, REL, L4, L4, SUMM, ((R, 3 * D), BF16)))
        end()
        bwd_conv1(xin, dx, da, sz, t, gsum, pv, pr)
        build_small(gsum, gb1, y, tau, gsm)

    def scatter(n, g, rows, out, which):
        bufs = r["bufs"][4 * which:4 * which + 4]
        return lambda: scatter_ticks(Place(4), g, rows, *bufs, out, r["rs_send"].at[n], r["rs_recv"].at[n])

    def fc_scatter(layer):
        out = r[f"sfc{layer}"]
        return Ticker([(i, scatter(4 * layer + i, gfc, pl.ds(a, b - a), out.at[pl.ds(a, b - a)], i)) for i, (a, b) in enumerate(SCATTERS)])

    def q_scatter(layer):
        return Ticker([(0, scatter(4 * layer + 2, gq, slice(None), r[f"sq{layer}"], 2))])

    def s_scatter(layer):
        return Ticker([(0, scatter(4 * layer + 3, gsm, slice(None), r[f"ss{layer}"], 3))])

    forward(0, xa, xb, None)

    def top(g, slope, n2, h2, inv2, dm):
        def emit(stage, stage2):
            cps.start("cot", r["cotangent"], stage)
            give_images(xa, stage2, sz)
            cps.start("out", stage2, r["output"])
            cps.wait("cot")
            take_images(stage, dxb, sz)
            cps.wait("out")
        scope(emit, STAGE, STAGE)
        first_half(1, dxb, da, g, slope, n2, h2, inv2, dm, Idle())
    forward(1, xb, xa, top)

    for i in (1, 2, 3):
        load_piece(0, i)
    cps.start("in0a", r["park0a"], a_low)
    if comm:
        rs = fc_scatter(1)
        rs()
    else:
        rs = Idle()
        cps.start("gfc1", gfc, r["gfc1"])

    def mid1():
        rs()

    def end1():
        rs()
        load_piece(0, 0)
        cps.start("in0h1", r["park0h1"], h1)
        cps.start("in0n1", r["park0n1"], n1)
        cps.start("in0inv1", r["park0inv1"], inv1)
    second_half(1, xb, dxb, da, xa, rs, mid1, end1)
    rs.finish()

    if comm:
        class Pair(Idle):
            def __init__(self):
                self.a, self.b = q_scatter(1), s_scatter(1)

            def __call__(self):
                self.a()
                self.b()

            def finish(self):
                self.a.finish()
                self.b.finish()
        rs2 = Pair()
        rs2()
    else:
        rs2 = Idle()
        cps.wait("gfc1")
        cps.start("gq1", gq, r["gq1"])
        cps.start("gsm1", gsm, r["gsm1"])
        cps.wait("gq1", "gsm1")

    def bottom(g, slope, n2, h2, inv2, dm):
        for name, ref in (("slope", slope), ("g", g), ("h2", h2), ("n2", n2), ("inv2", inv2)):
            cps.start("in0" + name, r["park0" + name], ref)
        first_half(0, da, dxb, g, slope, n2, h2, inv2, dm, rs2)
    scope(bottom, *vm(WIDE, WIDE, LOW, LOW, INV, LOW))
    rs2.finish()
    if comm:
        place = Place(4)
        far = [place.dev(z=place.off(k)) for k in range(1, 4)]
        near = [place.dev(x=1 - place.x), place.dev(y=1 - place.y), place.dev(c=1 - place.c)]
        for who in far + near:
            pl.semaphore_signal(r["credit"], inc=1, device_id=who, device_id_type=MESH)
        pl.semaphore_wait(r["credit"], 6)
        rs = fc_scatter(0)
        rsq = q_scatter(0)
        rss = s_scatter(0)
        rs()
    else:
        rs = rsq = rss = Idle()
        cps.start("gfc0", gfc, r["gfc0"])

    def mid0():
        rs.finish()
        rsq()

    def end0():
        rsq()

        def again(stage):
            cps.start("again", r["images"], stage)
            cps.wait("again")
            take_images(stage, xb)
        scope(again, STAGE)
        rsq()
    second_half(0, xb, da, dxb, xa, rs, mid0, end0)
    if comm:
        rss()
        rsq()
        rss()
    else:
        cps.start("gq0", gq, r["gq0"])
        cps.start("gsm0", gsm, r["gsm0"])

    def last(stage3):
        give_images(dxb, stage3)
        cps.start("dx", stage3, r["grad_images"])
        rss()
        rsq.finish()
        rss.finish()
        if not comm:
            cps.wait("gfc0", "gq0", "gsm0")
        cps.wait("dx")
    scope(last, pltpu.VMEM((NI, SLOT, D), F32))


def step(comm, images, cotangent, sz, *more):
    vmem = pltpu.VMEM
    if comm:
        inputs = ["images", "cotangent", "sz", "shard0", "shard1", "small"]
        in_specs = [ANY, ANY] + [VM] * 4
    else:
        inputs = ["images", "cotangent", "sz", "w0", "w1", "tab", "b1"]
        in_specs = [ANY, ANY, VM, ANY, ANY, VM, VM]
    outs = [("output", sd((NI, SLOT, D), BF16), ANY), ("grad_images", sd((NI, SLOT, D), F32), ANY)]
    shares = []
    for layer in (0, 1):
        if comm:
            shares += [(f"sfc{layer}", sd((144, D), F32), VM), (f"sq{layer}", sd((48, D), F32), VM), (f"ss{layer}", sd((16, 128), F32), VM)]
        else:
            shares += [(f"gfc{layer}", packed(144), ANY), (f"gq{layer}", packed(48), ANY), (f"gsm{layer}", packed(16, 128, F32), ANY)]
    outs += shares
    outs += [(f"park0{n}", sd(*sh), ANY) for n, sh in PARK0] + [(f"park1{n}", sd(*sh), ANY) for n, sh in PARK]
    if comm:
        outs += [("w0", packed(WROWS), ANY), ("w1", packed(WROWS), ANY)]
    scratch = [("W", vmem((2, 4, 2, 2, WROWS, D), BF16)), ("gfc", vmem((2, 4, 2, 2, 144, D), BF16)), ("gq", vmem((2, 4, 2, 2, 48, D), BF16)),
               ("gsm", vmem((2, 4, 2, 2, 16, 128), F32)), ("gsum", vmem((4, TROWS, 128), F32)), ("gb1", vmem((8, FF), F32)),
               ("tau", vmem((288, 128), F32)), ("pv", vmem(PADDED, F32)), ("pr", vmem(PADDED, F32)), ("n1", vmem(*LOW)), ("h1", vmem(*LOW)), ("inv1", vmem(*INV)), ("a", vmem(*LOW))]
    scratch += [(n, vmem(*L4)) for n in ("xa", "xb", "da", "dxb")] + [("copy_sems", pltpu.SemaphoreType.DMA((COPIES,)))]
    bufs = []
    if comm:
        sems = pltpu.SemaphoreType.DMA
        scratch += [("tab", vmem((2, 4, TROWS, 128), F32)), ("b1", vmem((2, 16, 128), F32)), ("gs", vmem((2, 4, 2, 2, 32, 128), F32)),
                    ("ag_send", sems((7, 8))), ("ag_recv", sems((7, 8))), ("rs_send", sems((8, 8))), ("rs_recv", sems((8, 8))), ("credit", pltpu.SemaphoreType.REGULAR)]
        for rows, width, dt in ((80, D, BF16), (64, D, BF16), (48, D, BF16), (16, 128, F32)):
            bufs += scatter_bufs(4, rows, width, dt)
    names = inputs + [n for n, _, _ in outs] + [n for n, _ in scratch]

    def kernel(*refs):
        count = len(names)
        r = list(refs[:count])
        step_kernel(comm, names + ["bufs"], *r, refs[count:])
    params = dict(vmem_limit_bytes=67043328)
    if comm:
        params.update(collective_id=0, has_side_effects=True)
    got = pl.pallas_call(
        kernel, out_shape=[o for _, o, _ in outs], in_specs=in_specs, out_specs=[sp for _, _, sp in outs],
        scratch_shapes=[sc for _, sc in scratch] + bufs, compiler_params=pltpu.CompilerParams(**params), name="step",
    )(images, cotangent, sz, *more)
    return got[:2 + len(shares)]


def window_mask():
    channel = lax.broadcasted_iota(jnp.int32, (49, D), 1)
    tap = lax.broadcasted_iota(jnp.int32, (49, D), 0)
    head = channel // (D // HEADS)
    reach = jnp.where(head < 2, 1, jnp.where(head < 5, 2, 3))
    return ((jnp.abs(tap // 7 - 3) <= reach) & (jnp.abs(tap % 7 - 3) <= reach)).astype(F32)


def blocks_of(flat, rows, cols):
    return flat.reshape(rows, cols // D, D).transpose(1, 0, 2).reshape(rows * cols // D, D)


def pack(qkv, proj, fc1, fc2, n):
    per = D // n
    return jnp.concatenate([blocks_of(qkv, per, 3 * D), proj.reshape(per, D), blocks_of(fc1, per, FF), fc2.reshape(FF // n, D)])


def tables(small):
    small = small.astype(F32)
    end = TABLE * D
    tb = small[:end].reshape(D, TABLE).T
    cpe = small[end + FF:].reshape(D, 10).T
    tab = jnp.concatenate([tb[:9], tb[9:] * window_mask(), jnp.zeros((CPE - TABLE, D), F32), cpe, jnp.zeros((TROWS - CPE - 10, D), F32)])
    return tab.reshape(TROWS, 4, 128).transpose(1, 0, 2), small[end:end + FF].reshape(16, 128)


def whole_weights(mine, small, n):
    per = D // n
    full = lax.all_gather(mine[None], AXES, axis=0, tiled=True)
    vec = lax.all_gather(small, AXES, axis=0, tiled=True)
    parts = [full[:, j * per:(j + 1) * per].reshape(32, D // 32, D) for j in range(8)] + [full[:, 8 * per:].reshape(32, FF // 32, D)]
    w = jnp.concatenate(parts, axis=1).reshape(4, 2, 2, 2, WROWS, D).transpose(3, 0, 1, 2, 4, 5)
    return w, *tables(vec)


def share_by_xla(gfc, gq, gsm, n):
    per = D // n

    def rows(a):
        return a.transpose(1, 2, 3, 0, 4, 5).reshape((32,) + a.shape[4:])
    gq, gfc, gsm = rows(gq), rows(gfc), rows(gsm)
    every = jnp.concatenate([gq, gfc[:, :80]], axis=1)
    parts = [every[:, 16 * j:16 * j + 16].reshape(n, per, D) for j in range(8)] + [gfc[:, 80:].reshape(n, FF // n, D)]
    vec = gsm[:, :9].reshape(n, -1)
    width = vec.shape[1]
    parts.append(jnp.pad(vec, ((0, 0), (0, -width % D))).reshape(n, -1, D).astype(BF16))
    share = lax.psum_scatter(jnp.concatenate(parts, axis=1), AXES, scatter_dimension=0, tiled=True)[0].astype(F32)
    mats = split_shares(share[:8 * per + FF // n], per)
    return (*mats, share[8 * per + FF // n:].reshape(-1)[:width])


def split_shares(share, per):
    def cols(first, count):
        return share[first * per:(first + count) * per].reshape(count, per, D).transpose(1, 0, 2).reshape(-1)
    return cols(0, 3), cols(3, 1), cols(4, 4), share[8 * per:].reshape(-1)


def shards(n, images, grid_sizes, qkv, proj, fc1, fc2, small, cotangent):
    layers = qkv.shape[0]
    mine = [pack(qkv[l], proj[l], fc1[l], fc2[l], n) for l in range(layers)]
    sz = jnp.broadcast_to(grid_sizes[:, None], (NI, 128))
    if n == 32:
        flat = jnp.pad(small.astype(F32).reshape(2, 9, 128), ((0, 0), (0, 7), (0, 0))).reshape(32, 128)
        output, dx, *got = step(True, images, cotangent, sz, mine[0], mine[1], flat)
        shares = [(*split_shares(jnp.concatenate([q, fc]), D // n), s[:9].reshape(-1)) for fc, q, s in (got[:3], got[3:])]
    else:
        held = [whole_weights(mine[l], small[l], n) for l in range(layers)]
        output, dx, *got = step(False, images, cotangent, sz, held[0][0], held[1][0], jnp.stack([held[0][1], held[1][1]]), jnp.stack([held[0][2], held[1][2]]))
        shares = [share_by_xla(*got[:3], n), share_by_xla(*got[3:], n)]
    grads = [jnp.stack([shares[l][i] for l in range(layers)]) for i in range(5)]
    return (output, dx, *grads)


def solution(mesh):
    n = mesh.shape["wide"] * mesh.shape["narrow"]
    from jax.sharding import PartitionSpec as P
    rows, flat = P(AXES, None, None), P(None, AXES)
    return jax.shard_map(
        functools.partial(shards, n), mesh=mesh,
        in_specs=(rows, P(AXES), flat, flat, flat, flat, flat, rows),
        out_specs=(rows, rows, flat, flat, flat, flat, flat),
        check_vma=False)
```

time: 835 us -> 401 us (0.48)
  waiting for transfers between devices: 420 us -> 0 us
  Pallas kernels: 312 us -> 366 us
  local copies, waits for them, and re-layouts: 56.1 us -> 23.5 us
  other arithmetic: 25.2 us -> 6.04 us
  between operations: 15.1 us -> 1.37 us
    reduce_scatter x2 -> x0, waiting for transfers between devices: 278 us -> none  [shards(): lax.psum_scatter(g, AXES, scatter_dimension=0, tiled=True)[0].astype(F32)]
    all_gather x2 -> x0, waiting for transfers between devices: 142 us -> none  [shards(): full = lax.all_gather(packed[l][None], AXES, axis=0, tiled=True)]
    pallas_call x6 -> x1, Pallas kernels: 312 us -> 366 us  [step(): pl.pallas_call(kernel, out_shape=[o for _, o, _ in outs], in_specs=in_spe...]
    slice x31 -> x4, local copies, waits for them, and re-layouts: 26.6 us -> 6.05 us  [shards(): mine = [pack(qkv[l], proj[l], fc1[l], fc2[l], n) for l in range(layers)]]
    unnamed x84 -> x27, local copies, waits for them, and re-layouts: 19.3 us -> 12.2 us
  transfers between devices with their start and end apart: 4 -> 0, of which waited for: 4 -> 0; matrix products, arithmetic and copies ran while one was open for 2% -> 0% of each run, Pallas kernels for 0% -> 0%
where the time goes in v4:
time: 401 us; the launch traced here: 397 us
  Pallas kernels  366 us (91%)
  local copies, waits for them, and re-layouts  23.5 us (6%)
  other arithmetic  6.04 us (2%)
    pallas_call x1, Pallas kernels, step(): pl.pallas_call(kernel, out_shape=[o for _, o, _ in outs], in_specs=in_spe...  366 us
    unnamed x27, local copies, waits for them, and re-layouts  12.2 us

profile of v4, /device:TPU:0, one launch (start us, length us, event | category | flops | bytes accessed | tf_op | source)
XLA Modules:
  0.0 397.0 jit_solution(18414108114513724651)
XLA Ops:
  0.6 1.4 broadcast_in_dim.2.refs_2_
  2.1 0.7 reshape.52
  2.8 0.6 bitcast_convert_fusion.refs_5_
  3.4 1.0 slice_reduce_fusion.6
  4.5 1.5 slice_reduce_fusion.4
  6.1 1.8 slice_reduce_fusion.1
  8.0 1.7 slice_reduce_fusion
  9.8 0.7 pad_maximum_fusion.3.refs_4_
  10.6 0.7 pad_maximum_fusion.2.refs_3_
  11.3 1.8 copy.31.refs_0_
  13.1 1.8 copy.32.refs_1_
  14.9 366.1 %step.1 = (bf16[16,82,512]{2,1,0:T(8,128)(2,1)}, f32[16,82,512]{2,1,0:T(8,128)}, f32[144,512]{1,0:T(8,128)}, f32[48,512]{1,0:T(8,128)}, f32[16,128]{1,0:T(8,128)...) custom-call(bf16[16,82,512]{2,1,0:T(8,128)(2,1)} %copy.31.refs_0_, ...), custom_call_target="tpu_custom_call" | custom-call | tf_op jit(solution)/shard_map/step/pallas_call | solution.py:1260
  381.1 2.9 copy.37
  384.1 0.6 pad_maximum_fusion.6
  384.7 0.6 slice_bitcast_fusion.2
  385.4 0.1 copy.42
  385.5 0.1 copy.36
  385.6 0.2 stack_reshape.27
  385.8 0.8 copy.40
  386.6 0.8 copy.39
  387.4 0.7 pad_maximum_fusion.5
  388.1 0.1 copy.35
  388.2 0.2 stack_reshape.26
  388.3 0.9 pad_maximum_fusion
  389.3 0.1 copy.41
  389.4 0.9 pad_maximum_fusion.1
  390.4 1.0 copy.50
  391.3 0.1 stack_reshape.24
  391.5 1.0 copy.49
  392.4 0.1 stack_reshape.25
  392.6 0.9 pad_maximum_fusion.4
  393.4 3.1 copy.38
  (31 shorter events, 0.4 us)
Async XLA Ops:
  0.6 10.6 %copy-start.1 = (bf16[16,82,512]{2,0,1:T(8,128)(2,1)S(1)}, bf16[16,82,512]{2,0,1:T(8,128)(2,1)}, u32[]{:S(2)}) copy-start(bf16[16,82,512]{2,0,1:T(8,128)(2,1)} %param.8) | copy-start | bytes 4030468
  6.1 7.0 %copy-start.2 = (bf16[16,82,512]{2,0,1:T(8,128)(2,1)S(1)}, bf16[16,82,512]{2,0,1:T(8,128)(2,1)}, u32[]{:S(2)}) copy-start(bf16[16,82,512]{2,0,1:T(8,128)(2,1)} %param.15) | copy-start | bytes 4030468
  381.1 2.9 copy-start.5
  381.1 2.9 copy-start.6
  381.1 3.6 copy-start.3
  381.1 3.6 copy-start.4
  384.7 8.7 %copy-start = (f32[16,82,512]{2,1,0:T(8,128)S(1)}, f32[16,82,512]{2,1,0:T(8,128)}, u32[]{:S(2)}) copy-start(f32[16,82,512]{2,1,0:T(8,128)} %get-tuple-element.31) | copy-start | bytes 8060932

commit v5 on v4

--- a/solution.py
+++ b/solution.py
@@ -118,7 +118,7 @@
                             acc[k] = acc[k] + up[x] * line[x + b]
             return tuple(acc)
         zero = jnp.zeros((8, 128), F32)
-        sums = lax.fori_loop(0, 2 * GRID, body, (zero,) * (len(part) * len(span)))
+        sums = lax.fori_loop(0, 2 * GRID, body, (zero,) * (len(part) * len(span)), unroll=2)
         for i, a in enumerate(part):
             for j, b in enumerate(span):
                 emit(a, b, sums[i * len(span) + j])
@@ -213,9 +213,17 @@
 
 def halves(fn):
     def body(i, c):
-        fn(pl.ds(pl.multiple_of(i * (R // 2), 16), R // 2))
-        return c
-    lax.fori_loop(0, 2, body, 0)
+        fn(pl.ds(pl.multiple_of(i // 2 * (R // 2), 16), R // 2), i % 2)
+        return c
+    lax.fori_loop(0, 4, body, 0)
+
+
+def cols256(j):
+    return pl.ds(pl.multiple_of(j * 256, 256), 256)
+
+
+def both_lanes(ref, at, j):
+    return jnp.concatenate([ref[2 * j, at, :], ref[2 * j + 1, at, :]], axis=1)
 
 
 def zero_tail(ref):
@@ -223,12 +231,11 @@
 
 
 def fwd_qkv(low, w, tab, q, k, v):
-    def fn(at):
+    def fn(at, j):
         h = low[at, :]
         for b, (ref, bias) in enumerate(((q, 4), (k, None), (v, 5))):
-            for j in range(2):
-                val = dot(h, weight(w, b, 0, D, slice(256 * j, 256 * j + 256)), 1, 0)
-                put2(ref, at, j, val if bias is None else val + row(tab, bias, j))
+            val = dot(h, weight(w, b, 0, D, cols256(j)), 1, 0)
+            put2(ref, at, j, val if bias is None else val + row(tab, bias, j))
     halves(fn)
     for ref in (q, k, v):
         zero_tail(ref)
@@ -287,7 +294,7 @@
         ref[2 * half + j, pl.ds(i, PADS, stride=NI), :] = val[:, 128 * j:128 * j + 128]
 
 
-def fwd_attn(q, p, v, s, f, first, count):
+def fwd_attn(q, p, v, s, f):
     def body(t, c):
         i, half = t // 2, t % 2
         pi = img_load(p, i, half).astype(BF16)
@@ -297,7 +304,7 @@
         qi = img_load(q, i, half).astype(BF16)
         img_store(f, i, half, dot(qi, summ, 1, 0) * 0.125)
         return c
-    lax.fori_loop(0, count, lambda t, c: body(t + first, c), 0, unroll=8)
+    lax.fori_loop(0, 2 * NI, body, 0, unroll=4)
 
 
 def fwd_conv3(v, q, f, sz, tab, rel, pv, radius, lg):
@@ -319,12 +326,12 @@
 
 
 def fwd_proj(att, w, tab, x1, a_low):
-    def fn(at):
-        low = full(att, at).astype(BF16)
-        a_low[at, :] = low
-        for j in range(2):
-            res = jnp.concatenate([x1[2 * j, at, :], x1[2 * j + 1, at, :]], axis=1)
-            put2(x1, at, j, res + dot(low, weight(w, 3, 0, D, slice(256 * j, 256 * j + 256)), 1, 0) + row(tab, 6, j))
+    def low(at):
+        a_low[at, :] = full(att, at).astype(BF16)
+    by_tiles(low)
+
+    def fn(at, j):
+        put2(x1, at, j, both_lanes(x1, at, j) + dot(a_low[at, :], weight(w, 3, 0, D, cols256(j)), 1, 0) + row(tab, 6, j))
     halves(fn)
 
 
@@ -336,7 +343,7 @@
     return jnp.where(u >= 0, 1.0 - tail, tail), e
 
 
-def fwd_fc1(low, w, b1, g, slope, first, count):
+def fwd_fc1(low, w, b1, g, slope):
     def body(j, c):
         cols = pl.ds(pl.multiple_of(j * 512, 512), 512)
         bias = jnp.concatenate([b1[pl.ds(4 * j + i, 1), :] for i in range(4)], axis=1)
@@ -345,15 +352,13 @@
         g[:, cols] = (u * cdf).astype(BF16)
         slope[:, cols] = (cdf + u * e * 0.3989422804014327).astype(BF16)
         return c
-    lax.fori_loop(0, count, lambda j, c: body(j + first, c), 0)
+    lax.fori_loop(0, 4, body, 0)
 
 
 def fwd_fc2(g, w, tab, x1):
-    def fn(at):
-        for j in range(2):
-            cols = slice(256 * j, 256 * j + 256)
-            res = jnp.concatenate([x1[2 * j, at, :], x1[2 * j + 1, at, :]], axis=1)
-            put2(x1, at, j, res + dot(g[at, :], jnp.concatenate([weight2(w, c, cols) for c in range(4)], axis=0), 1, 0) + row(tab, 7, j))
+    def fn(at, j):
+        wide = jnp.concatenate([weight2(w, c, cols256(j)) for c in range(4)], axis=0)
+        put2(x1, at, j, both_lanes(x1, at, j) + dot(g[at, :], wide, 1, 0) + row(tab, 7, j))
     halves(fn)
 
 
@@ -411,28 +416,35 @@
 
 
 def mm_nt(a, cols, g, first, blocks, out):
-    def fn(at):
-        for j in range(2):
-            w = jnp.concatenate([weight(g, first + b, 256 * j, 256, slice(None)) for b in range(blocks)], axis=1)
-            put2(out, at, j, dot(a[at, cols], w, 1, 1))
+    def fn(at, j):
+        def rows(b):
+            here = slice(16 * b, 16 * b + 16)
+            return jnp.concatenate([g[i % 2, 2 * j + i // 8, i // 4 % 2, i // 2 % 2, here, :] for i in range(16)], axis=0)
+        w = jnp.concatenate([rows(first + b) for b in range(blocks)], axis=1)
+        put2(out, at, j, dot(a[at, cols], w, 1, 1))
     halves(fn)
 
 
 def wgrad(left, right, gr, first, blocks):
-    for j in range(blocks):
-        tile = dot(left[...], right[:, 512 * j:512 * j + 512], 0, 0).astype(BF16)
+    def body(j, c):
+        tile = dot(left[...], right[:, pl.ds(pl.multiple_of(512 * j, 512), 512)], 0, 0).astype(BF16)
+        at = pl.ds(pl.multiple_of(first + 16 * j, 16), 16)
         for t in range(32):
-            gr[t % 2, t // 8, t // 4 % 2, t // 2 % 2, first + 16 * j:first + 16 * j + 16, :] = tile[16 * t:16 * t + 16]
+            gr[t % 2, t // 8, t // 4 % 2, t // 2 % 2, at, :] = tile[16 * t:16 * t + 16]
+        return c
+    lax.fori_loop(0, blocks, body, 0)
 
 
 def wgrad2(left, right, gr, first):
-    for j in range(4):
-        tile = dot(left[:, 512 * j:512 * j + 512], right[...], 0, 0).astype(BF16)
+    def body(j, c):
+        tile = dot(left[:, pl.ds(pl.multiple_of(512 * j, 512), 512)], right[...], 0, 0).astype(BF16)
         for i in range(8):
             gr[i % 2, j, i // 4, i // 2 % 2, first:first + 64, :] = tile[64 * i:64 * i + 64]
-
-
-def bwd_attn1(q, p, v, s, da, dq, dv, dk, first, count):
+        return c
+    lax.fori_loop(0, 4, body, 0)
+
+
+def bwd_attn1(q, p, v, s, da, dq, dv, dk):
     def body(t, c):
         i, half = t // 2, t % 2
         df = (img_load(da, i, half) * 0.125).astype(BF16)
@@ -446,7 +458,7 @@
         vi = img_load(v, i, half).astype(BF16)
         img_store(dk, i, half, dot(vi, dsum, 1, 1))
         return c
-    lax.fori_loop(0, count, lambda t, c: body(t + first, c), 0, unroll=8)
+    lax.fori_loop(0, 2 * NI, body, 0, unroll=4)
 
 
 def bwd_mix(q, p, v, rel, da, dq, dv, dk, sz, tab, gsum, pv, pr, radius, lg):
@@ -812,43 +824,71 @@
 REL = ((4, R, 128), F32)
 PARK = (("q", L4), ("p", L4), ("v", L4), ("rel", REL), ("s", SUMM))
 PARK0 = PARK + (("n1", LOW), ("h1", LOW), ("inv1", INV), ("a", LOW), ("n2", LOW), ("h2", LOW), ("inv2", INV), ("g", WIDE), ("slope", WIDE))
-GATHERS = ((0, 64), (64, 128), (128, 192))
+GATHERS = ((0, 0, 16, 0), (0, 16, 32, 1), (0, 32, 48, 2), (0, 48, 128, 4), (0, 128, 192, 6), (1, 0, 64, 8), (1, 64, 128, 10), (1, 128, 192, 12))
 PIECES = ((0, 48), (48, 64), (64, 128), (128, 192))
 SCATTERS = ((0, 80), (80, 144))
 
 
-def cell_reach():
-    cell_no = lax.broadcasted_iota(jnp.int32, (SLOT, 128), 0) - 1
-    y = jnp.zeros((SLOT, 128), jnp.int32)
-    for k in range(1, GRID):
-        y = y + jnp.where(cell_no >= GRID * k, 1, 0)
-    return jnp.where(cell_no < 0, -1, jnp.maximum(y, cell_no - GRID * y))
-
-
-def take_images(src, dst, sz=None):
-    reach = cell_reach() if sz is not None else None
+def take_rows(src, dst):
+    def fn(at):
+        spread(dst, at, src[at, :].astype(F32))
+    by_tiles(fn)
+
+
+def give_rows(src, dst):
+    def fn(at):
+        dst[at, :] = full(src, at).astype(dst.dtype)
+    by_tiles(fn)
+
+
+def split_rows(flat, packs):
+    def row(name, at, first, c):
+        val = flat[name][:, pl.ds(pl.multiple_of(at * 512, 512), 512)].astype(F32)
+        for layer in range(2):
+            packs[layer][pl.ds(first, 1), :] = val[layer:layer + 1, :]
+        return c
+
+    def narrow(i, c):
+        for j in range(3):
+            row("qkv", 3 * i + j, 16 * j + i, c)
+        row("proj", i, 48 + i, c)
+        for j in range(4):
+            row("fc1", 4 * i + j, 64 + 16 * j + i, c)
+            row("fc2", 4 * i + j, 128 + 4 * i + j, c)
+        return c
+    lax.fori_loop(0, 16, narrow, 0)
+
+
+def join_rows(layer, outs, fc, q):
+    def put(name, at, val):
+        outs[name][layer:layer + 1, pl.ds(pl.multiple_of(at * 512, 512), 512)] = val
 
     def body(i, c):
-        for g in range(4):
-            val = src[i, :, 128 * g:128 * g + 128].astype(F32)
-            if sz is not None:
-                val = jnp.where(reach < sz[pl.ds(i, 1), :], val, 0.0)
-            dst[g, pl.ds(i, SLOT, stride=NI), :] = val
-        return c
-    lax.fori_loop(0, NI, body, 0)
-
-
-def give_images(src, dst, sz=None):
-    reach = cell_reach() if sz is not None else None
-
-    def body(i, c):
-        for g in range(4):
-            val = src[g, pl.ds(i, SLOT, stride=NI), :]
-            if sz is not None:
-                val = jnp.where(reach < sz[pl.ds(i, 1), :], val, 0.0)
-            dst[i, :, 128 * g:128 * g + 128] = val.astype(dst.dtype)
-        return c
-    lax.fori_loop(0, NI, body, 0)
+        if q is not None:
+            for j in range(3):
+                put("qkv", 3 * i + j, q[pl.ds(16 * j + i, 1), :])
+        if fc is not None:
+            put("proj", i, fc[pl.ds(i, 1), :])
+            for j in range(4):
+                put("fc1", 4 * i + j, fc[pl.ds(16 + 16 * j + i, 1), :])
+                put("fc2", 4 * i + j, fc[pl.ds(80 + 4 * i + j, 1), :])
+        return c
+    lax.fori_loop(0, 16, body, 0)
+
+
+FLAT = (("qkv", 24576), ("proj", 8192), ("fc1", 32768), ("fc2", 32768), ("small", 1152))
+
+
+def mask_rows(ref, sz):
+    def body(t, c):
+        lg, y = t // GRID, t % GRID
+        for ig in range(2):
+            size = sz[8 * ig:8 * ig + 8, :]
+            for x in range(GRID):
+                at = at_cell(y, x, ig)
+                ref[lg, at, :] = jnp.where(size > jnp.maximum(y, x), ref[lg, at, :], 0.0)
+        return c
+    lax.fori_loop(0, 4 * GRID, body, 0)
 
 
 class Copies:
@@ -887,7 +927,7 @@
 
 def step_kernel(comm, names, *refs):
     r = dict(zip(names, refs))
-    cps = Copies(r["copy_sems"])
+    cps = Copies(r["cs"])
     sz, W, tab, b1 = r["sz"], r["W"], r["tab"], r["b1"]
     gsum, gb1, gfc, gq, gsm, tau = r["gsum"], r["gb1"], r["gfc"], r["gq"], r["gsm"], r["tau"]
     whbm = (r["w0"], r["w1"])
@@ -906,37 +946,53 @@
         a, b = PIECES[i]
         cps.start(f"W{i}", whbm[layer].at[ROWS6 + (pl.ds(a, b - a),)], W.at[ROWS6 + (pl.ds(a, b - a),)])
 
-    STAGE = pltpu.VMEM((NI, SLOT, D), BF16)
+    STAGE = pltpu.VMEM((R, D), BF16)
 
     if comm:
         place = Place(4)
         here = (place.c, place.z, place.x, place.y)
-        cps.start("own0", r["shard0"], r["w0"].at[here])
-        cps.start("own1", r["shard1"], r["w1"].at[here])
-        cps.start("own2", r["small"], r["gs"].at[here])
+        for name, _ in FLAT:
+            cps.start("flat" + name, r[name], r["st_" + name])
+        for i in range(NI):
+            sz[i:i + 1, :] = jnp.full((1, 128), r["sizes"][i], jnp.int32)
+        cps.wait("flatsmall")
+        r["osm"][...] = jnp.zeros((32, 128), F32)
+        for i in range(9):
+            val = r["st_small"][:, 128 * i:128 * i + 128].astype(F32)
+            for layer in range(2):
+                r["osm"][16 * layer + i:16 * layer + i + 1, :] = val[layer:layer + 1, :]
+        cps.start("own2", r["osm"], r["gs"].at[here])
         greet(place)
-        cps.wait("own2")
-        send, recv = r["ag_send"], r["ag_recv"]
+        send, recv = r["as"], r["ar"]
         tiny = Ticker([(0, lambda: gather_ticks(Place(4), r["gs"], slice(None), send.at[0], recv.at[0]))])
         lists = []
-        for layer in range(2):
-            for i, (a, b) in enumerate(GATHERS):
-                n = 3 * layer + i
-                lists.append((n, lambda n=n, layer=layer, a=a, b=b: gather_ticks(Place(4), whbm[layer], pl.ds(a, b - a), send.at[1 + n], recv.at[1 + n])))
+        for n, (layer, a, b, first) in enumerate(GATHERS):
+            lists.append((first, lambda n=n, layer=layer, a=a, b=b: gather_ticks(Place(4), whbm[layer], pl.ds(a, b - a), send.at[1 + n], recv.at[1 + n])))
         tick = Ticker(lists)
+        cps.wait("own2")
         tiny()
-        cps.wait("own0", "own1")
+
+        def pack_shards(p0, p1, b0, b1_):
+            cps.wait(*("flat" + n for n, _ in FLAT[:4]))
+            split_rows({n: r["st_" + n] for n, _ in FLAT[:4]}, (p0, p1))
+            b0[...] = p0[...].astype(BF16)
+            b1_[...] = p1[...].astype(BF16)
+            cps.start("own0", b0, r["w0"].at[here])
+            cps.start("own1", b1_, r["w1"].at[here])
+            tiny()
+            cps.wait("own0", "own1")
+        scope(pack_shards, *vm(((WROWS, D), F32), ((WROWS, D), F32), ((WROWS, D), BF16), ((WROWS, D), BF16)))
         tick()
         tiny()
 
         def begin(stage):
-            cps.start("images", r["images"], stage)
+            cps.start("images", r["img"], stage)
             cps.wait("images")
-            take_images(stage, xa)
+            take_rows(stage, xa)
         scope(begin, STAGE)
+        tick()
         tiny()
         tick()
-        tiny()
         tiny()
         build_tables(r["gs"], 0, tau, y, tab, b1)
         tick()
@@ -944,55 +1000,55 @@
         tick = Idle()
 
         def begin(stage):
-            cps.start("images", r["images"], stage)
+            cps.start("images", r["img"], stage)
             cps.wait("images")
-            take_images(stage, xa)
+            take_rows(stage, xa)
         scope(begin, STAGE)
 
     def forward(layer, xin, x1, keep):
         t = tab.at[layer]
         fwd_conv1(xin, sz, t, x1, pv)
-        tick()
+        if layer == 0:
+            tick()
         norm_phase(x1, t, 0, 1, n1, h1, inv1)
+        tick.upto(7 if layer == 0 else 13)
+        load_piece(layer, 0)
         if layer == 0:
+            for name in ("n1", "h1", "inv1"):
+                cps.start("out0" + name, r[name], r["park0" + name])
             if comm:
                 build_tables(r["gs"], 1, tau, y, tab, b1)
-            tick.upto(5)
-            load_piece(0, 0)
-            load_piece(0, 1)
-            for name in ("n1", "h1", "inv1"):
-                cps.start("out0" + name, r[name], r["park0" + name])
+        else:
+            load_piece(1, 1)
         cps.wait("W0")
 
         def attention(q, p, v, rel, f, s):
             def park(name, ref):
                 cps.start(f"park{layer}{name}", ref, r[f"park{layer}{name}"])
             fwd_qkv(h1, W, t, q, p, v)
-            if layer == 0:
-                tick.upto(8)
-                load_piece(1, 0)
-            else:
-                tick()
             park("q", q)
             park("v", v)
             fwd_softmax(p, sz)
             park("p", p)
-            tick()
-            fwd_attn(q, p, v, s, f, 0, 16)
-            tick()
-            fwd_attn(q, p, v, s, f, 16, 16)
+            if layer == 1:
+                tick()
+            fwd_attn(q, p, v, s, f)
             park("s", s)
             tick()
+            if layer == 1:
+                load_piece(1, 2)
             fwd_conv3(v, q, f, sz, t, rel, pv, 1, 0)
             fwd_conv3(v, q, f, sz, t, rel, pv, 2, 1)
+
+            def wide(i, c):
+                fwd_conv3(v, q, f, sz, t, rel, pv, 3, i + 2)
+                return c
+            lax.fori_loop(0, 2, wide, 0)
+            park("rel", rel)
             tick()
-
-            def wide(i, c):
-                fwd_conv3(v, q, f, sz, t, rel, pv, 3, i)
-                return c
-            lax.fori_loop(0, 2, lambda i, c: wide(i + 2, c), 0)
-            tick()
-            park("rel", rel)
+            if layer == 0:
+                load_piece(0, 1)
+                load_piece(0, 2)
             cps.wait("W1")
             fwd_proj(f, W, t, x1, a_low)
             cps.wait_all(f"park{layer}")
@@ -1003,235 +1059,222 @@
         def mlp(g, slope, n2, h2, inv2, dm):
             norm_phase(x1, t, 2, 3, n2, h2, inv2)
             if layer == 0:
-                tick.upto(6)
-                load_piece(0, 2)
-                tick.upto(7)
-                load_piece(0, 3)
-            else:
-                tick.upto(9)
-                load_piece(1, 2)
-                tick.finish()
-                load_piece(1, 3)
+                tick()
             cps.wait("W2")
-            fwd_fc1(h2, W, b1.at[layer], g, slope, 0, 2)
-            tick()
-            fwd_fc1(h2, W, b1.at[layer], g, slope, 2, 2)
+            fwd_fc1(h2, W, b1.at[layer], g, slope)
             if layer == 0:
                 for name, ref in (("g", g), ("slope", slope), ("n2", n2), ("h2", h2), ("inv2", inv2)):
                     cps.start("out0" + name, ref, r["park0" + name])
+                tick.upto(11)
+                load_piece(0, 3)
+            else:
+                tick.upto(17)
+                load_piece(1, 3)
             cps.wait("W3")
             fwd_fc2(g, W, t, x1)
             if layer == 0:
                 tick()
-                load_piece(1, 1)
                 cps.wait_all("out0")
             else:
                 keep(g, slope, n2, h2, inv2, dm)
         scope(mlp, *vm(WIDE, WIDE, LOW, LOW, INV, LOW))
 
-    def first_half(layer, dx, da, g, slope, n2, h2, inv2, dm, tick):
+    events = {}
+
+    def at(layer, point):
+        for event in events.get((layer, point), ()):
+            event()
+
+    def first_half(layer, dx, da, g, slope, n2, h2, inv2, dm):
         t = tab.at[layer]
         gsum[...] = jnp.zeros_like(gsum)
         bwd_cast_sum(dx, dm, gsum, 7)
         if layer == 0:
             cps.wait("in0slope", "W3")
         bwd_du(dm, W, slope, gb1)
-        tick()
+        at(layer, "e0")
         if layer == 0:
             cps.wait("in0g")
         wgrad2(g, dm, gfc, 80)
-        tick()
+        at(layer, "e1")
         if layer == 0:
             cps.wait("in0h2", "W2")
         wgrad(h2, slope, gfc, 16, 4)
-        tick()
+        at(layer, "e2")
         mm_nt(slope, slice(None), W, 4, 4, da)
+        at(layer, "e3")
         if layer == 0:
             cps.wait("in0n2", "in0inv2", "in0a", "W1")
         norm_back_phase(da, n2, inv2, t, 2, dx, dm, gsum, 2, 3, 6)
-        tick()
+        at(layer, "e4")
         wgrad(a_low, dm, gfc, 0, 1)
+        at(layer, "e5")
         mm_nt(dm, slice(None), W, 3, 1, da)
         zero_tail(da)
-        tick()
-
-    def second_half(layer, xin, dx, da, dv, tick, mid, end):
+
+    def second_half(layer, xin, dx, da, dv, end):
         t = tab.at[layer]
 
         def run(q, p, v, rel, dq, dk, s, dj):
             for name, ref in (("q", q), ("p", p), ("v", v), ("s", s), ("rel", rel)):
                 cps.start(f"in{layer}" + name, r[f"park{layer}{name}"], ref)
-            tick()
+            at(layer, "f0")
             cps.wait(*(f"in{layer}" + n for n in ("q", "p", "v", "s")))
-            bwd_attn1(q, p, v, s, da, dq, dv, dk, 0, 16)
-            tick()
-            bwd_attn1(q, p, v, s, da, dq, dv, dk, 16, 16)
-            tick()
+            bwd_attn1(q, p, v, s, da, dq, dv, dk)
+            at(layer, "f1")
             cps.wait(f"in{layer}rel")
             bwd_mix(q, p, v, rel, da, dq, dv, dk, sz, t, gsum, pv, pr, 1, 0)
-            tick()
+            at(layer, "f2")
             bwd_mix(q, p, v, rel, da, dq, dv, dk, sz, t, gsum, pv, pr, 2, 1)
-            tick()
+            at(layer, "f3")
 
             def wide(i, c):
-                bwd_mix(q, p, v, rel, da, dq, dv, dk, sz, t, gsum, pv, pr, 3, i)
+                bwd_mix(q, p, v, rel, da, dq, dv, dk, sz, t, gsum, pv, pr, 3, i + 2)
                 return c
-            lax.fori_loop(0, 2, lambda i, c: wide(i + 2, c), 0)
-            tick()
+            lax.fori_loop(0, 2, wide, 0)
+            at(layer, "f4")
             bwd_cast(dq, dk, dv, dj)
             if layer == 0:
                 cps.wait("W0", "in0h1")
             wgrad(h1, dj, gq, 0, 3)
-            mid()
+            at(layer, "f5")
             mm_nt(dj, slice(0, 1536), W, 0, 3, dq)
+            at(layer, "f6")
             if layer == 0:
                 cps.wait("in0n1", "in0inv1")
             norm_back_phase(dq, n1, inv1, t, 0, dx, None, gsum, 0, 1, None)
+            at(layer, "f7")
         scope(run, *vm(L4, L4, L4, REL, L4, L4, SUMM, ((R, 3 * D), BF16)))
         end()
+        at(layer, "f8")
         bwd_conv1(xin, dx, da, sz, t, gsum, pv, pr)
+        at(layer, "f9")
         build_small(gsum, gb1, y, tau, gsm)
-
-    def scatter(n, g, rows, out, which):
-        bufs = r["bufs"][4 * which:4 * which + 4]
-        return lambda: scatter_ticks(Place(4), g, rows, *bufs, out, r["rs_send"].at[n], r["rs_recv"].at[n])
-
-    def fc_scatter(layer):
-        out = r[f"sfc{layer}"]
-        return Ticker([(i, scatter(4 * layer + i, gfc, pl.ds(a, b - a), out.at[pl.ds(a, b - a)], i)) for i, (a, b) in enumerate(SCATTERS)])
-
-    def q_scatter(layer):
-        return Ticker([(0, scatter(4 * layer + 2, gq, slice(None), r[f"sq{layer}"], 2))])
-
-    def s_scatter(layer):
-        return Ticker([(0, scatter(4 * layer + 3, gsm, slice(None), r[f"ss{layer}"], 3))])
+        at(layer, "f10")
+
+    if comm:
+        def scatter(n, g, rows, out, which):
+            bufs = r["bufs"][4 * which:4 * which + 4]
+            return Ticker([(0, lambda: scatter_ticks(Place(4), g, rows, *bufs, out, r["rs"].at[n], r["rr"].at[n]))])
+
+        def release(which):
+            def run():
+                place = Place(4)
+                far = [place.dev(z=place.off(k)) for k in range(1, 4)]
+                near = [place.dev(x=1 - place.x), place.dev(y=1 - place.y), place.dev(c=1 - place.c)]
+                for who in far + near:
+                    pl.semaphore_signal(r["cr"].at[which], inc=1, device_id=who, device_id_type=MESH)
+            return run
+
+        def claim(which):
+            return lambda: pl.semaphore_wait(r["cr"].at[which], 6)
+        fa, fb, qt, st = {}, {}, {}, {}
+        for layer in (0, 1):
+            (a0, b0), (a1, b1_) = SCATTERS
+            out = r[f"sfc{layer}"]
+            fa[layer] = scatter(4 * layer, gfc, pl.ds(a0, b0 - a0), out.at[pl.ds(a0, b0 - a0)], 0)
+            fb[layer] = scatter(4 * layer + 1, gfc, pl.ds(a1, b1_ - a1), out.at[pl.ds(a1, b1_ - a1)], 1)
+            qt[layer] = scatter(4 * layer + 2, gq, slice(None), r[f"sq{layer}"], 2)
+            st[layer] = scatter(4 * layer + 3, gsm, slice(None), r[f"ss{layer}"], 3)
+        for layer in (0, 1):
+            A, B, Q = fa[layer], fb[layer], qt[layer]
+            events.update({
+                (layer, "e1"): [B], (layer, "e3"): [B], (layer, "e5"): [A], (layer, "f1"): [B, A], (layer, "f3"): [B, A], (layer, "f4"): [B, A],
+                (layer, "f5"): [Q], (layer, "f7"): [A, Q], (layer, "f9"): [Q], (layer, "f10"): [st[layer]]})
+        events[1, "f7"].append(release(0))
+        events[0, "e0"] = [qt[1], st[1]]
+        events[0, "e1"] = [qt[1], st[1], claim(0), fb[0]]
+        events[0, "e2"] = [st[1]]
+        events[0, "e3"] = [st[1], release(1), fb[0]]
+        events[0, "f5"] = [claim(1), qt[0]]
+    else:
+        def put(name, src):
+            return lambda: cps.start(name, src, r[name])
+        events.update({
+            (1, "f0"): [put("gfc1", gfc)], (1, "f4"): [lambda: cps.wait("gfc1")], (1, "f5"): [put("gq1", gq)], (1, "f10"): [put("gsm1", gsm)],
+            (0, "e0"): [lambda: cps.wait("gq1", "gsm1")], (0, "f0"): [put("gfc0", gfc)], (0, "f5"): [put("gq0", gq)], (0, "f10"): [put("gsm0", gsm)],
+        })
 
     forward(0, xa, xb, None)
 
     def top(g, slope, n2, h2, inv2, dm):
         def emit(stage, stage2):
-            cps.start("cot", r["cotangent"], stage)
-            give_images(xa, stage2, sz)
+            cps.start("cot", r["ct"], stage)
+            mask_rows(xa, sz)
+            give_rows(xa, stage2)
             cps.start("out", stage2, r["output"])
             cps.wait("cot")
-            take_images(stage, dxb, sz)
+            take_rows(stage, dxb)
+            mask_rows(dxb, sz)
             cps.wait("out")
         scope(emit, STAGE, STAGE)
-        first_half(1, dxb, da, g, slope, n2, h2, inv2, dm, Idle())
+        first_half(1, dxb, da, g, slope, n2, h2, inv2, dm)
     forward(1, xb, xa, top)
 
     for i in (1, 2, 3):
         load_piece(0, i)
     cps.start("in0a", r["park0a"], a_low)
-    if comm:
-        rs = fc_scatter(1)
-        rs()
-    else:
-        rs = Idle()
-        cps.start("gfc1", gfc, r["gfc1"])
-
-    def mid1():
-        rs()
 
     def end1():
-        rs()
         load_piece(0, 0)
-        cps.start("in0h1", r["park0h1"], h1)
-        cps.start("in0n1", r["park0n1"], n1)
-        cps.start("in0inv1", r["park0inv1"], inv1)
-    second_half(1, xb, dxb, da, xa, rs, mid1, end1)
-    rs.finish()
-
-    if comm:
-        class Pair(Idle):
-            def __init__(self):
-                self.a, self.b = q_scatter(1), s_scatter(1)
-
-            def __call__(self):
-                self.a()
-                self.b()
-
-            def finish(self):
-                self.a.finish()
-                self.b.finish()
-        rs2 = Pair()
-        rs2()
-    else:
-        rs2 = Idle()
-        cps.wait("gfc1")
-        cps.start("gq1", gq, r["gq1"])
-        cps.start("gsm1", gsm, r["gsm1"])
-        cps.wait("gq1", "gsm1")
+        for name, ref in (("h1", h1), ("n1", n1), ("inv1", inv1)):
+            cps.start("in0" + name, r["park0" + name], ref)
+    second_half(1, xb, dxb, da, xa, end1)
 
     def bottom(g, slope, n2, h2, inv2, dm):
         for name, ref in (("slope", slope), ("g", g), ("h2", h2), ("n2", n2), ("inv2", inv2)):
             cps.start("in0" + name, r["park0" + name], ref)
-        first_half(0, da, dxb, g, slope, n2, h2, inv2, dm, rs2)
+        first_half(0, da, dxb, g, slope, n2, h2, inv2, dm)
     scope(bottom, *vm(WIDE, WIDE, LOW, LOW, INV, LOW))
-    rs2.finish()
-    if comm:
-        place = Place(4)
-        far = [place.dev(z=place.off(k)) for k in range(1, 4)]
-        near = [place.dev(x=1 - place.x), place.dev(y=1 - place.y), place.dev(c=1 - place.c)]
-        for who in far + near:
-            pl.semaphore_signal(r["credit"], inc=1, device_id=who, device_id_type=MESH)
-        pl.semaphore_wait(r["credit"], 6)
-        rs = fc_scatter(0)
-        rsq = q_scatter(0)
-        rss = s_scatter(0)
-        rs()
-    else:
-        rs = rsq = rss = Idle()
-        cps.start("gfc0", gfc, r["gfc0"])
-
-    def mid0():
-        rs.finish()
-        rsq()
 
     def end0():
-        rsq()
-
         def again(stage):
-            cps.start("again", r["images"], stage)
+            cps.start("again", r["img"], stage)
             cps.wait("again")
-            take_images(stage, xb)
+            take_rows(stage, xb)
         scope(again, STAGE)
-        rsq()
-    second_half(0, xb, da, dxb, xa, rs, mid0, end0)
-    if comm:
-        rss()
-        rsq()
-        rss()
-    else:
-        cps.start("gq0", gq, r["gq0"])
-        cps.start("gsm0", gsm, r["gsm0"])
-
-    def last(stage3):
-        give_images(dxb, stage3)
-        cps.start("dx", stage3, r["grad_images"])
-        rss()
-        rsq.finish()
-        rss.finish()
+    second_half(0, xb, da, dxb, xa, end0)
+
+    def last(stage3, *flat):
+        give_rows(dxb, stage3)
+        cps.start("dx", stage3, r["gi"])
         if not comm:
-            cps.wait("gfc0", "gq0", "gsm0")
-        cps.wait("dx")
-    scope(last, pltpu.VMEM((NI, SLOT, D), F32))
+            cps.wait("gfc0", "gq0", "gsm0", "dx")
+            return
+        o = dict(zip([n for n, _ in FLAT], flat))
+        st[0]()
+        join_rows(1, o, r["sfc1"], r["sq1"])
+        qt[0]()
+        st[0]()
+        join_rows(0, o, r["sfc0"], None)
+        qt[0]()
+        st[0]()
+        join_rows(0, o, None, r["sq0"])
+        for name, _ in FLAT[:4]:
+            cps.start("g" + name, o[name], r["g_" + name])
+        st[0].finish()
+        for layer in (0, 1):
+            for i in range(9):
+                o["small"][layer:layer + 1, 128 * i:128 * i + 128] = r[f"ss{layer}"][i:i + 1, :]
+        cps.start("gsmall", o["small"], r["g_small"])
+        cps.wait("dx", *("g" + n for n, _ in FLAT))
+    scope(last, pltpu.VMEM((R, D), F32), *([pltpu.VMEM((2, n), F32) for _, n in FLAT] if comm else []))
 
 
 def step(comm, images, cotangent, sz, *more):
     vmem = pltpu.VMEM
     if comm:
-        inputs = ["images", "cotangent", "sz", "shard0", "shard1", "small"]
-        in_specs = [ANY, ANY] + [VM] * 4
+        inputs = ["img", "ct", "sizes"] + [n for n, _ in FLAT]
+        in_specs = [ANY, ANY, pl.BlockSpec(memory_space=pltpu.SMEM)] + [ANY] * 5
     else:
-        inputs = ["images", "cotangent", "sz", "w0", "w1", "tab", "b1"]
+        inputs = ["img", "ct", "sz", "w0", "w1", "tab", "b1"]
         in_specs = [ANY, ANY, VM, ANY, ANY, VM, VM]
-    outs = [("output", sd((NI, SLOT, D), BF16), ANY), ("grad_images", sd((NI, SLOT, D), F32), ANY)]
+    outs = [("output", sd((R, D), BF16), ANY), ("gi", sd((R, D), F32), ANY)]
     shares = []
+    if comm:
+        shares = [("g_" + n, sd((2, count), F32), ANY) for n, count in FLAT]
     for layer in (0, 1):
-        if comm:
-            shares += [(f"sfc{layer}", sd((144, D), F32), VM), (f"sq{layer}", sd((48, D), F32), VM), (f"ss{layer}", sd((16, 128), F32), VM)]
-        else:
+        if not comm:
             shares += [(f"gfc{layer}", packed(144), ANY), (f"gq{layer}", packed(48), ANY), (f"gsm{layer}", packed(16, 128, F32), ANY)]
     outs += shares
     outs += [(f"park0{n}", sd(*sh), ANY) for n, sh in PARK0] + [(f"park1{n}", sd(*sh), ANY) for n, sh in PARK]
@@ -1240,12 +1283,15 @@
     scratch = [("W", vmem((2, 4, 2, 2, WROWS, D), BF16)), ("gfc", vmem((2, 4, 2, 2, 144, D), BF16)), ("gq", vmem((2, 4, 2, 2, 48, D), BF16)),
                ("gsm", vmem((2, 4, 2, 2, 16, 128), F32)), ("gsum", vmem((4, TROWS, 128), F32)), ("gb1", vmem((8, FF), F32)),
                ("tau", vmem((288, 128), F32)), ("pv", vmem(PADDED, F32)), ("pr", vmem(PADDED, F32)), ("n1", vmem(*LOW)), ("h1", vmem(*LOW)), ("inv1", vmem(*INV)), ("a", vmem(*LOW))]
-    scratch += [(n, vmem(*L4)) for n in ("xa", "xb", "da", "dxb")] + [("copy_sems", pltpu.SemaphoreType.DMA((COPIES,)))]
+    scratch += [(n, vmem(*L4)) for n in ("xa", "xb", "da", "dxb")] + [("cs", pltpu.SemaphoreType.DMA((COPIES,)))]
     bufs = []
     if comm:
         sems = pltpu.SemaphoreType.DMA
+        for layer in (0, 1):
+            scratch += [(f"sfc{layer}", vmem((144, D), F32)), (f"sq{layer}", vmem((48, D), F32)), (f"ss{layer}", vmem((16, 128), F32))]
+        scratch += [("st_" + n, vmem((2, count), BF16)) for n, count in FLAT] + [("osm", vmem((32, 128), F32)), ("sz", vmem((NI, 128), jnp.int32))]
         scratch += [("tab", vmem((2, 4, TROWS, 128), F32)), ("b1", vmem((2, 16, 128), F32)), ("gs", vmem((2, 4, 2, 2, 32, 128), F32)),
-                    ("ag_send", sems((7, 8))), ("ag_recv", sems((7, 8))), ("rs_send", sems((8, 8))), ("rs_recv", sems((8, 8))), ("credit", pltpu.SemaphoreType.REGULAR)]
+                    ("as", sems((9, 8))), ("ar", sems((9, 8))), ("rs", sems((8, 8))), ("rr", sems((8, 8))), ("cr", pltpu.SemaphoreType.REGULAR((2,)))]
         for rows, width, dt in ((80, D, BF16), (64, D, BF16), (48, D, BF16), (16, 128, F32)):
             bufs += scatter_bufs(4, rows, width, dt)
     names = inputs + [n for n, _, _ in outs] + [n for n, _ in scratch]
@@ -1323,17 +1369,18 @@
 
 def shards(n, images, grid_sizes, qkv, proj, fc1, fc2, small, cotangent):
     layers = qkv.shape[0]
-    mine = [pack(qkv[l], proj[l], fc1[l], fc2[l], n) for l in range(layers)]
-    sz = jnp.broadcast_to(grid_sizes[:, None], (NI, 128))
+    images = images.transpose(1, 0, 2).reshape(R, D)
+    cotangent = cotangent.transpose(1, 0, 2).reshape(R, D)
     if n == 32:
-        flat = jnp.pad(small.astype(F32).reshape(2, 9, 128), ((0, 0), (0, 7), (0, 0))).reshape(32, 128)
-        output, dx, *got = step(True, images, cotangent, sz, mine[0], mine[1], flat)
-        shares = [(*split_shares(jnp.concatenate([q, fc]), D // n), s[:9].reshape(-1)) for fc, q, s in (got[:3], got[3:])]
+        output, dx, *grads = step(True, images, cotangent, grid_sizes, qkv, proj, fc1, fc2, small)
     else:
+        sz = jnp.broadcast_to(grid_sizes[:, None], (NI, 128))
+        mine = [pack(qkv[l], proj[l], fc1[l], fc2[l], n) for l in range(layers)]
         held = [whole_weights(mine[l], small[l], n) for l in range(layers)]
         output, dx, *got = step(False, images, cotangent, sz, held[0][0], held[1][0], jnp.stack([held[0][1], held[1][1]]), jnp.stack([held[0][2], held[1][2]]))
         shares = [share_by_xla(*got[:3], n), share_by_xla(*got[3:], n)]
-    grads = [jnp.stack([shares[l][i] for l in range(layers)]) for i in range(5)]
+        grads = [jnp.stack([shares[l][i] for l in range(layers)]) for i in range(5)]
+    output, dx = (a.reshape(SLOT, NI, D).transpose(1, 0, 2) for a in (output, dx))
     return (output, dx, *grads)
 
 

time: 401 us -> 344 us (0.86)
  Pallas kernels: 366 us -> 335 us
  local copies, waits for them, and re-layouts: 23.5 us -> 7.49 us
  other arithmetic: 6.04 us -> 0 us
    pallas_call x1, Pallas kernels: 366 us -> 335 us  [step(): pl.pallas_call(kernel, out_shape=[o for _, o, _ in outs], in_specs=in_spe...]
    slice x4 -> x0, local copies, waits for them, and re-layouts: 6.05 us -> none  [shards(): mine = [pack(qkv[l], proj[l], fc1[l], fc2[l], n) for l in range(layers)]]
    unnamed x27 -> x19, local copies, waits for them, and re-layouts: 12.2 us -> 7.49 us
    another operation x5 -> x0, other arithmetic: 4.04 us -> none  [shards(): grads = [jnp.stack([shares[l][i] for l in range(layers)]) for i in range(5)]]
where the time goes in v5:
time: 344 us
  Pallas kernels  335 us (97%)
  local copies, waits for them, and re-layouts  7.49 us (2%)
    pallas_call x1, Pallas kernels, step(): pl.pallas_call(kernel, out_shape=[o for _, o, _ in outs], in_specs=in_spe...  335 us
    unnamed x19, local copies, waits for them, and re-layouts  7.49 us

profile of v5, /device:TPU:0, one launch (start us, length us, event | category | flops | bytes accessed | tf_op | source)
XLA Modules:
  0.0 343.5 jit_solution(18173800905185253568)
XLA Ops:
  0.6 335.4 %step.1 = (bf16[1312,512]{1,0:T(8,128)(2,1)}, f32[1312,512]{1,0:T(8,128)}, f32[2,24576]{1,0:T(2,128)}, f32[2,8192]{1,0:T(2,128)}, f32[2,32768]{1,0:T(2,128)}, /*...) custom-call(bf16[1312,512]{1,0:T(8,128)(2,1)} %bitcast.13, ...), custom_call_target="tpu_custom_call" | custom-call | tf_op jit(solution)/shard_map/step/pallas_call | solution.py:1306
  336.0 0.0 copy-start
  336.0 2.6 copy.22
  338.6 0.0 copy-done
  338.7 0.0 copy-start.3
  338.7 0.0 copy-start.4
  338.7 0.0 copy-start.2
  338.7 0.0 copy-start.1
  338.7 0.0 copy-start.5
  338.7 1.5 copy.23
  340.2 0.0 copy-done.3
  340.2 0.7 copy.24
  340.9 0.0 copy-done.4
  340.9 0.6 copy.25
  341.5 0.0 copy-done.2
  341.5 0.7 copy.26
  342.2 0.0 copy-done.1
  342.2 0.7 copy.27
  342.9 0.0 copy-done.5
  342.9 0.6 copy.28
Async XLA Ops:
  336.0 2.7 copy-start
  338.7 1.5 copy-start.3
  338.7 2.2 copy-start.4
  338.7 2.9 copy-start.2
  338.7 3.6 %copy-start.1 = (f32[2,32768]{1,0:T(2,128)S(1)}, f32[2,32768]{1,0:T(2,128)}, u32[]{:S(2)}) copy-start(f32[2,32768]{1,0:T(2,128)} %get-tuple-element.33) | copy-start | bytes 786436
  338.7 4.3 %copy-start.5 = (f32[2,1152]{1,0:T(2,128)S(1)}, f32[2,1152]{1,0:T(2,128)}, u32[]{:S(2)}) copy-start(f32[2,1152]{1,0:T(2,128)} %get-tuple-element.34) | copy-start | bytes 27652

commit v6 on v5

--- a/solution.py
+++ b/solution.py
@@ -422,6 +422,13 @@
             return jnp.concatenate([g[i % 2, 2 * j + i // 8, i // 4 % 2, i // 2 % 2, here, :] for i in range(16)], axis=0)
         w = jnp.concatenate([rows(first + b) for b in range(blocks)], axis=1)
         put2(out, at, j, dot(a[at, cols], w, 1, 1))
+    halves(fn)
+
+
+def proj_back(dx, g, out):
+    def fn(at, j):
+        w = jnp.concatenate([g[i % 2, 2 * j + i // 8, i // 4 % 2, i // 2 % 2, 48:64, :] for i in range(16)], axis=0)
+        put2(out, at, j, dot(full(dx, at).astype(BF16), w, 1, 1))
     halves(fn)
 
 
@@ -1109,8 +1116,6 @@
         at(layer, "e4")
         wgrad(a_low, dm, gfc, 0, 1)
         at(layer, "e5")
-        mm_nt(dm, slice(None), W, 3, 1, da)
-        zero_tail(da)
 
     def second_half(layer, xin, dx, da, dv, end):
         t = tab.at[layer]
@@ -1118,7 +1123,8 @@
         def run(q, p, v, rel, dq, dk, s, dj):
             for name, ref in (("q", q), ("p", p), ("v", v), ("s", s), ("rel", rel)):
                 cps.start(f"in{layer}" + name, r[f"park{layer}{name}"], ref)
-            at(layer, "f0")
+            proj_back(dx, W, da)
+            zero_tail(da)
             cps.wait(*(f"in{layer}" + n for n in ("q", "p", "v", "s")))
             bwd_attn1(q, p, v, s, da, dq, dv, dk)
             at(layer, "f1")
@@ -1191,8 +1197,8 @@
         def put(name, src):
             return lambda: cps.start(name, src, r[name])
         events.update({
-            (1, "f0"): [put("gfc1", gfc)], (1, "f4"): [lambda: cps.wait("gfc1")], (1, "f5"): [put("gq1", gq)], (1, "f10"): [put("gsm1", gsm)],
-            (0, "e0"): [lambda: cps.wait("gq1", "gsm1")], (0, "f0"): [put("gfc0", gfc)], (0, "f5"): [put("gq0", gq)], (0, "f10"): [put("gsm0", gsm)],
+            (1, "e5"): [put("gfc1", gfc)], (1, "f4"): [lambda: cps.wait("gfc1")], (1, "f5"): [put("gq1", gq)], (1, "f10"): [put("gsm1", gsm)],
+            (0, "e0"): [lambda: cps.wait("gq1", "gsm1")], (0, "e5"): [put("gfc0", gfc)], (0, "f5"): [put("gq0", gq)], (0, "f10"): [put("gsm0", gsm)],
         })
 
     forward(0, xa, xb, None)
@@ -1211,12 +1217,13 @@
         first_half(1, dxb, da, g, slope, n2, h2, inv2, dm)
     forward(1, xb, xa, top)
 
-    for i in (1, 2, 3):
+    for i in (2, 3):
         load_piece(0, i)
     cps.start("in0a", r["park0a"], a_low)
 
     def end1():
         load_piece(0, 0)
+        load_piece(0, 1)
         for name, ref in (("h1", h1), ("n1", n1), ("inv1", inv1)):
             cps.start("in0" + name, r["park0" + name], ref)
     second_half(1, xb, dxb, da, xa, end1)

time: 344 us -> 341 us (level)
  no operation moved by 1% of the time
where the time goes in v6:
time: 341 us
  Pallas kernels  332 us (97%)
  local copies, waits for them, and re-layouts  7.49 us (2%)
    pallas_call x1, Pallas kernels, step(): pl.pallas_call(kernel, out_shape=[o for _, o, _ in outs], in_specs=in_spe...  332 us
    unnamed x19, local copies, waits for them, and re-layouts  7.49 us

profile of v6, /device:TPU:0, one launch (start us, length us, event | category | flops | bytes accessed | tf_op | source)
XLA Modules:
  0.0 340.7 jit_solution(8854617622513313902)
XLA Ops:
  0.6 332.5 %step.1 = (bf16[1312,512]{1,0:T(8,128)(2,1)}, f32[1312,512]{1,0:T(8,128)}, f32[2,24576]{1,0:T(2,128)}, f32[2,8192]{1,0:T(2,128)}, f32[2,32768]{1,0:T(2,128)}, /*...) custom-call(bf16[1312,512]{1,0:T(8,128)(2,1)} %bitcast.13, ...), custom_call_target="tpu_custom_call" | custom-call | tf_op jit(solution)/shard_map/step/pallas_call | solution.py:1313
  333.1 0.0 copy-start
  333.1 2.6 copy.22
  335.8 0.0 copy-done
  335.8 0.0 copy-start.3
  335.8 0.0 copy-start.4
  335.8 0.0 copy-start.2
  335.8 0.0 copy-start.1
  335.8 0.0 copy-start.5
  335.8 1.5 copy.23
  337.3 0.0 copy-done.3
  337.3 0.7 copy.24
  338.0 0.0 copy-done.4
  338.0 0.6 copy.25
  338.7 0.0 copy-done.2
  338.7 0.7 copy.26
  339.4 0.0 copy-done.1
  339.4 0.7 copy.27
  340.1 0.0 copy-done.5
  340.1 0.6 copy.28
Async XLA Ops:
  333.1 2.7 copy-start
  335.8 1.5 copy-start.3
  335.8 2.2 copy-start.4
  335.8 2.9 copy-start.2
  335.8 3.6 %copy-start.1 = (f32[2,32768]{1,0:T(2,128)S(1)}, f32[2,32768]{1,0:T(2,128)}, u32[]{:S(2)}) copy-start(f32[2,32768]{1,0:T(2,128)} %get-tuple-element.33) | copy-start | bytes 786436
  335.8 4.3 %copy-start.5 = (f32[2,1152]{1,0:T(2,128)S(1)}, f32[2,1152]{1,0:T(2,128)}, u32[]{:S(2)}) copy-start(f32[2,1152]{1,0:T(2,128)} %get-tuple-element.34) | copy-start | bytes 27652
